TPU v7x, 128 devices: a whole 4x4x4 slice. The times are simulated.
128 devices in a mesh: gx: 16 (over x, z), gy: 8 (over y, core).
Axes of the slice: x: 4, y: 4, z: 4, core: 2. Of those that a mesh axis runs over, the one named last changes fastest.
Arguments:
- velocity: float32 [3, 256, 256, 256], P(None, 'gx', 'gy'), may hold values from -6 to 6
- owner_block: int32 [262144, 1], P(('gx', 'gy')), may hold values from 0 to 127, as said below
- base_x: int32 [262144], P(('gx', 'gy')), may hold values from 0 to 16
- base_y: int32 [262144], P(('gx', 'gy')), may hold values from 0 to 32
- base_z: int32 [262144], P(('gx', 'gy')), may hold values from 0 to 255
- delta_weights: float32 [12, 262144], P(None, ('gx', 'gy')), may hold values from 0.1 to 1
- marker_offset: float32 [3, 262144], P(None, ('gx', 'gy')), may hold values from -4 to 4
- sphere_motion: float32 [6, 256], P(None, ('gx', 'gy')), may hold values from -6 to 6
- contact_sphere: int32 [512], P(('gx', 'gy')), may hold values from 0 to 255, as said below
- contact_partner: int32 [512], P(('gx', 'gy')), may hold values from 0 to 255
Outputs:
- velocity_star: float32 [3, 256, 256, 256], P(None, 'gx', 'gy')
- new_motion: float32 [6, 256], P(None, ('gx', 'gy'))
Inputs may be any that keep to these rules, and one draw needn't show every extreme that they name: `owner_block`: block b stands at gx index b // 8 and gy index b % 8. Each marker's owner block is the block of the device that holds the marker or one of the eight blocks beside it (periodic along gx, none beyond the walls along gy). Among the markers of one device, at most 256 have any one owner block other than that device's own, and in every device exactly 256 have one such block. `contact_sphere`: entry k names one of the 2 spheres k // 4 * 2 and after, those of the device that holds entry k.
All inputs are finite; a program needn't handle non-finite values.
Results may differ from a plain program's by a relative error of at most 0.0003.
Values sent between devices are 32-bit elements; how exact they have to be, the bound alone decides.
No kernel may reach another device: no remote copies, remote signals or barrier semaphores. Data moves between devices by JAX's collectives and lax.ppermute only.
A program may use at most 64 MiB of HBM per device.

v0:
```python
import jax
import jax.numpy as jnp
from jax import lax
from jax.sharding import PartitionSpec as P

ITERS = 4


DIFFUSION = 1.0
RESPONSE = 0.5
DASHPOT = 0.1


def with_halo(array, sides, width):
    for axis, dim in sides:
        size, length = (lax.axis_size(axis), array.shape[dim])
        up = [(i, (i + 1) % size) for i in range(size)]
        down = [(j, i) for i, j in up]
        last = lax.slice_in_dim(array, length - width, length, axis=dim)
        leading = lax.slice_in_dim(array, 0, width, axis=dim)
        before = lax.ppermute(last, axis, up)
        after = lax.ppermute(leading, axis, down)
        array = jnp.concatenate([before, array, after], axis=dim)
    return array


def weight_table(start, weights, extent, wrapped):
    positions = jnp.arange(extent, dtype=jnp.int32)[:, None]
    table = jnp.zeros((extent, start.shape[0]), jnp.float32)
    for offset in range(4):
        target_cell = start + offset
        if wrapped:
            target_cell = target_cell % extent
        table = table + weights[offset][None, :] * (positions == target_cell[None, :]).astype(
            jnp.float32
        )
    return table


def sample_field(field, table_x, table_y, table_z):
    extent_z = field.shape[3]
    partial_z = jnp.dot(field.reshape(-1, extent_z), table_z, precision=lax.Precision.HIGHEST)
    partial_z = partial_z.reshape(3, field.shape[1], field.shape[2], -1)
    partial_y = jnp.sum(partial_z * table_y[None, None, :, :], axis=2)
    return jnp.sum(partial_y * table_x[None, :, :], axis=1)


def deposit_field(forces, table_x, table_y, table_z):
    spread_xy = forces[:, None, None, :] * table_x[None, :, None, :] * table_y[None, None, :, :]
    count = forces.shape[1]
    flat = lax.dot_general(
        spread_xy.reshape(-1, count),
        table_z,
        (((1,), (1,)), ((), ())),
        precision=lax.Precision.HIGHEST,
    )
    return flat.reshape(3, table_x.shape[0], table_y.shape[0], table_z.shape[0])


def wall_mask(row_index, row_count, span_y, margin):
    rows_ext = jnp.arange(span_y + 2 * margin, dtype=jnp.int32)
    global_row = row_index * span_y - margin + rows_ext
    inside = jnp.logical_and(global_row >= 0, global_row < span_y * row_count)
    return inside.astype(jnp.float32)


def faces(state, margin, row_index, row_count):
    grown = with_halo(state, (("gx", 1), ("gy", 2)), margin)
    return grown * wall_mask(row_index, row_count, state.shape[2], margin)[None, None, :, None]


def relax(grown, rhs_part):
    center = grown[:, 1:-1, 1:-1]
    beside_all = grown[:, 2:, 1:-1] + grown[:, :-2, 1:-1] + grown[:, 1:-1, 2:] + grown[:, 1:-1, :-2]
    beside_all = beside_all + jnp.roll(center, -1, 3) + jnp.roll(center, 1, 3)
    return (rhs_part + DIFFUSION * beside_all) / (1.0 + 6.0 * DIFFUSION)


def send_requests(buffer):
    width_rows = buffer.shape[0]
    grown = with_halo(buffer.reshape(width_rows, 3, 3, -1), (("gx", 1), ("gy", 2)), 1)
    return grown[:, 0::2, 0::2].reshape(width_rows, -1)


def send_force_replies(buffer):
    grown = with_halo(buffer.reshape(3, 3, 3, -1), (("gx", 1), ("gy", 2)), 1)
    return grown[:, 0::2, 0::2].reshape(3, -1)


def on_device(
    velocity,
    owner_block,
    base_x,
    base_y,
    base_z,
    delta_weights,
    marker_offset,
    sphere_motion,
    contact_sphere,
    contact_partner,
):
    span_x = velocity.shape[1]
    span_y = velocity.shape[2]
    extent_z = velocity.shape[3]
    row_count = lax.axis_size("gy")
    column_count = lax.axis_size("gx")
    here = lax.axis_index(("gx", "gy"))
    row_index = lax.axis_index("gy")
    column_index = lax.axis_index("gx")
    grown_field = with_halo(velocity, (("gx", 1), ("gy", 2)), 2)
    grown_field = grown_field * wall_mask(row_index, row_count, span_y, 2)[None, None, :, None]
    markers = base_x.shape[0]
    spheres_here = sphere_motion.shape[1]
    per_sphere = markers // spheres_here
    capacity = markers // 8
    owner = owner_block[:, 0]
    at_home = owner == here
    home_weight = at_home.astype(jnp.float32)
    lanes = 9
    step_x = (owner // row_count - column_index + 1 + column_count) % column_count
    step_y = owner % row_count - row_index + 1
    lane = step_x * 3 + step_y
    hits = (lane[:, None] == jnp.arange(lanes, dtype=jnp.int32)[None, :]).astype(jnp.int32)
    hits = hits * (1 - at_home.astype(jnp.int32))[:, None]
    ranked = jnp.sum((jnp.cumsum(hits, axis=0) - hits) * hits, axis=1)
    total_slots = lanes * capacity
    slots = jnp.where(at_home, total_slots, lane * capacity + ranked)
    fetch_slots = jnp.minimum(slots, total_slots - 1)
    linear = sphere_motion[0:3]
    angular = sphere_motion[3:6]
    marker_linear = jnp.broadcast_to(linear[:, :, None], (3, spheres_here, per_sphere)).reshape(
        3, markers
    )
    marker_angular = jnp.broadcast_to(angular[:, :, None], (3, spheres_here, per_sphere)).reshape(
        3, markers
    )
    target = marker_linear + jnp.cross(marker_angular, marker_offset, axis=0)
    coords = jnp.stack([base_x, base_y, base_z]).astype(jnp.float32)
    payload = jnp.concatenate([delta_weights, coords, target], axis=0)
    width_rows = payload.shape[0]
    outgoing = (
        jnp.zeros((width_rows, total_slots), jnp.float32).at[:, slots].set(payload, mode="drop")
    )
    arrived = send_requests(outgoing)
    cell_start = arrived[12:15].astype(jnp.int32)
    start_x = jnp.concatenate([base_x, cell_start[0]])
    start_y = jnp.concatenate([base_y, cell_start[1]])
    start_z = jnp.concatenate([base_z, cell_start[2]])
    weights_all = jnp.concatenate([delta_weights, arrived[0:12]], axis=1)
    table_x = weight_table(start_x, weights_all[0:4], span_x + 4, False)
    table_y = weight_table(start_y, weights_all[4:8], span_y + 4, False)
    table_z = weight_table(start_z, weights_all[8:12], extent_z, True)
    sampled_all = sample_field(grown_field, table_x, table_y, table_z)
    sampled_home = sampled_all[:, :markers]
    sampled = sampled_all[:, markers:]
    slot_force = arrived[15:18] - sampled
    returned = send_force_replies(slot_force)
    force = jnp.where(at_home[None, :], target - sampled_home, returned[:, fetch_slots])
    forces_all = jnp.concatenate([force * home_weight[None, :], slot_force], axis=1)
    spread = deposit_field(forces_all, table_x, table_y, table_z)
    rims = with_halo(spread, (("gx", 1), ("gy", 2)), 2)
    lower = (row_index > 0).astype(jnp.float32)
    upper = (row_index < row_count - 1).astype(jnp.float32)
    source = spread[:, 2 : span_x + 2, 2 : span_y + 2]
    source = source.at[:, 0:2].add(rims[:, 0:2, 4 : span_y + 4])
    source = source.at[:, span_x - 2 :].add(rims[:, span_x + 6 :, 4 : span_y + 4])
    source = source.at[:, :, 0:2].add(lower * rims[:, 4 : span_x + 4, 0:2])
    source = source.at[:, :, span_y - 2 :].add(upper * rims[:, 4 : span_x + 4, span_y + 6 :])
    source = source.at[:, 0:2, 0:2].add(lower * rims[:, 0:2, 0:2])
    source = source.at[:, 0:2, span_y - 2 :].add(upper * rims[:, 0:2, span_y + 6 :])
    source = source.at[:, span_x - 2 :, 0:2].add(lower * rims[:, span_x + 6 :, 0:2])
    source = source.at[:, span_x - 2 :, span_y - 2 :].add(
        upper * rims[:, span_x + 6 :, span_y + 6 :]
    )
    push = jnp.sum(force.reshape(3, spheres_here, per_sphere), axis=-1) / per_sphere
    twist = (
        jnp.sum(
            jnp.cross(marker_offset, force, axis=0).reshape(3, spheres_here, per_sphere), axis=-1
        )
        / per_sphere
    )
    moved = linear - RESPONSE * push
    turned = angular - RESPONSE * twist
    everyone = lax.all_gather(moved, ("gx", "gy"), axis=1, tiled=True)
    all_spheres = everyone.shape[1]
    pick_partner = (
        contact_partner[:, None] == jnp.arange(all_spheres, dtype=jnp.int32)[None, :]
    ).astype(jnp.float32)
    partner_moved = jnp.dot(everyone, pick_partner.T, precision=lax.Precision.HIGHEST)
    local_sphere = contact_sphere - here * spheres_here
    pick_own = (jnp.arange(spheres_here, dtype=jnp.int32)[:, None] == local_sphere[None, :]).astype(
        jnp.float32
    )
    own_moved = jnp.dot(moved, pick_own, precision=lax.Precision.HIGHEST)
    spring = jnp.dot(partner_moved - own_moved, pick_own.T, precision=lax.Precision.HIGHEST)
    settled = moved + DASHPOT * spring
    new_motion = jnp.concatenate([settled, turned], axis=0)
    rhs = velocity + source
    state = rhs
    rhs_cycle = rhs
    for sweep_pair in range(ITERS // 2):
        grown = faces(state, 2, row_index, row_count)
        if sweep_pair == 0:
            rhs_cycle = grown[:, 1:-1, 1:-1]
        middle = relax(grown, rhs_cycle)
        middle = middle * wall_mask(row_index, row_count, span_y, 1)[None, None, :, None]
        state = relax(middle, rhs)
    return (state, new_motion)


def solution(mesh):
    placed = (
        P(None, "gx", "gy", None),
        P(("gx", "gy"), None),
        P(("gx", "gy")),
        P(("gx", "gy")),
        P(("gx", "gy")),
        P(None, ("gx", "gy")),
        P(None, ("gx", "gy")),
        P(None, ("gx", "gy")),
        P(("gx", "gy")),
        P(("gx", "gy")),
    )
    return jax.shard_map(
        on_device,
        mesh=mesh,
        in_specs=placed,
        out_specs=(P(None, "gx", "gy", None), P(None, ("gx", "gy"))),
        check_vma=False,
    )
```

profile of v0, /device:TPU:1, one launch (start us, length us, event | category | flops | bytes accessed | tf_op | source)
XLA Modules:
  0.0 262.9 jit_solution(7945562148109077479)
XLA Ops:
  2.5 6.8 %collective-permute-start.1 = (f32[3,2,32,256]{3,2,1,0:T(8,128)}, f32[3,2,32,256]{3,2,1,0:T(8,128)}, u32[]{:S(2)}, u32[]{:S(2)}) collective-permute-start(f32[3,2,32,256]{3,2,1,0:T(8,128)} %get-tuple-element.145), channel_id=1, source_target_pairs={{8,0},{16,8},{24,16},{32,24},{40,32},{48,40},{56,48},{64,56},{72,6... | collective-permute-start | bytes 589832 | tf_op jit(solution)/shard_map/ppermute | solution.py:22
  11.3 2.6 reduce-window.6
  16.0 5.9 %scatter_custom_fusion = f32[18,2304]{0,1:T(8,128)S(1)} fusion(s32[2048]{0:T(1024)S(1)} %bitcast.93, f32[2048,18]{1,0:T(8,128)S(1)} %copy.59, f32[]{:T(128)} %constant.346.clone.1), kind=kCustom, calls=%fused_computation.79 | custom fusion | bytes 165892 | tf_op jit(solution)/shard_map/scatter | solution.py:142
  22.5 4.8 %collective-permute-start.5 = (f32[18,1,3,256]{3,2,1,0:T(4,128)S(1)}, f32[18,1,3,256]{3,2,1,0:T(4,128)S(1)}, u32[]{:S(2)}, u32[]{:S(2)}) collective-permute-start(f32[18,1,3,256]{3,2,1,0:T(4,128)S(1)} %get-tuple-element.152), channel_id=1, source_target_pairs={{8,0},{16,8},{24,16},{32,24},{40,32},{48,40},{56,48},{64,56},{72,6... | collective-permute-start | bytes 165896 | tf_op jit(solution)/shard_map/ppermute | solution.py:22
  30.6 2.7 %collective-permute-start.6 = (f32[18,5,1,256]{3,2,1,0:T(1,128)S(1)}, f32[18,5,1,256]{3,2,1,0:T(1,128)S(1)}, u32[]{:S(2)}, u32[]{:S(2)}) collective-permute-start(f32[18,5,1,256]{3,2,1,0:T(1,128)S(1)} %get-tuple-element.147), channel_id=1, source_target_pairs={{0,1},{1,2},{2,3},{3,4},{4,5},{5,6},{6,7},{7,0},{8,9},{9,10},{10,1... | collective-permute-start | bytes 276488 | tf_op jit(solution)/shard_map/ppermute | solution.py:21
  45.1 2.7 %collective-permute-done.3 = f32[3,20,2,256]{3,2,1,0:T(2,128)S(1)} collective-permute-done((f32[3,20,2,256]{3,2,1,0:T(2,128)S(1)}, f32[3,20,2,256]{3,2,1,0:T(2,128)S(1)}, u32[]{:S(2)}, u32[]{:S(2)}) %collective-permute-start.3) | collective-permute-done | bytes 122912 | tf_op jit(solution)/shard_map/ppermute | solution.py:22
  48.3 46.2 %multiply_reduce_fusion = f32[3,20,4352]{2,1,0:T(8,128)S(1)} fusion(f32[36,4352]{1,0:T(8,128)S(1)} %select_add_fusion.3, f32[4352]{0:T(1024)S(1)} %get-tuple-element.107, s32[4352]{0:T(1024)S(1)} %get-tuple-element.172, f32[4352]{0:T(1024)S(1)} %get-tuple-element.108, s32[4352]{0:T(1024)S(1)} %get-tuple-element.171, f32[4352]{0:T(1024)S(1)} %get-tuple-element.109, ...), kind=kOutput, calls=%fused_computation.4 | convolution fusion | flops 28908576768 | bytes 4022272 | tf_op jit(solution)/shard_map/dot_general | solution.py:42
  95.4 4.8 %collective-permute-start.9 = (f32[3,1,3,256]{3,2,1,0:T(4,128)S(1)}, f32[3,1,3,256]{3,2,1,0:T(4,128)S(1)}, u32[]{:S(2)}, u32[]{:S(2)}) collective-permute-start(f32[3,1,3,256]{3,2,1,0:T(4,128)S(1)} %get-tuple-element.161), channel_id=1, source_target_pairs={{8,0},{16,8},{24,16},{32,24},{40,32},{48,40},{56,48},{64,56},{72,6... | collective-permute-start | bytes 27656 | tf_op jit(solution)/shard_map/ppermute | solution.py:22
  103.2 3.6 %fusion.112 = f32[256,4352,1,1]{1,0,3,2:T(8,128)} fusion(f32[4352]{0:T(1024)S(1)} %get-tuple-element.107, s32[4352]{0:T(1024)S(1)} %get-tuple-element.172, f32[4352]{0:T(1024)S(1)} %get-tuple-element.108, s32[4352]{0:T(1024)S(1)} %get-tuple-element.171, f32[4352]{0:T(1024)S(1)} %get-tuple-element.109, s32[4352]{0:T(1024)S(1)} %get-tuple-element.170, ...), kind=kLoop, calls=%fused_computation.7.clone.2 | loop fusion | flops 12255232 | bytes 4595712 | tf_op jit(solution)/shard_map/dot_general | solution.py:51
  107.3 5.5 %gather_fusion = f32[2048,3]{1,0:T(8,128)S(1)} fusion(f32[3,2304]{0,1:T(8,128)S(1)} %bitcast.73, s32[2048]{0:T(1024)S(1)} %broadcast_clamp_fusion), kind=kCustom, calls=%fused_computation | custom fusion | bytes 57344 | tf_op jit(solution)/shard_map/gather | solution.py:158
  114.0 35.5 %fusion = f32[3,20,36,256]{3,2,1,0:T(8,128)S(1)} fusion(f32[3,20,4352]{2,1,0:T(8,128)S(1)} %broadcast_multiply_fusion, f32[36,4352]{1,0:T(8,128)S(1)} %select_add_fusion.3, f32[256,4352,1,1]{1,0,3,2:T(8,128)} %fusion.112), kind=kOutput, calls=%fused_computation.2 | convolution fusion | flops 28887183360 | bytes 8339456 | tf_op jit(solution)/shard_map/dot_general | solution.py:51
  151.2 5.8 %collective-permute-start.13 = (f32[3,2,36,256]{3,2,1,0:T(8,128)S(1)}, f32[3,2,36,256]{3,2,1,0:T(8,128)S(1)}, u32[]{:S(2)}, u32[]{:S(2)}) collective-permute-start(f32[3,2,36,256]{3,2,1,0:T(8,128)S(1)} %get-tuple-element.125), channel_id=1, source_target_pairs={{8,0},{16,8},{24,16},{32,24},{40,32},{48,40},{56,48},{64,56},{72,6... | collective-permute-start | bytes 663560 | tf_op jit(solution)/shard_map/ppermute | solution.py:22
  157.3 2.9 %collective-permute-done.13 = f32[3,2,36,256]{3,2,1,0:T(8,128)S(1)} collective-permute-done((f32[3,2,36,256]{3,2,1,0:T(8,128)S(1)}, f32[3,2,36,256]{3,2,1,0:T(8,128)S(1)}, u32[]{:S(2)}, u32[]{:S(2)}) %collective-permute-start.13) | collective-permute-done | bytes 221216 | tf_op jit(solution)/shard_map/ppermute | solution.py:22
  160.2 5.2 %collective-permute-done.12 = f32[3,2,36,256]{3,2,1,0:T(8,128)S(1)} collective-permute-done((f32[3,2,36,256]{3,2,1,0:T(8,128)S(1)}, f32[3,2,36,256]{3,2,1,0:T(8,128)S(1)}, u32[]{:S(2)}, u32[]{:S(2)}) %collective-permute-start.12) | collective-permute-done | bytes 221216 | tf_op jit(solution)/shard_map/ppermute | solution.py:21
  165.5 4.4 %collective-permute-start.15 = (f32[3,24,2,256]{3,2,1,0:T(2,128)S(1)}, f32[3,24,2,256]{3,2,1,0:T(2,128)S(1)}, u32[]{:S(2)}, u32[]{:S(2)}) collective-permute-start(f32[3,24,2,256]{3,2,1,0:T(2,128)S(1)} %get-tuple-element.115), channel_id=1, source_target_pairs={{1,0},{2,1},{3,2},{4,3},{5,4},{6,5},{7,6},{0,7},{9,8},{10,9},{11,1... | collective-permute-start | bytes 442376 | tf_op jit(solution)/shard_map/ppermute | solution.py:22
  177.0 2.7 %add_select_fusion.4 = f32[3,2,2,256]{3,2,1,0:T(2,128)S(1)} fusion(f32[3,24,2,256]{3,2,1,0:T(2,128)S(1)} %collective-permute-done.15, f32[3,16,32,256]{3,2,1,0:T(8,128)} %fusion.66, s32[]{:T(128)} %bitcast.22, s32[]{:T(128)} %bitcast.23, pred[]{:T(512)} %and_reduce_fusion, f32[]{:T(128)S(6)} %convert_element_type.60), kind=kLoop, calls=%fused_computation.159 | loop fusion | flops 9216 | bytes 36877 | tf_op jit(solution)/shard_map/select.13
  179.8 2.7 %scatter-add.35 = f32[3,16,32,256]{3,2,1,0:T(8,128)} dynamic-update-slice(f32[3,16,32,256]{3,2,1,0:T(8,128)} %fusion.66, f32[3,2,2,256]{3,2,1,0:T(2,128)S(1)} %add_select_fusion.4, s32[]{:T(128)} %constant.344.clone.1, s32[]{:T(128)} %bitcast.22, s32[]{:T(128)} %bitcast.23, s32[]{:T(128)} %constant.344.clone.1) | dynamic-update-slice | bytes 24580 | tf_op jit(solution)/shard_map/scatter-add | solution.py:170
  187.6 4.8 %collective-permute-start.17 = (f32[3,2,32,256]{3,2,1,0:T(8,128)S(1)}, f32[3,2,32,256]{3,2,1,0:T(8,128)S(1)}, u32[]{:S(2)}, u32[]{:S(2)}) collective-permute-start(f32[3,2,32,256]{3,2,1,0:T(8,128)S(1)} %get-tuple-element.144), channel_id=1, source_target_pairs={{8,0},{16,8},{24,16},{32,24},{40,32},{48,40},{56,48},{64,56},{72,6... | collective-permute-start | bytes 589832 | tf_op jit(solution)/shard_map/ppermute | solution.py:22
  192.5 37.0 %all-gather = f32[128,2,3]{2,1,0:T(2,128)S(1)} all-gather(f32[1,2,3]{2,1,0:T(2,128)S(1)} %get-tuple-element.178), channel_id=1, replica_groups=mesh['gx'=16,'gy'=8] {'gx','gy'}, dimensions={0}, use_global_device_ids=true | all-gather | bytes 3096 | tf_op jit(solution)/shard_map/all_gather | solution.py:184
  231.5 2.7 %collective-permute-done.19 = f32[3,20,2,256]{3,2,1,0:T(2,128)S(1)} collective-permute-done((f32[3,20,2,256]{3,2,1,0:T(2,128)S(1)}, f32[3,20,2,256]{3,2,1,0:T(2,128)S(1)}, u32[]{:S(2)}, u32[]{:S(2)}) %collective-permute-start.19) | collective-permute-done | bytes 122912 | tf_op jit(solution)/shard_map/ppermute | solution.py:22
  241.7 3.5 %collective-permute-start.21 = (f32[3,2,32,256]{3,2,1,0:T(8,128)S(1)}, f32[3,2,32,256]{3,2,1,0:T(8,128)S(1)}, u32[]{:S(2)}, u32[]{:S(2)}) collective-permute-start(f32[3,2,32,256]{3,2,1,0:T(8,128)S(1)} %get-tuple-element.142), channel_id=1, source_target_pairs={{8,0},{16,8},{24,16},{32,24},{40,32},{48,40},{56,48},{64,56},{72,6... | collective-permute-start | bytes 589832 | tf_op jit(solution)/shard_map/ppermute | solution.py:22
  245.4 3.6 %collective-permute-done.20 = f32[3,2,32,256]{3,2,1,0:T(8,128)S(1)} collective-permute-done((f32[3,2,32,256]{3,2,1,0:T(8,128)S(1)}, f32[3,2,32,256]{3,2,1,0:T(8,128)S(1)}, u32[]{:S(2)}, u32[]{:S(2)}) %collective-permute-start.20) | collective-permute-done | bytes 196640 | tf_op jit(solution)/shard_map/ppermute | solution.py:21
  252.7 2.7 %collective-permute-done.23 = f32[3,20,2,256]{3,2,1,0:T(2,128)S(1)} collective-permute-done((f32[3,20,2,256]{3,2,1,0:T(2,128)S(1)}, f32[3,20,2,256]{3,2,1,0:T(2,128)S(1)}, u32[]{:S(2)}, u32[]{:S(2)}) %collective-permute-start.23) | collective-permute-done | bytes 122912 | tf_op jit(solution)/shard_map/ppermute | solution.py:22
  257.2 2.5 fusion.31
  (193 shorter events, 59.5 us)
Async XLA Ops:
  2.5 39.6 %collective-permute-start.1 = (f32[3,2,32,256]{3,2,1,0:T(8,128)}, f32[3,2,32,256]{3,2,1,0:T(8,128)}, u32[]{:S(2)}, u32[]{:S(2)}) collective-permute-start(f32[3,2,32,256]{3,2,1,0:T(8,128)} %get-tuple-element.145), channel_id=1, source_target_pairs={{8,0},{16,8},{24,16},{32,24},{40,32},{48,40},{56,48},{64,56},{72,6... | collective-permute-start | bytes 589832 | tf_op jit(solution)/shard_map/ppermute | solution.py:22
  9.3 31.7 %collective-permute-start = (f32[3,2,32,256]{3,2,1,0:T(8,128)}, f32[3,2,32,256]{3,2,1,0:T(8,128)}, u32[]{:S(2)}, u32[]{:S(2)}) collective-permute-start(f32[3,2,32,256]{3,2,1,0:T(8,128)} %get-tuple-element.146), channel_id=1, source_target_pairs={{0,8},{8,16},{16,24},{24,32},{32,40},{40,48},{48,56},{56,64},{64,7... | collective-permute-start | bytes 589832 | tf_op jit(solution)/shard_map/ppermute | solution.py:21
  22.4 8.1 %collective-permute-start.4 = (f32[18,1,3,256]{3,2,1,0:T(4,128)S(1)}, f32[18,1,3,256]{3,2,1,0:T(4,128)S(1)}, u32[]{:S(2)}, u32[]{:S(2)}) collective-permute-start(f32[18,1,3,256]{3,2,1,0:T(4,128)S(1)} %get-tuple-element.151), channel_id=1, source_target_pairs={{0,8},{8,16},{16,24},{24,32},{32,40},{40,48},{48,56},{56,64},{64,7... | collective-permute-start | bytes 165896 | tf_op jit(solution)/shard_map/ppermute | solution.py:21
  22.5 8.0 %collective-permute-start.5 = (f32[18,1,3,256]{3,2,1,0:T(4,128)S(1)}, f32[18,1,3,256]{3,2,1,0:T(4,128)S(1)}, u32[]{:S(2)}, u32[]{:S(2)}) collective-permute-start(f32[18,1,3,256]{3,2,1,0:T(4,128)S(1)} %get-tuple-element.152), channel_id=1, source_target_pairs={{8,0},{16,8},{24,16},{32,24},{40,32},{48,40},{56,48},{64,56},{72,6... | collective-permute-start | bytes 165896 | tf_op jit(solution)/shard_map/ppermute | solution.py:22
  30.6 4.3 %collective-permute-start.6 = (f32[18,5,1,256]{3,2,1,0:T(1,128)S(1)}, f32[18,5,1,256]{3,2,1,0:T(1,128)S(1)}, u32[]{:S(2)}, u32[]{:S(2)}) collective-permute-start(f32[18,5,1,256]{3,2,1,0:T(1,128)S(1)} %get-tuple-element.147), channel_id=1, source_target_pairs={{0,1},{1,2},{2,3},{3,4},{4,5},{5,6},{6,7},{7,0},{8,9},{9,10},{10,1... | collective-permute-start | bytes 276488 | tf_op jit(solution)/shard_map/ppermute | solution.py:21
  33.4 4.0 %collective-permute-start.7 = (f32[18,5,1,256]{3,2,1,0:T(1,128)S(1)}, f32[18,5,1,256]{3,2,1,0:T(1,128)S(1)}, u32[]{:S(2)}, u32[]{:S(2)}) collective-permute-start(f32[18,5,1,256]{3,2,1,0:T(1,128)S(1)} %get-tuple-element.148), channel_id=1, source_target_pairs={{1,0},{2,1},{3,2},{4,3},{5,4},{6,5},{7,6},{0,7},{9,8},{10,9},{11,1... | collective-permute-start | bytes 276488 | tf_op jit(solution)/shard_map/ppermute | solution.py:22
  43.2 1.9 collective-permute-start.2
  43.2 4.6 %collective-permute-start.3 = (f32[3,20,2,256]{3,2,1,0:T(2,128)S(1)}, f32[3,20,2,256]{3,2,1,0:T(2,128)S(1)}, u32[]{:S(2)}, u32[]{:S(2)}) collective-permute-start(f32[3,20,2,256]{3,2,1,0:T(2,128)S(1)} %get-tuple-element.140), channel_id=1, source_target_pairs={{1,0},{2,1},{3,2},{4,3},{5,4},{6,5},{7,6},{0,7},{9,8},{10,9},{11,1... | collective-permute-start | bytes 368648 | tf_op jit(solution)/shard_map/ppermute | solution.py:22
  94.8 5.9 %collective-permute-start.8 = (f32[3,1,3,256]{3,2,1,0:T(4,128)S(1)}, f32[3,1,3,256]{3,2,1,0:T(4,128)S(1)}, u32[]{:S(2)}, u32[]{:S(2)}) collective-permute-start(f32[3,1,3,256]{3,2,1,0:T(4,128)S(1)} %get-tuple-element.162), channel_id=1, source_target_pairs={{0,8},{8,16},{16,24},{24,32},{32,40},{40,48},{48,56},{56,64},{64,7... | collective-permute-start | bytes 27656 | tf_op jit(solution)/shard_map/ppermute | solution.py:21
  95.4 5.6 %collective-permute-start.9 = (f32[3,1,3,256]{3,2,1,0:T(4,128)S(1)}, f32[3,1,3,256]{3,2,1,0:T(4,128)S(1)}, u32[]{:S(2)}, u32[]{:S(2)}) collective-permute-start(f32[3,1,3,256]{3,2,1,0:T(4,128)S(1)} %get-tuple-element.161), channel_id=1, source_target_pairs={{8,0},{16,8},{24,16},{32,24},{40,32},{48,40},{56,48},{64,56},{72,6... | collective-permute-start | bytes 27656 | tf_op jit(solution)/shard_map/ppermute | solution.py:22
  101.1 5.7 %collective-permute-start.10 = (f32[3,5,1,256]{3,2,1,0:T(1,128)S(1)}, f32[3,5,1,256]{3,2,1,0:T(1,128)S(1)}, u32[]{:S(2)}, u32[]{:S(2)}) collective-permute-start(f32[3,5,1,256]{3,2,1,0:T(1,128)S(1)} %get-tuple-element.159), channel_id=1, source_target_pairs={{0,1},{1,2},{2,3},{3,4},{4,5},{5,6},{6,7},{7,0},{8,9},{9,10},{10,1... | collective-permute-start | bytes 46088 | tf_op jit(solution)/shard_map/ppermute | solution.py:21
  101.9 4.9 %collective-permute-start.11 = (f32[3,5,1,256]{3,2,1,0:T(1,128)S(1)}, f32[3,5,1,256]{3,2,1,0:T(1,128)S(1)}, u32[]{:S(2)}, u32[]{:S(2)}) collective-permute-start(f32[3,5,1,256]{3,2,1,0:T(1,128)S(1)} %get-tuple-element.160), channel_id=1, source_target_pairs={{1,0},{2,1},{3,2},{4,3},{5,4},{6,5},{7,6},{0,7},{9,8},{10,9},{11,1... | collective-permute-start | bytes 46088 | tf_op jit(solution)/shard_map/ppermute | solution.py:22
  151.2 8.9 %collective-permute-start.13 = (f32[3,2,36,256]{3,2,1,0:T(8,128)S(1)}, f32[3,2,36,256]{3,2,1,0:T(8,128)S(1)}, u32[]{:S(2)}, u32[]{:S(2)}) collective-permute-start(f32[3,2,36,256]{3,2,1,0:T(8,128)S(1)} %get-tuple-element.125), channel_id=1, source_target_pairs={{8,0},{16,8},{24,16},{32,24},{40,32},{48,40},{56,48},{64,56},{72,6... | collective-permute-start | bytes 663560 | tf_op jit(solution)/shard_map/ppermute | solution.py:22
  157.0 8.4 %collective-permute-start.12 = (f32[3,2,36,256]{3,2,1,0:T(8,128)S(1)}, f32[3,2,36,256]{3,2,1,0:T(8,128)S(1)}, u32[]{:S(2)}, u32[]{:S(2)}) collective-permute-start(f32[3,2,36,256]{3,2,1,0:T(8,128)S(1)} %get-tuple-element.126), channel_id=1, source_target_pairs={{0,8},{8,16},{16,24},{24,32},{32,40},{40,48},{48,56},{56,64},{64,7... | collective-permute-start | bytes 663560 | tf_op jit(solution)/shard_map/ppermute | solution.py:21
  165.5 8.4 %collective-permute-start.15 = (f32[3,24,2,256]{3,2,1,0:T(2,128)S(1)}, f32[3,24,2,256]{3,2,1,0:T(2,128)S(1)}, u32[]{:S(2)}, u32[]{:S(2)}) collective-permute-start(f32[3,24,2,256]{3,2,1,0:T(2,128)S(1)} %get-tuple-element.115), channel_id=1, source_target_pairs={{1,0},{2,1},{3,2},{4,3},{5,4},{6,5},{7,6},{0,7},{9,8},{10,9},{11,1... | collective-permute-start | bytes 442376 | tf_op jit(solution)/shard_map/ppermute | solution.py:22
  169.9 2.4 collective-permute-start.14
  187.6 42.0 %collective-permute-start.16 = (f32[3,2,32,256]{3,2,1,0:T(8,128)S(1)}, f32[3,2,32,256]{3,2,1,0:T(8,128)S(1)}, u32[]{:S(2)}, u32[]{:S(2)}) collective-permute-start(f32[3,2,32,256]{3,2,1,0:T(8,128)S(1)} %get-tuple-element.143), channel_id=1, source_target_pairs={{0,8},{8,16},{16,24},{24,32},{32,40},{40,48},{48,56},{56,64},{64,7... | collective-permute-start | bytes 589832 | tf_op jit(solution)/shard_map/ppermute | solution.py:21
  187.6 41.9 %collective-permute-start.17 = (f32[3,2,32,256]{3,2,1,0:T(8,128)S(1)}, f32[3,2,32,256]{3,2,1,0:T(8,128)S(1)}, u32[]{:S(2)}, u32[]{:S(2)}) collective-permute-start(f32[3,2,32,256]{3,2,1,0:T(8,128)S(1)} %get-tuple-element.144), channel_id=1, source_target_pairs={{8,0},{16,8},{24,16},{32,24},{40,32},{48,40},{56,48},{64,56},{72,6... | collective-permute-start | bytes 589832 | tf_op jit(solution)/shard_map/ppermute | solution.py:22
  229.6 1.9 collective-permute-start.18
  229.6 4.6 %collective-permute-start.19 = (f32[3,20,2,256]{3,2,1,0:T(2,128)S(1)}, f32[3,20,2,256]{3,2,1,0:T(2,128)S(1)}, u32[]{:S(2)}, u32[]{:S(2)}) collective-permute-start(f32[3,20,2,256]{3,2,1,0:T(2,128)S(1)} %get-tuple-element.138), channel_id=1, source_target_pairs={{1,0},{2,1},{3,2},{4,3},{5,4},{6,5},{7,6},{0,7},{9,8},{10,9},{11,1... | collective-permute-start | bytes 368648 | tf_op jit(solution)/shard_map/ppermute | solution.py:22
  240.2 8.8 %collective-permute-start.20 = (f32[3,2,32,256]{3,2,1,0:T(8,128)S(1)}, f32[3,2,32,256]{3,2,1,0:T(8,128)S(1)}, u32[]{:S(2)}, u32[]{:S(2)}) collective-permute-start(f32[3,2,32,256]{3,2,1,0:T(8,128)S(1)} %get-tuple-element.141), channel_id=1, source_target_pairs={{0,8},{8,16},{16,24},{24,32},{32,40},{40,48},{48,56},{56,64},{64,7... | collective-permute-start | bytes 589832 | tf_op jit(solution)/shard_map/ppermute | solution.py:21
  241.7 7.3 %collective-permute-start.21 = (f32[3,2,32,256]{3,2,1,0:T(8,128)S(1)}, f32[3,2,32,256]{3,2,1,0:T(8,128)S(1)}, u32[]{:S(2)}, u32[]{:S(2)}) collective-permute-start(f32[3,2,32,256]{3,2,1,0:T(8,128)S(1)} %get-tuple-element.142), channel_id=1, source_target_pairs={{8,0},{16,8},{24,16},{32,24},{40,32},{48,40},{56,48},{64,56},{72,6... | collective-permute-start | bytes 589832 | tf_op jit(solution)/shard_map/ppermute | solution.py:22
  249.1 3.6 %collective-permute-start.22 = (f32[3,20,2,256]{3,2,1,0:T(2,128)S(1)}, f32[3,20,2,256]{3,2,1,0:T(2,128)S(1)}, u32[]{:S(2)}, u32[]{:S(2)}) collective-permute-start(f32[3,20,2,256]{3,2,1,0:T(2,128)S(1)} %get-tuple-element.135), channel_id=1, source_target_pairs={{0,1},{1,2},{2,3},{3,4},{4,5},{5,6},{6,7},{7,0},{8,9},{9,10},{10,1... | collective-permute-start | bytes 368648 | tf_op jit(solution)/shard_map/ppermute | solution.py:21
  250.9 4.6 %collective-permute-start.23 = (f32[3,20,2,256]{3,2,1,0:T(2,128)S(1)}, f32[3,20,2,256]{3,2,1,0:T(2,128)S(1)}, u32[]{:S(2)}, u32[]{:S(2)}) collective-permute-start(f32[3,20,2,256]{3,2,1,0:T(2,128)S(1)} %get-tuple-element.136), channel_id=1, source_target_pairs={{1,0},{2,1},{3,2},{4,3},{5,4},{6,5},{7,6},{0,7},{9,8},{10,9},{11,1... | collective-permute-start | bytes 368648 | tf_op jit(solution)/shard_map/ppermute | solution.py:22
  (18 other events, 285.0 us)
where the time goes:
time: 268 us; the launch traced here: 263 us
  matrix products  82.3 us (31%)
  starting transfers between devices  44.4 us (17%)
  other arithmetic  38.6 us (14%)
  blocking collectives  37 us (14%)
  local copies, waits for them, and re-layouts  31.5 us (12%)
  waiting for transfers between devices  27.4 us (10%)
    dot_general x1, matrix products, sample_field(): jnp.dot(field.reshape(-1, extent_z), table_z, precision=lax.Precision.HIG...  46.2 us
    ppermute x12, starting transfers between devices, with_halo(): after = lax.ppermute(leading, axis, down)  37.3 us
    all_gather x1, blocking collectives, on_device(): everyone = lax.all_gather(moved, ('gx', 'gy'), axis=1, tiled=True)  37 us
    dot_general x1, matrix products, deposit_field(): lax.dot_general(spread_xy.reshape(-1, count), table_z, (((1,), (1,)), (()...  35.5 us
    ppermute x12, waiting for transfers between devices, with_halo(): after = lax.ppermute(leading, axis, down)  13.8 us
    ppermute x12, waiting for transfers between devices, with_halo(): before = lax.ppermute(last, axis, up)  13.5 us
    ppermute x12, starting transfers between devices, with_halo(): before = lax.ppermute(last, axis, up)  7.09 us
    another operation x6, other arithmetic  6.33 us
  transfers between devices with their start and end apart: 24, of which 13 were waited for; matrix products, arithmetic and copies ran while one was open for 12% of the time, Pallas kernels for 0%

commit v1 on v0

v1 whole, which is shorter than its diff:
```python
import functools

import jax
import jax.numpy as jnp
from jax import lax
from jax.experimental import pallas as pl
from jax.experimental.pallas import tpu as pltpu
from jax.sharding import PartitionSpec as P

F32 = jnp.float32
BF16 = jnp.bfloat16
I32 = jnp.int32

ITERS = 4
DIFFUSION = 1.0
RESPONSE = 0.5
DASHPOT = 0.1

ROWS = 24
TILE = 256
WIN = 8
CYR = 112


TRAVEL = ((0, 0), (-1, 0), (1, 0), (-1, -1), (0, -1), (1, -1), (-1, 1), (0, 1), (1, 1))

VMEM = pl.BlockSpec(memory_space=pltpu.VMEM)
SMEM = pl.BlockSpec(memory_space=pltpu.SMEM)
HBM = pl.BlockSpec(memory_space=pltpu.HBM)


def params(mib):
    return pltpu.CompilerParams(vmem_limit_bytes=mib * 1024 * 1024)


def split(value):
    high = value.astype(BF16)
    low = (value - high.astype(F32)).astype(BF16)
    return high, low


def counting_ranks(bin_of, start_of, bins_here):
    markers = bin_of.shape[1]
    bins = (lax.broadcasted_iota(I32, (32, markers), 0) == bin_of).astype(F32)
    bins16 = bins.astype(BF16)
    ramp_i = lax.broadcasted_iota(I32, (TILE, TILE), 0)
    ramp_j = lax.broadcasted_iota(I32, (TILE, TILE), 1)
    upper = (ramp_i < ramp_j).astype(F32).astype(BF16)
    totals = lax.dot_general(
        jnp.ones((8, markers), BF16), bins16, (((1,), (1,)), ((), ())), preferred_element_type=F32
    )
    row = lax.broadcasted_iota(I32, (32, 32), 0)
    col = lax.broadcasted_iota(I32, (32, 32), 1)
    before = jnp.where(jnp.logical_and(col < row, row < bins_here), totals[0:1, :], 0.0)
    bin_row = lax.broadcasted_iota(I32, (32, 1), 0)
    start = jnp.where(
        bin_row < bins_here, jnp.sum(before, axis=1, keepdims=True), start_of(bin_row).astype(F32)
    )
    slots = []
    for b in range(markers // TILE):
        mine = bins[:, b * TILE : (b + 1) * TILE]
        ranks = jnp.dot(bins16[:, b * TILE : (b + 1) * TILE], upper, preferred_element_type=F32)
        slots.append(jnp.sum(mine * (ranks + start), axis=0, keepdims=True))
        start = start + jnp.sum(mine, axis=1, keepdims=True)
    return jnp.concatenate(slots, axis=1).astype(I32)


def gather_tile(both, slot, tile):
    place = lax.broadcasted_iota(I32, (TILE, slot.shape[1]), 0)
    pick = (slot - tile * TILE == place).astype(F32).astype(BF16)
    out = lax.dot_general(both, pick, (((1,), (1,)), ((), ())), preferred_element_type=F32)
    return out[0:ROWS] + out[ROWS : 2 * ROWS]


def halves(value):
    high, low = split(value)
    return jnp.concatenate([high.astype(F32), low.astype(F32)], axis=0).astype(BF16)


def route_kernel(
    where, motion, owner_h, bx_h, by_h, bz_h, weights_h, offset_h, velocity_h,
    to_left, to_right, middle, to_down, to_up, slot_out, both_out, linear,
    owner, bx, by, bz, weights, offset, vel, rec, sems, edge_sem, *, gx, gy_shift
):
    markers = owner.shape[1]
    blocks = markers // TILE
    nx, ny = vel.shape[1:3]
    moves = []
    for k, (src, dst) in enumerate(
        ((owner_h, owner), (bx_h, bx), (by_h, by), (bz_h, bz), (weights_h, weights), (offset_h, offset))
    ):
        move = pltpu.make_async_copy(src, dst, sems.at[k])
        move.start()
        moves.append(move)
    whole = pltpu.make_async_copy(velocity_h, vel, edge_sem.at[0])
    whole.start()
    for move in moves:
        move.wait()
    own = owner[...]
    step_x = (lax.shift_right_logical(own, gy_shift) - where[0] + 1) & (gx - 1)
    step_y = (own & ((1 << gy_shift) - 1)) - where[1] + 1
    lane = step_x * 3 + step_y
    bin_of = jnp.where(lane == 4, bx[...], 17 + lane)
    slot = counting_ranks(bin_of, lambda b: markers + (b - 17) * TILE, 17)
    slot_out[...] = slot

    first = lax.broadcasted_iota(I32, (1, markers), 1) < markers // 2
    speed = [jnp.where(first, motion[0, c], motion[1, c]) for c in range(6)]
    off = [offset[c : c + 1, :] for c in range(3)]
    target = [
        speed[0] + (speed[4] * off[2] - speed[5] * off[1]),
        speed[1] + (speed[5] * off[0] - speed[3] * off[2]),
        speed[2] + (speed[3] * off[1] - speed[4] * off[0]),
    ]
    rec[0:12, :] = weights[...]
    rec[12:13, :] = bx[...].astype(F32)
    rec[13:14, :] = by[...].astype(F32)
    rec[14:15, :] = bz[...].astype(F32)
    for c in range(3):
        rec[15 + c : 16 + c, :] = target[c]
    rec[18:21, :] = offset[...]
    rec[21:22, :] = jnp.where(first, 0.0, 1.0)
    rec[22:23, :] = jnp.ones((1, markers), F32)
    rec[23:24, :] = jnp.zeros((1, markers), F32)
    both = halves(rec[...])
    both_out[...] = both
    base = 6 * ny
    for k in range(3):
        to_left[base + k * ROWS : base + (k + 1) * ROWS, :] = gather_tile(both, slot, blocks + k)
        to_right[base + k * ROWS : base + (k + 1) * ROWS, :] = gather_tile(both, slot, blocks + 6 + k)
    middle[0] = gather_tile(both, slot, blocks + 3)
    middle[1] = gather_tile(both, slot, blocks + 5)

    lane_row = lax.broadcasted_iota(I32, (1, 128), 1)
    line = jnp.zeros((1, 128), F32)
    for s in range(2):
        for c in range(3):
            line = jnp.where(lane_row == 108 + 6 * s + c, motion[s, c], line)
    linear[...] = line
    whole.wait()
    for c in range(3):
        for x in range(2):
            rows = pl.ds((c * 2 + x) * ny, ny)
            to_left[rows, :] = vel[c, x]
            to_right[rows, :] = vel[c, nx - 2 + x]

    for x in range(nx):
        for c in range(3):
            at = (x + 2) * 6 + c * 2
            to_down[at : at + 2, :] = vel[c, x, 0:2, :]
            to_up[at : at + 2, :] = vel[c, x, ny - 2 : ny, :]


def home_kernel(slot, both, home):
    count = jnp.sum((slot[...] < slot.shape[1]).astype(F32)).astype(I32)
    for t in range(home.shape[0]):
        home[t] = jnp.zeros((ROWS, TILE), F32)

    def tile(t, carry):
        home[t] = gather_tile(both[...], slot[...], t)
        return carry

    lax.fori_loop(0, (count + TILE - 1) // TILE, tile, 0)


def turn_kernel(got_left, got_right, middle, own_down, own_up, to_down, to_up, *, nx, ny):
    base = 6 * ny
    lists = (nx + 4) * 6
    for out, own, cut, pick, mid in (
        (to_down, own_down, 0, 0, 0),
        (to_up, own_up, ny - 2, 2, 1),
    ):
        out[0:lists, :] = own[0:lists, :]
        for x in range(2):
            for c in range(3):
                at = (c * 2 + x) * ny + cut
                to = x * 6 + c * 2
                out[to : to + 2, :] = got_right[at : at + 2, :]
                to = (nx + 2 + x) * 6 + c * 2
                out[to : to + 2, :] = got_left[at : at + 2, :]
        out[lists : lists + ROWS, :] = got_left[base + pick * ROWS : base + (pick + 1) * ROWS, :]
        out[lists + ROWS : lists + 2 * ROWS, :] = middle[mid]
        out[lists + 2 * ROWS : lists + 3 * ROWS, :] = (
            got_right[base + pick * ROWS : base + (pick + 1) * ROWS, :]
        )


def chain(distance, rows):
    value = jnp.where(distance == 3, rows[3], 0.0)
    for k in (2, 1, 0):
        value = jnp.where(distance == k, rows[k], value)
    return value


def couple_kernel(
    vel, got_left, got_right, got_down, got_up, home, linear,
    part, send_l, send_r, message,
    fcat, lists, arrived, tn, tt, sacc, scat, sums,
):
    nx = vel.shape[1] + 4
    cells = vel.shape[2]
    tall = cells + 4
    zero_pad = jnp.zeros((CYR - 3 * tall, vel.shape[3]), F32)

    def fill_own(x, carry):
        for c in range(3):
            part[x + 2, c * tall + 2 : c * tall + 2 + cells, :] = vel[c, x]
        return carry

    lax.fori_loop(0, nx - 4, fill_own, 0)
    for x in range(2):
        for c in range(3):
            rows = pl.ds((c * 2 + x) * cells, cells)
            part[x, c * tall + 2 : c * tall + 2 + cells, :] = got_right[rows, :]
            part[nx - 2 + x, c * tall + 2 : c * tall + 2 + cells, :] = got_left[rows, :]

    zero2 = jnp.zeros((2, vel.shape[3]), F32)
    for x in range(nx):
        for c in range(3):
            rows = pl.ds(x * 6 + c * 2, 2)
            part[x, c * tall : c * tall + 2, :] = got_up[rows, :]
            part[x, c * tall + 2 + cells : (c + 1) * tall, :] = got_down[rows, :]
        part[x, 3 * tall : CYR, :] = zero_pad

    def fill_rest(x, carry):
        high, low = split(part[x])
        fcat[x, :, 0:256] = high
        fcat[x, :, 256:512] = low
        fcat[x, :, 512:768] = high
        for c in range(3):
            part[x, c * tall : c * tall + 2, :] = zero2
            part[x, c * tall + 2 + cells : (c + 1) * tall, :] = zero2
        return carry

    lax.fori_loop(0, nx, fill_rest, 0)
    for x in (0, 1, nx - 2, nx - 1):
        part[x] = jnp.zeros((CYR, vel.shape[3]), F32)

    base = 6 * cells + ROWS
    after = nx * 6
    arrived[:, 0:TILE] = got_left[base : base + ROWS, :]
    arrived[:, TILE : 2 * TILE] = got_right[base : base + ROWS, :]
    for k in range(3):
        rows = pl.ds(after + k * ROWS, ROWS)
        arrived[:, (2 + k) * TILE : (3 + k) * TILE] = got_down[rows, :]
        arrived[:, (5 + k) * TILE : (6 + k) * TILE] = got_up[rows, :]
    total_lanes = arrived.shape[1]
    lane_at = lax.broadcasted_iota(I32, (1, total_lanes), 1)
    arrived[23:24, :] = (1 + lax.shift_right_logical(lane_at, 8)).astype(F32)
    valid_all = arrived[22:23, :] > 0.5
    count = jnp.sum(arrived[22:23, :]).astype(I32)
    bin_all = jnp.where(valid_all, arrived[12:13, :].astype(I32), 17)
    slot = counting_ranks(bin_all, lambda b: 0 * b + total_lanes, 17)
    both = halves(arrived[...])
    blocks = home.shape[0]
    for t in range(blocks):
        lists[t] = home[t]
        lists[blocks + t] = jnp.zeros((ROWS, TILE), F32)

    def gather_one(t, carry):
        lists[blocks + t] = gather_tile(both, slot, t)
        return carry

    lax.fori_loop(0, (count + TILE - 1) // TILE, gather_one, 0)
    sums[...] = jnp.zeros(sums.shape, F32)

    row = lax.broadcasted_iota(I32, (CYR, 1), 0)
    comp = (row >= tall).astype(I32) + (row >= 2 * tall).astype(I32)
    y_of = jnp.where(row < 3 * tall, row - comp * tall, -100)
    comp = jnp.where(row < 3 * tall, comp, 3)
    z_of = lax.broadcasted_iota(I32, (256, TILE), 0)
    win_row = lax.broadcasted_iota(I32, (WIN, TILE), 0)
    group_of = lax.broadcasted_iota(I32, (128, TILE), 0)

    def tile_body(t, carry):
        rec = lists[t]
        valid = rec[22:23] > 0.5
        bxf = rec[12:13]
        x_first = jnp.min(jnp.where(valid, bxf, 99.0)).astype(I32)
        x_last = jnp.max(jnp.where(valid, bxf, -9.0)).astype(I32)
        windows = jnp.where(x_last < 0, 0, (x_last - x_first + 4 + WIN - 1) // WIN)

        @pl.when(windows > 0)
        def _():
            bxi = bxf.astype(I32)
            byi = rec[13:14].astype(I32)
            bzi = rec[14:15].astype(I32)
            table_z = chain((z_of - bzi) & 255, [rec[8 + k : 9 + k] for k in range(4)])
            high, low = split(table_z)
            tn[0:256, :] = high
            tn[256:512, :] = high
            tn[512:768, :] = low
            tt[:, 0:256] = high
            tt[:, 256:512] = high
            tt[:, 512:768] = low
            table_y = chain(y_of - byi, [rec[4 + k : 5 + k] for k in range(4)])
            sacc[...] = jnp.zeros(sacc.shape, F32)

            def window(w):
                begin = x_first + w * WIN
                x0 = jnp.minimum(begin, nx - WIN)
                x_at = win_row + x0
                table_x = chain(x_at - bxi, [rec[k : k + 1] for k in range(4)])
                return x0, jnp.where(x_at >= begin, table_x, 0.0)

            def sample(w, c):
                x0, table_x = window(w)
                block = fcat[pl.ds(x0, WIN)].reshape(WIN * CYR, 768)
                got = jnp.dot(block, tn[...], preferred_element_type=F32)
                total = sacc[...]
                for i in range(WIN):
                    total = total + table_x[i : i + 1] * got[i * CYR : (i + 1) * CYR]
                sacc[...] = total
                return c

            lax.fori_loop(0, windows, sample, 0)
            weighted = sacc[...] * table_y
            force = [
                rec[15 + c : 16 + c]
                - jnp.sum(jnp.where(comp == c, weighted, 0.0), axis=0, keepdims=True)
                for c in range(3)
            ]
            by_row = jnp.where(comp == 0, force[0], jnp.where(comp == 1, force[1], force[2]))
            plane = table_y * by_row

            def deposit(w, c):
                x0, table_x = window(w)
                for i in range(WIN):
                    hi, lo = split(table_x[i : i + 1] * plane)
                    scat[i, :, 0:256] = hi
                    scat[i, :, 256:512] = lo
                    scat[i, :, 512:768] = hi
                made = lax.dot_general(
                    scat[...].reshape(WIN * CYR, 768),
                    tt[...],
                    (((1,), (1,)), ((), ())),
                    preferred_element_type=F32,
                )
                part[pl.ds(x0, WIN)] += made.reshape(WIN, CYR, 256)
                return c

            lax.fori_loop(0, windows, deposit, 0)
            off = [rec[18 + c : 19 + c] for c in range(3)]
            turn = [
                off[1] * force[2] - off[2] * force[1],
                off[2] * force[0] - off[0] * force[2],
                off[0] * force[1] - off[1] * force[0],
            ]
            stack = jnp.concatenate(force + turn + [jnp.zeros((2, TILE), F32)], axis=0)
            group = (2.0 * rec[23:24] + rec[21:22]).astype(I32)
            member = (group_of == group).astype(F32).astype(BF16)
            found = lax.dot_general(
                member, halves(stack), (((1,), (1,)), ((), ())), preferred_element_type=F32
            )
            sums[:, 0:16] += found

        return carry

    lax.fori_loop(0, 2 * blocks, tile_body, 0)
    lane_of = lax.broadcasted_iota(I32, (128, 128), 1)
    low_part = pltpu.roll(sums[...], 120, axis=1)
    joined = jnp.where(lane_of < 6, sums[...] + low_part, 0.0)
    line = linear[...] + joined[0:1]
    for k in range(1, 18):
        line = line + pltpu.roll(joined[k : k + 1], 6 * k, axis=1)
    message[...] = jnp.broadcast_to(line, message.shape)
    for x in range(6):
        send_l[x] = part[x]
        send_r[x] = part[nx - 6 + x]


def motion(where, contact_own, contact_other, got, out, moved, *, gx, gy, per_sphere):
    here = where[0] * gy + where[1]
    data = got[...]
    total = jnp.zeros(data.shape, F32)
    devices = gx * gy
    for k, (dx, dy) in enumerate(TRAVEL):
        piece = data
        shift = (-(gy * dx + dy)) % devices
        if shift:
            piece = pltpu.roll(piece, shift, axis=0)
        if k:
            piece = pltpu.roll(piece, 128 - 12 * k, axis=1)
        total = total + piece
    linear = pltpu.roll(data, 128 - 108, axis=1)
    moved[...] = linear - (RESPONSE / per_sphere) * total
    lane = lax.broadcasted_iota(I32, (1, 128), 1)
    mine = moved[pl.ds(here, 1), :]
    spring = jnp.zeros((1, 128), F32)
    for k in range(contact_own.shape[0]):
        partner = contact_other[k]
        line = moved[pl.ds(lax.shift_right_logical(partner, 1), 1), :]
        local = contact_own[k] - here * 2
        which = partner & 1
        same = jnp.where(which == local, line, 0.0)
        higher = jnp.where(which < local, pltpu.roll(line, 6, axis=1), 0.0)
        lower = jnp.where(which > local, pltpu.roll(line, 122, axis=1), 0.0)
        of_own = jnp.logical_and(lane >= local * 6, lane < local * 6 + 3)
        spring = spring + jnp.where(of_own, same + higher + lower - mine, 0.0)
    out[...] = mine + DASHPOT * spring


def edges_kernel(
    where, contact_own, contact_other, got, part, got_l, got_r, low, high, line, moved,
    *, tall, gx, gy, per_sphere
):
    motion(where, contact_own, contact_other, got, line, moved, gx=gx, gy=gy, per_sphere=per_sphere)
    nx = part.shape[0]
    for x in range(nx + 4):
        for c in range(3):
            for ref, at in ((low, c * tall), (high, (c + 1) * tall - 6)):
                rows = pl.ds(at, 6)
                pieces = []
                if 2 <= x < nx + 2:
                    pieces.append(part[x - 2, rows, :])
                if x < 6:
                    pieces.append(got_l[x, rows, :])
                if x >= nx - 2:
                    pieces.append(got_r[x - (nx - 2), rows, :])
                total = pieces[0]
                for piece in pieces[1:]:
                    total = total + piece
                ref[x * 18 + c * 6 : x * 18 + c * 6 + 6, :] = total


def relax_kernel(where, part, got_l, got_r, low, high, out, rhs, va, vb, *, tall, rows):
    nx = part.shape[0]
    long = nx + 4
    high_y = tall + 4
    y_at = lax.broadcasted_iota(I32, (high_y, 1), 0) - 4 + where[1] * (tall - 4)
    inside = jnp.logical_and(y_at >= 0, y_at < rows)
    mask = jnp.broadcast_to(inside.astype(F32), (high_y, 256))
    factor = jnp.broadcast_to(
        jnp.where(inside, 1.0 / (1.0 + 6.0 * DIFFUSION), 0.0), (high_y, 256)
    )
    zero2 = jnp.zeros((2, 256), F32)

    def fill(x, sources):
        for c in range(3):
            rows_of = pl.ds(c * tall, tall)
            total = sources[0][0][sources[0][1], rows_of, :]
            for ref, at in sources[1:]:
                total = total + ref[at, rows_of, :]
            rhs[c, x, 0:2, :] = zero2
            rhs[c, x, high_y - 2 : high_y, :] = zero2
            rhs[c, x, 2 : 2 + tall, :] = total

    for x in range(6):
        fill(x, [(got_l, x)] + ([(part, x - 2)] if x >= 2 else []))
        fill(long - 6 + x, [(got_r, x)] + ([(part, nx - 4 + x)] if x < 4 else []))

    def middle(x, carry):
        fill(x, [(part, x - 2)])
        return carry

    lax.fori_loop(6, long - 6, middle, 0)
    for x in range(long):
        for c in range(3):
            at = pl.ds(x * 18 + c * 6, 6)
            rhs[c, x, 0:6, :] += low[at, :]
            rhs[c, x, high_y - 6 : high_y, :] += high[at, :]

    def finish(x, carry):
        for c in range(3):
            rhs[c, x] = rhs[c, x] * mask
        return carry

    lax.fori_loop(0, long, finish, 0)

    state = rhs
    for sweep in range(ITERS):
        target = (va, vb)[sweep % 2]
        last = sweep == ITERS - 1

        def layer(x, carry, state=state, target=target, last=last):
            for c in range(3):
                here = state[c, x]
                near = state[c, x - 1] + state[c, x + 1]
                near = near + (pltpu.roll(here, 1, axis=1) + pltpu.roll(here, 255, axis=1))
                near = near + (pltpu.roll(here, 1, axis=0) + pltpu.roll(here, high_y - 1, axis=0))
                new = (rhs[c, x] + DIFFUSION * near) * factor
                if last:
                    out[c, x - 4] = new[4 : high_y - 4]
                else:
                    target[c, x] = new
            return carry

        lax.fori_loop(sweep + 1, long - 1 - sweep, layer, 0, unroll=2)
        state = target


def on_device(
    velocity,
    owner_block,
    base_x,
    base_y,
    base_z,
    delta_weights,
    marker_offset,
    sphere_motion,
    contact_sphere,
    contact_partner,
):
    nx, ny, nz = velocity.shape[1:]
    gx = lax.axis_size("gx")
    gy = lax.axis_size("gy")
    where = jnp.stack([lax.axis_index("gx"), lax.axis_index("gy")]).astype(I32)
    markers = base_x.shape[0]
    spheres = sphere_motion.shape[1]
    per_sphere = markers // spheres
    blocks = markers // TILE
    tall = ny + 4
    x_up = [(i, (i + 1) % gx) for i in range(gx)]
    x_down = [(j, i) for i, j in x_up]
    y_up = [(i, i + 1) for i in range(gy - 1)]
    y_down = [(j, i) for i, j in y_up]

    def array(*shape, dtype=F32):
        return jax.ShapeDtypeStruct(shape, dtype)

    x_rows = 6 * ny + 3 * ROWS
    y_rows = 6 * (nx + 4) + 3 * ROWS
    to_left, to_right, middle, own_down, own_up, slot, both, linear = pl.pallas_call(
        functools.partial(route_kernel, gx=gx, gy_shift=gy.bit_length() - 1),
        out_shape=(
            array(x_rows, nz),
            array(x_rows, nz),
            array(2, ROWS, TILE),
            array(y_rows, nz),
            array(y_rows, nz),
            array(1, markers, dtype=I32),
            array(2 * ROWS, markers, dtype=BF16),
            array(1, 128),
        ),
        in_specs=[SMEM, SMEM] + [HBM] * 7,
        out_specs=(VMEM,) * 8,
        scratch_shapes=[
            pltpu.VMEM((1, markers), I32),
            pltpu.VMEM((1, markers), I32),
            pltpu.VMEM((1, markers), I32),
            pltpu.VMEM((1, markers), I32),
            pltpu.VMEM((12, markers), F32),
            pltpu.VMEM((3, markers), F32),
            pltpu.VMEM((3, nx, ny, nz), F32),
            pltpu.VMEM((ROWS, markers), F32),
            pltpu.SemaphoreType.DMA((6,)),
            pltpu.SemaphoreType.DMA((1,)),
        ],
        compiler_params=params(16),
        name="route",
    )(
        where,
        sphere_motion.T,
        owner_block.reshape(1, markers),
        base_x.reshape(1, markers),
        base_y.reshape(1, markers),
        base_z.reshape(1, markers),
        delta_weights,
        marker_offset,
        velocity,
    )
    got_left = lax.ppermute(to_left, "gx", x_down)
    got_right = lax.ppermute(to_right, "gx", x_up)
    home = pl.pallas_call(
        home_kernel,
        out_shape=array(blocks, ROWS, TILE),
        in_specs=[VMEM] * 2,
        out_specs=VMEM,
        compiler_params=params(8),
        cost_estimate=pl.CostEstimate(flops=2_000_000_000, bytes_accessed=0, transcendentals=0),
        name="home",
    )(slot, both)
    to_down, to_up = pl.pallas_call(
        functools.partial(turn_kernel, nx=nx, ny=ny),
        out_shape=(array(y_rows, nz),) * 2,
        in_specs=[VMEM] * 5,
        out_specs=(VMEM,) * 2,
        compiler_params=params(4),
        name="turn",
    )(got_left, got_right, middle, own_down, own_up)
    got_down = lax.ppermute(to_down, "gy", y_down)
    got_up = lax.ppermute(to_up, "gy", y_up)

    devices = gx * gy
    slab = array(6, CYR, nz)
    part, send_l, send_r, message = pl.pallas_call(
        couple_kernel,
        out_shape=(array(nx + 4, CYR, nz), slab, slab, array(devices, 128)),
        in_specs=[VMEM] * 7,
        out_specs=(VMEM,) * 4,
        scratch_shapes=[
            pltpu.VMEM((nx + 4, CYR, 768), BF16),
            pltpu.VMEM((2 * blocks, ROWS, TILE), F32),
            pltpu.VMEM((ROWS, markers), F32),
            pltpu.VMEM((768, 256), BF16),
            pltpu.VMEM((256, 768), BF16),
            pltpu.VMEM((CYR, TILE), F32),
            pltpu.VMEM((WIN, CYR, 768), BF16),
            pltpu.VMEM((128, 128), F32),
        ],
        compiler_params=params(24),
        name="couple",
    )(velocity, got_left, got_right, got_down, got_up, home, linear)

    got_r = lax.ppermute(send_l, "gx", x_down)
    got_l = lax.ppermute(send_r, "gx", x_up)
    everyone = lax.all_to_all(message, ("gx", "gy"), 0, 0, tiled=True)
    strip = array((nx + 8) * 18, nz)
    low, high, line = pl.pallas_call(
        functools.partial(edges_kernel, tall=tall, gx=gx, gy=gy, per_sphere=per_sphere),
        out_shape=(strip, strip, array(1, 128)),
        in_specs=[SMEM] * 3 + [VMEM] * 4,
        out_specs=(VMEM,) * 3,
        scratch_shapes=[pltpu.VMEM((devices, 128), F32)],
        compiler_params=params(4),
        name="edges",
    )(where, contact_sphere, contact_partner, everyone, part, got_l, got_r)
    found = line[0, 0 : 6 * spheres].reshape(spheres, 6).T
    new_motion = found + jnp.concatenate([jnp.zeros((3, spheres), F32), sphere_motion[3:6]], axis=0)

    got_high = lax.ppermute(low, "gy", y_down)
    got_low = lax.ppermute(high, "gy", y_up)
    grown = pltpu.VMEM((3, nx + 8, tall + 4, nz), F32)
    state = pl.pallas_call(
        functools.partial(relax_kernel, tall=tall, rows=ny * gy),
        out_shape=array(3, nx, ny, nz),
        in_specs=[SMEM] + [VMEM] * 5,
        out_specs=VMEM,
        scratch_shapes=[grown, grown, grown],
        compiler_params=params(16),
        name="relax",
    )(where, part, got_l, got_r, got_low, got_high)
    return (state, new_motion)


def solution(mesh):
    placed = (
        P(None, "gx", "gy", None),
        P(("gx", "gy"), None),
        P(("gx", "gy")),
        P(("gx", "gy")),
        P(("gx", "gy")),
        P(None, ("gx", "gy")),
        P(None, ("gx", "gy")),
        P(None, ("gx", "gy")),
        P(("gx", "gy")),
        P(("gx", "gy")),
    )
    return jax.shard_map(
        on_device,
        mesh=mesh,
        in_specs=placed,
        out_specs=(P(None, "gx", "gy", None), P(None, ("gx", "gy"))),
        check_vma=False,
    )
```

time: 268 us -> 110 us (0.41); the launches traced: 263 us -> 109 us
  matrix products: 82.3 us -> 0 us
  Pallas kernels: 0 us -> 39.5 us
  other arithmetic: 38.6 us -> 0.71 us
  local copies, waits for them, and re-layouts: 31.5 us -> 7.84 us
  starting transfers between devices: 44.4 us -> 23.4 us
  blocking collectives: 37 us -> 18.4 us
  waiting for transfers between devices: 27.4 us -> 18.7 us
    dot_general x5 -> x0, matrix products: 82.3 us -> none  [the longest x1 46.2 us: sample_field(): jnp.dot(field.reshape(-1, extent_z), table_z, precision=lax.Precision.HIG...]
    pallas_call x0 -> x6, Pallas kernels: none -> 39.5 us  [the longest x1 21.3 us: on_device(): pl.pallas_call(couple_kernel, out_shape=(array(nx + 4, CYR, nz), slab, sl...]
    all_gather x1 -> x0, blocking collectives: 37 us -> none  [on_device(): everyone = lax.all_gather(moved, ('gx', 'gy'), axis=1, tiled=True)]
    ppermute x24 -> x8, starting transfers between devices: 44.4 us -> 23.4 us  [the longest x1 6.84 us: on_device(): got_left = lax.ppermute(to_left, 'gx', x_down)]
    all_to_all x0 -> x1, blocking collectives: none -> 18.4 us  [on_device(): everyone = lax.all_to_all(message, ('gx', 'gy'), 0, 0, tiled=True)]
    slice x28 -> x2, local copies, waits for them, and re-layouts: 12 us -> 0.09 us  [the longest x1 0.07 us: on_device(): sphere_motion[3:6]]
    scatter-add x7 -> x0, other arithmetic: 9.96 us -> none  [the longest x1 1.7 us: on_device(): source.at[:, :, span_y - 2:].add(upper * rims[:, 4:span_x + 4, span_y + 6:])]
    ppermute x24 -> x8, waiting for transfers between devices: 27.4 us -> 18.7 us  [the longest x1 5.24 us: on_device(): got_right = lax.ppermute(to_right, 'gx', x_up)]
  transfers between devices with their start and end apart: 24 -> 8, of which waited for: 13 -> 5; matrix products, arithmetic and copies ran while one was open for 12% -> 1% of each run, Pallas kernels for 0% -> 1%
where the time goes in v1:
time: 110 us; the launch traced here: 109 us
  Pallas kernels  39.5 us (36%)
  starting transfers between devices  23.4 us (21%)
  waiting for transfers between devices  18.7 us (17%)
  blocking collectives  18.4 us (17%)
  local copies, waits for them, and re-layouts  7.84 us (7%)
    pallas_call x1, Pallas kernels, on_device(): pl.pallas_call(couple_kernel, out_shape=(array(nx + 4, CYR, nz), slab, sl...  21.3 us
    all_to_all x1, blocking collectives, on_device(): everyone = lax.all_to_all(message, ('gx', 'gy'), 0, 0, tiled=True)  18.4 us
    pallas_call x1, Pallas kernels, on_device(): pl.pallas_call(functools.partial(relax_kernel, tall=tall, rows=ny * gy),...  10.9 us
    unnamed x28, local copies, waits for them, and re-layouts  7.66 us
    ppermute x1, starting transfers between devices, on_device(): got_left = lax.ppermute(to_left, 'gx', x_down)  6.84 us
    ppermute x1, waiting for transfers between devices, on_device(): got_right = lax.ppermute(to_right, 'gx', x_up)  5.24 us
    ppermute x1, waiting for transfers between devices, on_device(): got_left = lax.ppermute(to_left, 'gx', x_down)  5.16 us
    ppermute x1, starting transfers between devices, on_device(): got_r = lax.ppermute(send_l, 'gx', x_down)  4.77 us
  transfers between devices with their start and end apart: 8, of which 5 were waited for; matrix products, arithmetic and copies ran while one was open for 1% of the time, Pallas kernels for 1%

profile of v1, /device:TPU:1, one launch (start us, length us, event | category | flops | bytes accessed | tf_op | source)
XLA Modules:
  0.0 109.3 jit_solution(10192961731271915386)
XLA Ops:
  0.7 1.4 %copy-done = f32[3,16,32,256]{3,2,1,0:T(8,128)S(1)} copy-done((f32[3,16,32,256]{3,2,1,0:T(8,128)S(1)}, f32[3,16,32,256]{3,2,1,0:T(8,128)}, u32[]{:S(2)}) %copy-start) | copy-done | bytes 1572888
  2.1 0.9 copy-done.4
  3.0 0.8 copy-done.5
  3.8 0.7 copy-done.6
  4.5 0.7 copy-done.7
  5.9 0.7 copy-done.9
  7.2 4.0 %route.1 = (f32[264,256]{1,0:T(8,128)S(1)}, f32[264,256]{1,0:T(8,128)S(1)}, f32[2,24,256]{2,1,0:T(8,128)S(1)}, f32[192,256]{1,0:T(8,128)S(1)}, f32[192,256]{1,0:...) custom-call(s32[2]{0:T(128)S(1)} %pad_add_fusion.where, ...), custom_call_target="tpu_custom_call" | custom-call | tf_op jit(solution)/shard_map/route/pallas_call | solution.py:523
  11.3 6.8 %collective-permute-start = (f32[264,256]{1,0:T(8,128)S(1)}, f32[264,256]{1,0:T(8,128)S(1)}, u32[]{:S(2)}, u32[]{:S(2)}) collective-permute-start(f32[264,256]{1,0:T(8,128)S(1)} %get-tuple-element.19), channel_id=1, source_target_pairs={{8,0},{16,8},{24,16},{32,24},{40,32},{48,40},{56,48},{64,56},{72,6... | collective-permute-start | bytes 811016 | tf_op jit(solution)/shard_map/ppermute | solution.py:562
  18.1 5.2 %collective-permute-done.got_left = f32[264,256]{1,0:T(8,128)S(1)} collective-permute-done((f32[264,256]{1,0:T(8,128)S(1)}, f32[264,256]{1,0:T(8,128)S(1)}, u32[]{:S(2)}, u32[]{:S(2)}) %collective-permute-start) | collective-permute-done | bytes 270368 | tf_op jit(solution)/shard_map/ppermute | solution.py:562
  23.3 5.2 %collective-permute-done.1.got_right = f32[264,256]{1,0:T(8,128)S(1)} collective-permute-done((f32[264,256]{1,0:T(8,128)S(1)}, f32[264,256]{1,0:T(8,128)S(1)}, u32[]{:S(2)}, u32[]{:S(2)}) %collective-permute-start.1) | collective-permute-done | bytes 270368 | tf_op jit(solution)/shard_map/ppermute | solution.py:563
  28.6 3.7 %collective-permute-start.2 = (f32[192,256]{1,0:T(8,128)S(1)}, f32[192,256]{1,0:T(8,128)S(1)}, u32[]{:S(2)}, u32[]{:S(2)}) collective-permute-start(f32[192,256]{1,0:T(8,128)S(1)} %get-tuple-element.24), channel_id=1, source_target_pairs={{1,0},{2,1},{3,2},{4,3},{5,4},{6,5},{7,6},{9,8},{10,9},{11,10},{12... | collective-permute-start | bytes 589832 | tf_op jit(solution)/shard_map/ppermute | solution.py:581
  32.3 3.1 %collective-permute-start.3 = (f32[192,256]{1,0:T(8,128)S(1)}, f32[192,256]{1,0:T(8,128)S(1)}, u32[]{:S(2)}, u32[]{:S(2)}) collective-permute-start(f32[192,256]{1,0:T(8,128)S(1)} %get-tuple-element.25), channel_id=1, source_target_pairs={{0,1},{1,2},{2,3},{3,4},{4,5},{5,6},{6,7},{8,9},{9,10},{10,11},{11... | collective-permute-start | bytes 589832 | tf_op jit(solution)/shard_map/ppermute | solution.py:582
  35.4 1.4 %home.1 = f32[8,24,256]{2,1,0:T(8,128)S(1)} custom-call(s32[1,2048]{1,0:T(1,128)S(1)} %get-tuple-element.26.slot, bf16[48,2048]{1,0:T(8,128)(2,1)S(1)} %get-tuple-element.27.both), custom_call_target="tpu_custom_call" | custom-call | flops 2000000000 | tf_op jit(solution)/shard_map/home/pallas_call | solution.py:564
  36.9 1.1 %collective-permute-done.3.got_up = f32[192,256]{1,0:T(8,128)S(1)} collective-permute-done((f32[192,256]{1,0:T(8,128)S(1)}, f32[192,256]{1,0:T(8,128)S(1)}, u32[]{:S(2)}, u32[]{:S(2)}) %collective-permute-start.3) | collective-permute-done | bytes 196640 | tf_op jit(solution)/shard_map/ppermute | solution.py:582
  38.0 21.3 %couple.1 = (f32[20,112,256]{2,1,0:T(8,128)S(1)}, f32[6,112,256]{2,1,0:T(8,128)S(1)}, f32[6,112,256]{2,1,0:T(8,128)S(1)}, f32[128,128]{1,0:T(8,128)S(1)}) custom-call(f32[3,16,32,256]{3,2,1,0:T(8,128)S(1)} %copy-done.1, f32[264,256]{1,0:T(8,128)S(1)} %collective-permute-done.got_left, f32[264,256]{1,0:T(8,128)S(1)} %collective-permute-done.1.got_right, ...), custom_call_target="tpu_custom_call" | custom-call | tf_op jit(solution)/shard_map/couple/pallas_call | solution.py:586
  59.4 4.8 %collective-permute-start.5 = (f32[6,112,256]{2,1,0:T(8,128)S(1)}, f32[6,112,256]{2,1,0:T(8,128)S(1)}, u32[]{:S(2)}, u32[]{:S(2)}) collective-permute-start(f32[6,112,256]{2,1,0:T(8,128)S(1)} %get-tuple-element.31), channel_id=1, source_target_pairs={{8,0},{16,8},{24,16},{32,24},{40,32},{48,40},{56,48},{64,56},{72,6... | collective-permute-start | bytes 2064392 | tf_op jit(solution)/shard_map/ppermute | solution.py:605
  64.2 18.4 %all_to_all.11 = f32[128,1,128]{2,1,0:T(1,128)S(1)} all-to-all(f32[128,1,128]{2,1,0:T(1,128)S(1)} %bitcast.14), channel_id=1, replica_groups=mesh['gx'=16,'gy'=8] {'gx','gy'}, dimensions={0} | all-to-all | bytes 131072 | tf_op jit(solution)/shard_map/all_to_all | solution.py:607
  82.6 1.8 %edges.1 = (f32[432,256]{1,0:T(8,128)}, f32[432,256]{1,0:T(8,128)}, f32[1,128]{1,0:T(1,128)S(1)}) custom-call(s32[2]{0:T(128)S(1)} %pad_add_fusion.where, s32[4]{0:T(128)S(1)} %copy-done.12, s32[4]{0:T(128)S(1)} %copy-done.13, f32[128,128]{1,0:T(8,128)S(1)} %bitcast.13, f32[20,112,256]{2,1,0:T(8,128)S(1)} %get-tuple-element.29.part, ...), custom_call_target="tpu_custom_call" | custom-call | tf_op jit(solution)/shard_map/edges/pallas_call | solution.py:609
  84.4 2.9 %collective-permute-start.6 = (f32[432,256]{1,0:T(8,128)}, f32[432,256]{1,0:T(8,128)S(1)}, u32[]{:S(2)}, u32[]{:S(2)}) collective-permute-start(f32[432,256]{1,0:T(8,128)} %get-tuple-element.33), channel_id=1, source_target_pairs={{0,1},{1,2},{2,3},{3,4},{4,5},{5,6},{6,7},{8,9},{9,10},{10,11},{11... | collective-permute-start | bytes 1327112 | tf_op jit(solution)/shard_map/ppermute | solution.py:622
  87.4 1.9 %collective-permute-start.7 = (f32[432,256]{1,0:T(8,128)}, f32[432,256]{1,0:T(8,128)}, u32[]{:S(2)}, u32[]{:S(2)}) collective-permute-start(f32[432,256]{1,0:T(8,128)} %get-tuple-element.34), channel_id=1, source_target_pairs={{1,0},{2,1},{3,2},{4,3},{5,4},{6,5},{7,6},{9,8},{10,9},{11,10},{12... | collective-permute-start | bytes 1327112 | tf_op jit(solution)/shard_map/ppermute | solution.py:621
  90.1 2.8 %collective-permute-done.6.low = f32[432,256]{1,0:T(8,128)S(1)} collective-permute-done((f32[432,256]{1,0:T(8,128)}, f32[432,256]{1,0:T(8,128)S(1)}, u32[]{:S(2)}, u32[]{:S(2)}) %collective-permute-start.6) | collective-permute-done | bytes 442400 | tf_op jit(solution)/shard_map/ppermute | solution.py:622
  92.9 4.4 %collective-permute-done.7.high = f32[432,256]{1,0:T(8,128)} collective-permute-done((f32[432,256]{1,0:T(8,128)}, f32[432,256]{1,0:T(8,128)}, u32[]{:S(2)}, u32[]{:S(2)}) %collective-permute-start.7) | collective-permute-done | bytes 442400 | tf_op jit(solution)/shard_map/ppermute | solution.py:621
  97.3 1.1 %copy-done.3 = f32[6,112,256]{2,1,0:T(8,128)S(1)} copy-done((f32[6,112,256]{2,1,0:T(8,128)S(1)}, f32[6,112,256]{2,1,0:T(8,128)}, u32[]{:S(2)}) %copy-start.3) | copy-done | bytes 688152
  98.4 10.9 %relax.1 = f32[3,16,32,256]{3,2,1,0:T(8,128)} custom-call(s32[2]{0:T(128)S(1)} %pad_add_fusion.where, f32[20,112,256]{2,1,0:T(8,128)S(1)} %get-tuple-element.29.part, f32[6,112,256]{2,1,0:T(8,128)S(1)} %collective-permute-done.4.got_l, f32[6,112,256]{2,1,0:T(8,128)S(1)} %copy-done.3, f32[432,256]{1,0:T(8,128)S(1)} %collective-permute-done.6.low, ...), custom_call_target="tpu_custom_call" | custom-call | tf_op jit(solution)/shard_map/relax/pallas_call | solution.py:624
  (32 shorter events, 2.4 us)
Async XLA Ops:
  0.7 1.4 %copy-start = (f32[3,16,32,256]{3,2,1,0:T(8,128)S(1)}, f32[3,16,32,256]{3,2,1,0:T(8,128)}, u32[]{:S(2)}) copy-start(f32[3,16,32,256]{3,2,1,0:T(8,128)} %vel.1) | copy-start | bytes 4718596
  2.1 0.9 copy-start.4
  3.0 0.8 copy-start.5
  3.8 0.7 copy-start.6
  4.5 0.7 copy-start.7
  5.2 0.7 copy-start.8
  5.9 0.7 copy-start.9
  6.6 0.7 copy-start.10
  11.3 12.0 %collective-permute-start = (f32[264,256]{1,0:T(8,128)S(1)}, f32[264,256]{1,0:T(8,128)S(1)}, u32[]{:S(2)}, u32[]{:S(2)}) collective-permute-start(f32[264,256]{1,0:T(8,128)S(1)} %get-tuple-element.19), channel_id=1, source_target_pairs={{8,0},{16,8},{24,16},{32,24},{40,32},{48,40},{56,48},{64,56},{72,6... | collective-permute-start | bytes 811016 | tf_op jit(solution)/shard_map/ppermute | solution.py:562
  18.1 10.4 %collective-permute-start.1 = (f32[264,256]{1,0:T(8,128)S(1)}, f32[264,256]{1,0:T(8,128)S(1)}, u32[]{:S(2)}, u32[]{:S(2)}) collective-permute-start(f32[264,256]{1,0:T(8,128)S(1)} %get-tuple-element.20), channel_id=1, source_target_pairs={{0,8},{8,16},{16,24},{24,32},{32,40},{40,48},{48,56},{56,64},{64,7... | collective-permute-start | bytes 811016 | tf_op jit(solution)/shard_map/ppermute | solution.py:563
  28.6 8.3 %collective-permute-start.2 = (f32[192,256]{1,0:T(8,128)S(1)}, f32[192,256]{1,0:T(8,128)S(1)}, u32[]{:S(2)}, u32[]{:S(2)}) collective-permute-start(f32[192,256]{1,0:T(8,128)S(1)} %get-tuple-element.24), channel_id=1, source_target_pairs={{1,0},{2,1},{3,2},{4,3},{5,4},{6,5},{7,6},{9,8},{10,9},{11,10},{12... | collective-permute-start | bytes 589832 | tf_op jit(solution)/shard_map/ppermute | solution.py:581
  32.3 5.7 %collective-permute-start.3 = (f32[192,256]{1,0:T(8,128)S(1)}, f32[192,256]{1,0:T(8,128)S(1)}, u32[]{:S(2)}, u32[]{:S(2)}) collective-permute-start(f32[192,256]{1,0:T(8,128)S(1)} %get-tuple-element.25), channel_id=1, source_target_pairs={{0,1},{1,2},{2,3},{3,4},{4,5},{5,6},{6,7},{8,9},{9,10},{10,11},{11... | collective-permute-start | bytes 589832 | tf_op jit(solution)/shard_map/ppermute | solution.py:582
  35.4 2.6 %copy-start.1 = (f32[3,16,32,256]{3,2,1,0:T(8,128)S(1)}, f32[3,16,32,256]{3,2,1,0:T(8,128)}, u32[]{:S(2)}) copy-start(f32[3,16,32,256]{3,2,1,0:T(8,128)} %vel.1) | copy-start | bytes 4718596
  36.9 45.7 %copy-start.12 = (s32[4]{0:T(128)S(1)}, s32[4]{0:T(128)}, u32[]{:S(2)}) copy-start(s32[4]{0:T(128)} %contact_own.1) | copy-start | bytes 52
  36.9 45.7 %copy-start.13 = (s32[4]{0:T(128)S(1)}, s32[4]{0:T(128)}, u32[]{:S(2)}) copy-start(s32[4]{0:T(128)} %contact_other.1) | copy-start | bytes 52
  59.4 23.2 %collective-permute-start.4 = (f32[6,112,256]{2,1,0:T(8,128)S(1)}, f32[6,112,256]{2,1,0:T(8,128)S(1)}, u32[]{:S(2)}, u32[]{:S(2)}) collective-permute-start(f32[6,112,256]{2,1,0:T(8,128)S(1)} %get-tuple-element.30), channel_id=1, source_target_pairs={{0,8},{8,16},{16,24},{24,32},{32,40},{40,48},{48,56},{56,64},{64,7... | collective-permute-start | bytes 2064392 | tf_op jit(solution)/shard_map/ppermute | solution.py:606
  59.4 23.2 %collective-permute-start.5 = (f32[6,112,256]{2,1,0:T(8,128)S(1)}, f32[6,112,256]{2,1,0:T(8,128)S(1)}, u32[]{:S(2)}, u32[]{:S(2)}) collective-permute-start(f32[6,112,256]{2,1,0:T(8,128)S(1)} %get-tuple-element.31), channel_id=1, source_target_pairs={{8,0},{16,8},{24,16},{32,24},{40,32},{48,40},{56,48},{64,56},{72,6... | collective-permute-start | bytes 2064392 | tf_op jit(solution)/shard_map/ppermute | solution.py:605
  82.6 1.8 %copy-start.2 = (f32[6,112,256]{2,1,0:T(8,128)}, f32[6,112,256]{2,1,0:T(8,128)S(1)}, u32[]{:S(2)}) copy-start(f32[6,112,256]{2,1,0:T(8,128)S(1)} %collective-permute-done.5.got_r) | copy-start | bytes 2064388
  82.6 6.7 %copy-start.11 = (f32[6,2]{0,1:T(2,128)S(1)}, f32[6,2]{0,1:T(2,128)}, u32[]{:S(2)}) copy-start(f32[6,2]{0,1:T(2,128)} %param.17) | copy-start | bytes 148
  84.4 8.5 %collective-permute-start.6 = (f32[432,256]{1,0:T(8,128)}, f32[432,256]{1,0:T(8,128)S(1)}, u32[]{:S(2)}, u32[]{:S(2)}) collective-permute-start(f32[432,256]{1,0:T(8,128)} %get-tuple-element.33), channel_id=1, source_target_pairs={{0,1},{1,2},{2,3},{3,4},{4,5},{5,6},{6,7},{8,9},{9,10},{10,11},{11... | collective-permute-start | bytes 1327112 | tf_op jit(solution)/shard_map/ppermute | solution.py:622
  87.4 9.9 %collective-permute-start.7 = (f32[432,256]{1,0:T(8,128)}, f32[432,256]{1,0:T(8,128)}, u32[]{:S(2)}, u32[]{:S(2)}) collective-permute-start(f32[432,256]{1,0:T(8,128)} %get-tuple-element.34), channel_id=1, source_target_pairs={{1,0},{2,1},{3,2},{4,3},{5,4},{6,5},{7,6},{9,8},{10,9},{11,10},{12... | collective-permute-start | bytes 1327112 | tf_op jit(solution)/shard_map/ppermute | solution.py:621
  97.3 1.1 %copy-start.3 = (f32[6,112,256]{2,1,0:T(8,128)S(1)}, f32[6,112,256]{2,1,0:T(8,128)}, u32[]{:S(2)}) copy-start(f32[6,112,256]{2,1,0:T(8,128)} %copy-done.2) | copy-start | bytes 2064388

commit v2 on v1

--- a/solution.py
+++ b/solution.py
@@ -18,6 +18,7 @@
 
 ROWS = 24
 TILE = 256
+UNROLL = 4
 WIN = 8
 CYR = 112
 
@@ -72,22 +73,36 @@
     return out[0:ROWS] + out[ROWS : 2 * ROWS]
 
 
+def sort_out(index, first, second, out_first, out_second):
+    even = (index & 1) == 0
+    out_first[...] = jnp.where(even, first[...], second[...])
+    out_second[...] = jnp.where(even, second[...], first[...])
+
+
 def halves(value):
     high, low = split(value)
     return jnp.concatenate([high.astype(F32), low.astype(F32)], axis=0).astype(BF16)
 
 
 def route_kernel(
-    where, motion, owner_h, bx_h, by_h, bz_h, weights_h, offset_h, velocity_h,
-    to_left, to_right, middle, to_down, to_up, slot_out, both_out, linear,
-    owner, bx, by, bz, weights, offset, vel, rec, sems, edge_sem, *, gx, gy_shift
+    where, motion_h, owner_h, bx_h, by_h, bz_h, weights_h, offset_h, velocity_h,
+    to_a, to_b, middle, to_down, to_up, slot_out, both_out, linear,
+    motion, owner, bx, by, bz, weights, offset, vel, rec, sems, edge_sem, *, gx, gy_shift
 ):
     markers = owner.shape[1]
     blocks = markers // TILE
     nx, ny = vel.shape[1:3]
     moves = []
     for k, (src, dst) in enumerate(
-        ((owner_h, owner), (bx_h, bx), (by_h, by), (bz_h, bz), (weights_h, weights), (offset_h, offset))
+        (
+            (owner_h, owner),
+            (bx_h, bx),
+            (by_h, by),
+            (bz_h, bz),
+            (weights_h, weights),
+            (offset_h, offset),
+            (motion_h, motion),
+        )
     ):
         move = pltpu.make_async_copy(src, dst, sems.at[k])
         move.start()
@@ -125,9 +140,11 @@
     both = halves(rec[...])
     both_out[...] = both
     base = 6 * ny
-    for k in range(3):
-        to_left[base + k * ROWS : base + (k + 1) * ROWS, :] = gather_tile(both, slot, blocks + k)
-        to_right[base + k * ROWS : base + (k + 1) * ROWS, :] = gather_tile(both, slot, blocks + 6 + k)
+    even = (where[0] & 1) == 0
+    for ref, up in ((to_a, even), (to_b, jnp.logical_not(even))):
+        tile = blocks + jnp.where(up, 6, 0)
+        for k in range(3):
+            ref[base + k * ROWS : base + (k + 1) * ROWS, :] = gather_tile(both, slot, tile + k)
     middle[0] = gather_tile(both, slot, blocks + 3)
     middle[1] = gather_tile(both, slot, blocks + 5)
 
@@ -141,8 +158,8 @@
     for c in range(3):
         for x in range(2):
             rows = pl.ds((c * 2 + x) * ny, ny)
-            to_left[rows, :] = vel[c, x]
-            to_right[rows, :] = vel[c, nx - 2 + x]
+            to_a[rows, :] = vel[c, jnp.where(even, nx - 2, 0) + x]
+            to_b[rows, :] = vel[c, jnp.where(even, 0, nx - 2) + x]
 
     for x in range(nx):
         for c in range(3):
@@ -163,12 +180,15 @@
     lax.fori_loop(0, (count + TILE - 1) // TILE, tile, 0)
 
 
-def turn_kernel(got_left, got_right, middle, own_down, own_up, to_down, to_up, *, nx, ny):
+def turn_kernel(
+    where, got_a, got_b, middle, own_down, own_up, to_a, to_b, got_left, got_right, down, up, *, nx, ny
+):
+    sort_out(where[0], got_a, got_b, got_left, got_right)
     base = 6 * ny
     lists = (nx + 4) * 6
     for out, own, cut, pick, mid in (
-        (to_down, own_down, 0, 0, 0),
-        (to_up, own_up, ny - 2, 2, 1),
+        (down, own_down, 0, 0, 0),
+        (up, own_up, ny - 2, 2, 1),
     ):
         out[0:lists, :] = own[0:lists, :]
         for x in range(2):
@@ -183,6 +203,7 @@
         out[lists + 2 * ROWS : lists + 3 * ROWS, :] = (
             got_right[base + pick * ROWS : base + (pick + 1) * ROWS, :]
         )
+    sort_out(where[1], up, down, to_a, to_b)
 
 
 def chain(distance, rows):
@@ -193,13 +214,15 @@
 
 
 def couple_kernel(
-    vel, got_left, got_right, got_down, got_up, home, linear,
-    part, send_l, send_r, message,
-    fcat, lists, arrived, tn, tt, sacc, scat, sums,
+    where, vel, got_xa, got_xb, got_ya, got_yb, home, linear,
+    part, send_a, send_b, message,
+    got_left, got_right, got_down, got_up, fcat, lists, arrived, tn, tt, sacc, scat, sums,
 ):
     nx = vel.shape[1] + 4
     cells = vel.shape[2]
     tall = cells + 4
+    sort_out(where[0], got_xa, got_xb, got_left, got_right)
+    sort_out(where[1], got_ya, got_yb, got_down, got_up)
     zero_pad = jnp.zeros((CYR - 3 * tall, vel.shape[3]), F32)
 
     def fill_own(x, carry):
@@ -364,9 +387,10 @@
     for k in range(1, 18):
         line = line + pltpu.roll(joined[k : k + 1], 6 * k, axis=1)
     message[...] = jnp.broadcast_to(line, message.shape)
+    even = (where[0] & 1) == 0
     for x in range(6):
-        send_l[x] = part[x]
-        send_r[x] = part[nx - 6 + x]
+        send_a[x] = part[jnp.where(even, nx - 6, 0) + x]
+        send_b[x] = part[jnp.where(even, 0, nx - 6) + x]
 
 
 def motion(where, contact_own, contact_other, got, out, moved, *, gx, gy, per_sphere):
@@ -401,11 +425,12 @@
 
 
 def edges_kernel(
-    where, contact_own, contact_other, got, part, got_l, got_r, low, high, line, moved,
-    *, tall, gx, gy, per_sphere
+    where, contact_own, contact_other, got, part, got_a, got_b, to_a, to_b, line,
+    moved, low, high, *, tall, gx, gy, per_sphere
 ):
     motion(where, contact_own, contact_other, got, line, moved, gx=gx, gy=gy, per_sphere=per_sphere)
     nx = part.shape[0]
+    even = (where[0] & 1) == 0
     for x in range(nx + 4):
         for c in range(3):
             for ref, at in ((low, c * tall), (high, (c + 1) * tall - 6)):
@@ -414,65 +439,78 @@
                 if 2 <= x < nx + 2:
                     pieces.append(part[x - 2, rows, :])
                 if x < 6:
-                    pieces.append(got_l[x, rows, :])
+                    pieces.append(jnp.where(even, got_b[x, rows, :], got_a[x, rows, :]))
                 if x >= nx - 2:
-                    pieces.append(got_r[x - (nx - 2), rows, :])
+                    y = x - (nx - 2)
+                    pieces.append(jnp.where(even, got_a[y, rows, :], got_b[y, rows, :]))
                 total = pieces[0]
                 for piece in pieces[1:]:
                     total = total + piece
                 ref[x * 18 + c * 6 : x * 18 + c * 6 + 6, :] = total
-
-
-def relax_kernel(where, part, got_l, got_r, low, high, out, rhs, va, vb, *, tall, rows):
+    sort_out(where[1], high, low, to_a, to_b)
+
+
+def middle_kernel(where, part, got_a, got_b, rhs, *, tall):
     nx = part.shape[0]
     long = nx + 4
     high_y = tall + 4
-    y_at = lax.broadcasted_iota(I32, (high_y, 1), 0) - 4 + where[1] * (tall - 4)
+    even = (where[0] & 1) == 0
+    zero2 = jnp.zeros((2, 256), F32)
+
+    def fill(x, sources):
+        for c in range(3):
+            rows_of = pl.ds(c * tall, tall)
+            total = sources[0](rows_of)
+            for source in sources[1:]:
+                total = total + source(rows_of)
+            rhs[c, x, 0:2, :] = zero2
+            rhs[c, x, high_y - 2 : high_y, :] = zero2
+            rhs[c, x, 2 : 2 + tall, :] = total
+
+    def from_part(at):
+        return lambda rows_of: part[at, rows_of, :]
+
+    def chosen(at, first, second):
+        return lambda rows_of: jnp.where(even, first[at, rows_of, :], second[at, rows_of, :])
+
+    for x in range(6):
+        fill(x, [chosen(x, got_b, got_a)] + ([from_part(x - 2)] if x >= 2 else []))
+        fill(
+            long - 6 + x,
+            [chosen(x, got_a, got_b)] + ([from_part(nx - 4 + x)] if x < 4 else []),
+        )
+
+    def centre(x, carry):
+        fill(x, [from_part(x - 2)])
+        return carry
+
+    lax.fori_loop(6, long - 6, centre, 0)
+
+
+def relax_kernel(where, grown, got_a, got_b, out_h, rhs, va, vb, low, high, out, sems, *, rows):
+    long, high_y = grown.shape[1:3]
+    span = high_y - 8
+    nx = long - 8
+    sort_out(where[1], got_b, got_a, low, high)
+    y_at = lax.broadcasted_iota(I32, (high_y, 1), 0) - 4 + where[1] * span
     inside = jnp.logical_and(y_at >= 0, y_at < rows)
     mask = jnp.broadcast_to(inside.astype(F32), (high_y, 256))
     factor = jnp.broadcast_to(
         jnp.where(inside, 1.0 / (1.0 + 6.0 * DIFFUSION), 0.0), (high_y, 256)
     )
-    zero2 = jnp.zeros((2, 256), F32)
-
-    def fill(x, sources):
-        for c in range(3):
-            rows_of = pl.ds(c * tall, tall)
-            total = sources[0][0][sources[0][1], rows_of, :]
-            for ref, at in sources[1:]:
-                total = total + ref[at, rows_of, :]
-            rhs[c, x, 0:2, :] = zero2
-            rhs[c, x, high_y - 2 : high_y, :] = zero2
-            rhs[c, x, 2 : 2 + tall, :] = total
-
-    for x in range(6):
-        fill(x, [(got_l, x)] + ([(part, x - 2)] if x >= 2 else []))
-        fill(long - 6 + x, [(got_r, x)] + ([(part, nx - 4 + x)] if x < 4 else []))
-
-    def middle(x, carry):
-        fill(x, [(part, x - 2)])
-        return carry
-
-    lax.fori_loop(6, long - 6, middle, 0)
+    gap = jnp.zeros((high_y - 12, 256), F32)
     for x in range(long):
         for c in range(3):
             at = pl.ds(x * 18 + c * 6, 6)
-            rhs[c, x, 0:6, :] += low[at, :]
-            rhs[c, x, high_y - 6 : high_y, :] += high[at, :]
-
-    def finish(x, carry):
-        for c in range(3):
-            rhs[c, x] = rhs[c, x] * mask
-        return carry
-
-    lax.fori_loop(0, long, finish, 0)
+            edge = jnp.concatenate([low[at, :], gap, high[at, :]], axis=0)
+            rhs[c, x] = (grown[c, x] + edge) * mask
 
     state = rhs
     for sweep in range(ITERS):
         target = (va, vb)[sweep % 2]
         last = sweep == ITERS - 1
 
-        def layer(x, carry, state=state, target=target, last=last):
+        def layer(x, state=state, target=target, last=last):
             for c in range(3):
                 here = state[c, x]
                 near = state[c, x - 1] + state[c, x + 1]
@@ -483,10 +521,22 @@
                     out[c, x - 4] = new[4 : high_y - 4]
                 else:
                     target[c, x] = new
+
+        def group(g, carry, sweep=sweep, layer=layer, last=last):
+            for k in range(UNROLL):
+                layer(jnp.minimum(sweep + 1 + g * UNROLL + k, long - 2 - sweep))
+            if last:
+                for c in range(3):
+                    part = pl.ds(g * UNROLL, UNROLL)
+                    pltpu.make_async_copy(out.at[c, part], out_h.at[c, part], sems.at[g * 3 + c]).start()
             return carry
 
-        lax.fori_loop(sweep + 1, long - 1 - sweep, layer, 0, unroll=2)
+        lax.fori_loop(0, (long - 2 - 2 * sweep + UNROLL - 1) // UNROLL, group, 0)
         state = target
+    for g in range(nx // UNROLL):
+        for c in range(3):
+            part = pl.ds(g * UNROLL, UNROLL)
+            pltpu.make_async_copy(out.at[c, part], out_h.at[c, part], sems.at[g * 3 + c]).wait()
 
 
 def on_device(
@@ -510,17 +560,34 @@
     per_sphere = markers // spheres
     blocks = markers // TILE
     tall = ny + 4
-    x_up = [(i, (i + 1) % gx) for i in range(gx)]
-    x_down = [(j, i) for i, j in x_up]
-    y_up = [(i, i + 1) for i in range(gy - 1)]
-    y_down = [(j, i) for i, j in y_up]
+
+    def pairs(size, first, wrap):
+        both_ways = []
+        for i in range(first, size, 2):
+            j = (i + 1) % size
+            if j or wrap:
+                both_ways += [(i, j), (j, i)]
+        return both_ways
+
+    def swap_x(first, second):
+        return (
+            lax.ppermute(first, "gx", pairs(gx, 0, True)),
+            lax.ppermute(second, "gx", pairs(gx, 1, True)),
+        )
+
+    def swap_y(first, second):
+        return (
+            lax.ppermute(first, "gy", pairs(gy, 0, False)),
+            lax.ppermute(second, "gy", pairs(gy, 1, False)),
+        )
+
 
     def array(*shape, dtype=F32):
         return jax.ShapeDtypeStruct(shape, dtype)
 
     x_rows = 6 * ny + 3 * ROWS
     y_rows = 6 * (nx + 4) + 3 * ROWS
-    to_left, to_right, middle, own_down, own_up, slot, both, linear = pl.pallas_call(
+    to_a, to_b, middle, own_down, own_up, slot, both, linear = pl.pallas_call(
         functools.partial(route_kernel, gx=gx, gy_shift=gy.bit_length() - 1),
         out_shape=(
             array(x_rows, nz),
@@ -532,9 +599,10 @@
             array(2 * ROWS, markers, dtype=BF16),
             array(1, 128),
         ),
-        in_specs=[SMEM, SMEM] + [HBM] * 7,
+        in_specs=[SMEM] + [HBM] * 8,
         out_specs=(VMEM,) * 8,
         scratch_shapes=[
+            pltpu.SMEM((spheres, 6), F32),
             pltpu.VMEM((1, markers), I32),
             pltpu.VMEM((1, markers), I32),
             pltpu.VMEM((1, markers), I32),
@@ -543,24 +611,28 @@
             pltpu.VMEM((3, markers), F32),
             pltpu.VMEM((3, nx, ny, nz), F32),
             pltpu.VMEM((ROWS, markers), F32),
-            pltpu.SemaphoreType.DMA((6,)),
+            pltpu.SemaphoreType.DMA((7,)),
             pltpu.SemaphoreType.DMA((1,)),
         ],
         compiler_params=params(16),
         name="route",
     )(
         where,
-        sphere_motion.T,
-        owner_block.reshape(1, markers),
-        base_x.reshape(1, markers),
-        base_y.reshape(1, markers),
-        base_z.reshape(1, markers),
-        delta_weights,
-        marker_offset,
-        velocity,
+        *(
+            pltpu.with_memory_space_constraint(a, pltpu.HBM)
+            for a in (
+                sphere_motion.T,
+                owner_block.reshape(1, markers),
+                base_x.reshape(1, markers),
+                base_y.reshape(1, markers),
+                base_z.reshape(1, markers),
+                delta_weights,
+                marker_offset,
+                velocity,
+            )
+        ),
     )
-    got_left = lax.ppermute(to_left, "gx", x_down)
-    got_right = lax.ppermute(to_right, "gx", x_up)
+    got_xa, got_xb = swap_x(to_a, to_b)
     home = pl.pallas_call(
         home_kernel,
         out_shape=array(blocks, ROWS, TILE),
@@ -570,25 +642,32 @@
         cost_estimate=pl.CostEstimate(flops=2_000_000_000, bytes_accessed=0, transcendentals=0),
         name="home",
     )(slot, both)
-    to_down, to_up = pl.pallas_call(
-        functools.partial(turn_kernel, nx=nx, ny=ny),
-        out_shape=(array(y_rows, nz),) * 2,
-        in_specs=[VMEM] * 5,
-        out_specs=(VMEM,) * 2,
-        compiler_params=params(4),
-        name="turn",
-    )(got_left, got_right, middle, own_down, own_up)
-    got_down = lax.ppermute(to_down, "gy", y_down)
-    got_up = lax.ppermute(to_up, "gy", y_up)
+    x_buffer = pltpu.VMEM((x_rows, nz), F32)
+    y_buffer = pltpu.VMEM((y_rows, nz), F32)
+    got_ya, got_yb = swap_y(
+        *pl.pallas_call(
+            functools.partial(turn_kernel, nx=nx, ny=ny),
+            out_shape=(array(y_rows, nz),) * 2,
+            in_specs=[SMEM] + [VMEM] * 5,
+            out_specs=(VMEM,) * 2,
+            scratch_shapes=[x_buffer, x_buffer, y_buffer, y_buffer],
+            compiler_params=params(4),
+            name="turn",
+        )(where, got_xa, got_xb, middle, own_down, own_up)
+    )
 
     devices = gx * gy
     slab = array(6, CYR, nz)
-    part, send_l, send_r, message = pl.pallas_call(
+    part, send_a, send_b, message = pl.pallas_call(
         couple_kernel,
         out_shape=(array(nx + 4, CYR, nz), slab, slab, array(devices, 128)),
-        in_specs=[VMEM] * 7,
+        in_specs=[SMEM] + [VMEM] * 7,
         out_specs=(VMEM,) * 4,
         scratch_shapes=[
+            x_buffer,
+            x_buffer,
+            y_buffer,
+            y_buffer,
             pltpu.VMEM((nx + 4, CYR, 768), BF16),
             pltpu.VMEM((2 * blocks, ROWS, TILE), F32),
             pltpu.VMEM((ROWS, markers), F32),
@@ -600,36 +679,51 @@
         ],
         compiler_params=params(24),
         name="couple",
-    )(velocity, got_left, got_right, got_down, got_up, home, linear)
-
-    got_r = lax.ppermute(send_l, "gx", x_down)
-    got_l = lax.ppermute(send_r, "gx", x_up)
+    )(where, velocity, got_xa, got_xb, got_ya, got_yb, home, linear)
+
+    got_a, got_b = swap_x(send_a, send_b)
     everyone = lax.all_to_all(message, ("gx", "gy"), 0, 0, tiled=True)
     strip = array((nx + 8) * 18, nz)
-    low, high, line = pl.pallas_call(
+    strip_buffer = pltpu.VMEM(strip.shape, F32)
+    to_ya, to_yb, line = pl.pallas_call(
         functools.partial(edges_kernel, tall=tall, gx=gx, gy=gy, per_sphere=per_sphere),
         out_shape=(strip, strip, array(1, 128)),
         in_specs=[SMEM] * 3 + [VMEM] * 4,
         out_specs=(VMEM,) * 3,
-        scratch_shapes=[pltpu.VMEM((devices, 128), F32)],
+        scratch_shapes=[pltpu.VMEM((devices, 128), F32), strip_buffer, strip_buffer],
         compiler_params=params(4),
         name="edges",
-    )(where, contact_sphere, contact_partner, everyone, part, got_l, got_r)
+    )(where, contact_sphere, contact_partner, everyone, part, got_a, got_b)
     found = line[0, 0 : 6 * spheres].reshape(spheres, 6).T
     new_motion = found + jnp.concatenate([jnp.zeros((3, spheres), F32), sphere_motion[3:6]], axis=0)
-
-    got_high = lax.ppermute(low, "gy", y_down)
-    got_low = lax.ppermute(high, "gy", y_up)
-    grown = pltpu.VMEM((3, nx + 8, tall + 4, nz), F32)
+    got_ea, got_eb = swap_y(to_ya, to_yb)
+    grown = pl.pallas_call(
+        functools.partial(middle_kernel, tall=tall),
+        out_shape=array(3, nx + 8, tall + 4, nz),
+        in_specs=[SMEM] + [VMEM] * 3,
+        out_specs=VMEM,
+        compiler_params=params(4),
+        cost_estimate=pl.CostEstimate(flops=2_000_000_000, bytes_accessed=0, transcendentals=0),
+        name="middle",
+    )(where, part, got_a, got_b)
+    buffer = pltpu.VMEM(grown.shape, F32)
     state = pl.pallas_call(
-        functools.partial(relax_kernel, tall=tall, rows=ny * gy),
+        functools.partial(relax_kernel, rows=ny * gy),
         out_shape=array(3, nx, ny, nz),
-        in_specs=[SMEM] + [VMEM] * 5,
-        out_specs=VMEM,
-        scratch_shapes=[grown, grown, grown],
-        compiler_params=params(16),
+        in_specs=[SMEM] + [VMEM] * 3,
+        out_specs=HBM,
+        scratch_shapes=[
+            buffer,
+            buffer,
+            buffer,
+            strip_buffer,
+            strip_buffer,
+            pltpu.VMEM((3, nx, ny, nz), F32),
+            pltpu.SemaphoreType.DMA((3 * (nx // UNROLL),)),
+        ],
+        compiler_params=params(20),
         name="relax",
-    )(where, part, got_l, got_r, got_low, got_high)
+    )(where, grown, got_ea, got_eb)
     return (state, new_motion)
 
 

time: 110 us -> 98.9 us (0.90); the launches traced: 109 us -> 99.4 us
  blocking collectives: 18.4 us -> 0 us
  waiting for transfers between devices: 18.7 us -> 28 us
  local copies, waits for them, and re-layouts: 7.84 us -> 0.2 us
  starting transfers between devices: 23.4 us -> 27.1 us
  Pallas kernels: 39.5 us -> 42.7 us
    all_to_all x1 -> x0, blocking collectives: 18.4 us -> none  [on_device(): everyone = lax.all_to_all(message, ('gx', 'gy'), 0, 0, tiled=True)]
    all_to_all x0 -> x1, waiting for transfers between devices: none -> 14.8 us  [on_device(): everyone = lax.all_to_all(message, ('gx', 'gy'), 0, 0, tiled=True)]
    all_to_all x0 -> x1, starting transfers between devices: none -> 7.8 us  [on_device(): everyone = lax.all_to_all(message, ('gx', 'gy'), 0, 0, tiled=True)]
    unnamed x28 -> x8, local copies, waits for them, and re-layouts: 7.66 us -> 0.03 us
    ppermute x8, waiting for transfers between devices: 18.7 us -> 13.2 us  [the longest x2 7.25 us: swap_y(): lax.ppermute(second, 'gy', pairs(gy, 1, False))]
    ppermute x8, starting transfers between devices: 23.4 us -> 19.3 us  [the longest x2 9.16 us: swap_x(): lax.ppermute(second, 'gx', pairs(gx, 1, True))]
    pallas_call x1 -> x2, Pallas kernels: 10.9 us -> 10.8 us  [the longest x1 9.24 us: on_device(): pl.pallas_call(functools.partial(relax_kernel, rows=ny * gy), out_shape=a...]
  transfers between devices with their start and end apart: 8 -> 9, of which waited for: 5 -> 5; matrix products, arithmetic and copies ran while one was open for 1% -> 1% of each run, Pallas kernels for 1% -> 4%
where the time goes in v2:
time: 98.9 us; the launch traced here: 99.4 us
  Pallas kernels  42.7 us (43%)
  waiting for transfers between devices  28 us (28%)
  starting transfers between devices  27.1 us (27%)
    pallas_call x1, Pallas kernels, on_device(): pl.pallas_call(couple_kernel, out_shape=(array(nx + 4, CYR, nz), slab, sl...  21.8 us
    all_to_all x1, waiting for transfers between devices, on_device(): everyone = lax.all_to_all(message, ('gx', 'gy'), 0, 0, tiled=True)  14.8 us
    pallas_call x1, Pallas kernels, on_device(): pl.pallas_call(functools.partial(relax_kernel, rows=ny * gy), out_shape=a...  9.24 us
    ppermute x2, starting transfers between devices, swap_x(): lax.ppermute(second, 'gx', pairs(gx, 1, True))  9.16 us
    all_to_all x1, starting transfers between devices, on_device(): everyone = lax.all_to_all(message, ('gx', 'gy'), 0, 0, tiled=True)  7.8 us
    ppermute x2, waiting for transfers between devices, swap_y(): lax.ppermute(second, 'gy', pairs(gy, 1, False))  7.25 us
    ppermute x2, starting transfers between devices, swap_y(): lax.ppermute(second, 'gy', pairs(gy, 1, False))  5.01 us
    pallas_call x1, Pallas kernels, on_device(): pl.pallas_call(functools.partial(route_kernel, gx=gx, gy_shift=gy.bit_len...  4.64 us
  transfers between devices with their start and end apart: 9, of which 5 were waited for; matrix products, arithmetic and copies ran while one was open for 1% of the time, Pallas kernels for 4%

profile of v2, /device:TPU:1, one launch (start us, length us, event | category | flops | bytes accessed | tf_op | source)
XLA Modules:
  0.0 99.4 jit_solution(1253701434656520140)
XLA Ops:
  0.6 0.1 pad_add_fusion.where
  0.7 4.6 %route.1 = (f32[264,256]{1,0:T(8,128)S(1)}, f32[264,256]{1,0:T(8,128)S(1)}, f32[2,24,256]{2,1,0:T(8,128)S(1)}, f32[192,256]{1,0:T(8,128)S(1)}, f32[192,256]{1,0:...) custom-call(s32[2]{0:T(128)S(1)} %pad_add_fusion.where, f32[2,6]{1,0:T(2,128)} %bitcast.18, ...), custom_call_target="tpu_custom_call" | custom-call | tf_op jit(solution)/shard_map/route/pallas_call | solution.py:590
  5.4 2.5 %collective-permute-start = (f32[264,256]{1,0:T(8,128)S(1)}, f32[264,256]{1,0:T(8,128)S(1)}, u32[]{:S(2)}, u32[]{:S(2)}) collective-permute-start(f32[264,256]{1,0:T(8,128)S(1)} %get-tuple-element.19), channel_id=1, source_target_pairs={{0,8},{8,0},{16,24},{24,16},{32,40},{40,32},{48,56},{56,48},{64,72... | collective-permute-start | bytes 811016 | tf_op jit(solution)/shard_map/ppermute | solution.py:574
  7.9 4.4 %collective-permute-start.1 = (f32[264,256]{1,0:T(8,128)S(1)}, f32[264,256]{1,0:T(8,128)S(1)}, u32[]{:S(2)}, u32[]{:S(2)}) collective-permute-start(f32[264,256]{1,0:T(8,128)S(1)} %get-tuple-element.20), channel_id=1, source_target_pairs={{8,16},{16,8},{24,32},{32,24},{40,48},{48,40},{56,64},{64,56},{72,... | collective-permute-start | bytes 811016 | tf_op jit(solution)/shard_map/ppermute | solution.py:575
  12.3 1.7 %collective-permute-done.got_a.got_xa = f32[264,256]{1,0:T(8,128)S(1)} collective-permute-done((f32[264,256]{1,0:T(8,128)S(1)}, f32[264,256]{1,0:T(8,128)S(1)}, u32[]{:S(2)}, u32[]{:S(2)}) %collective-permute-start) | collective-permute-done | bytes 270368 | tf_op jit(solution)/shard_map/ppermute | solution.py:574
  14.1 4.2 %collective-permute-done.1.got_b.got_xb = f32[264,256]{1,0:T(8,128)S(1)} collective-permute-done((f32[264,256]{1,0:T(8,128)S(1)}, f32[264,256]{1,0:T(8,128)S(1)}, u32[]{:S(2)}, u32[]{:S(2)}) %collective-permute-start.1) | collective-permute-done | bytes 270368 | tf_op jit(solution)/shard_map/ppermute | solution.py:575
  18.3 0.6 turn.1
  18.9 1.9 %collective-permute-start.2 = (f32[192,256]{1,0:T(8,128)S(1)}, f32[192,256]{1,0:T(8,128)S(1)}, u32[]{:S(2)}, u32[]{:S(2)}) collective-permute-start(f32[192,256]{1,0:T(8,128)S(1)} %get-tuple-element.24), channel_id=1, source_target_pairs={{0,1},{1,0},{2,3},{3,2},{4,5},{5,4},{6,7},{7,6},{8,9},{9,8},{10,11... | collective-permute-start | bytes 589832 | tf_op jit(solution)/shard_map/ppermute | solution.py:580
  20.8 3.1 %collective-permute-start.3 = (f32[192,256]{1,0:T(8,128)S(1)}, f32[192,256]{1,0:T(8,128)S(1)}, u32[]{:S(2)}, u32[]{:S(2)}) collective-permute-start(f32[192,256]{1,0:T(8,128)S(1)} %get-tuple-element.25), channel_id=1, source_target_pairs={{1,2},{2,1},{3,4},{4,3},{5,6},{6,5},{9,10},{10,9},{11,12},{12,11},... | collective-permute-start | bytes 589832 | tf_op jit(solution)/shard_map/ppermute | solution.py:581
  23.9 2.3 %home.1 = f32[8,24,256]{2,1,0:T(8,128)S(1)} custom-call(s32[1,2048]{1,0:T(1,128)S(1)} %get-tuple-element.26.slot, bf16[48,2048]{1,0:T(8,128)(2,1)S(1)} %get-tuple-element.27.both), custom_call_target="tpu_custom_call" | custom-call | flops 2000000000 | tf_op jit(solution)/shard_map/home/pallas_call | solution.py:636
  26.3 1.5 %collective-permute-done.3.got_yb = f32[192,256]{1,0:T(8,128)S(1)} collective-permute-done((f32[192,256]{1,0:T(8,128)S(1)}, f32[192,256]{1,0:T(8,128)S(1)}, u32[]{:S(2)}, u32[]{:S(2)}) %collective-permute-start.3) | collective-permute-done | bytes 196640 | tf_op jit(solution)/shard_map/ppermute | solution.py:581
  27.8 21.8 %couple.1 = (f32[20,112,256]{2,1,0:T(8,128)S(1)}, f32[6,112,256]{2,1,0:T(8,128)}, f32[6,112,256]{2,1,0:T(8,128)}, f32[128,128]{1,0:T(8,128)}) custom-call(s32[2]{0:T(128)S(1)} %pad_add_fusion.where, f32[3,16,32,256]{3,2,1,0:T(8,128)S(1)} %copy-done, f32[264,256]{1,0:T(8,128)S(1)} %collective-permute-done.got_a.got_xa, ...), custom_call_target="tpu_custom_call" | custom-call | tf_op jit(solution)/shard_map/couple/pallas_call | solution.py:661
  49.6 4.7 %collective-permute-start.5 = (f32[6,112,256]{2,1,0:T(8,128)}, f32[6,112,256]{2,1,0:T(8,128)}, u32[]{:S(2)}, u32[]{:S(2)}) collective-permute-start(f32[6,112,256]{2,1,0:T(8,128)} %get-tuple-element.31), channel_id=1, source_target_pairs={{8,16},{16,8},{24,32},{32,24},{40,48},{48,40},{56,64},{64,56},{72,... | collective-permute-start | bytes 2064392 | tf_op jit(solution)/shard_map/ppermute | solution.py:575
  54.3 7.8 %all-to-all-start = ((f32[128,1,128]{2,1,0:T(1,128)}), f32[128,1,128]{2,1,0:T(1,128)S(1)}, u32[]{:S(2)}, u32[]{:S(2)}) async-start(f32[128,1,128]{2,1,0:T(1,128)} %bitcast.8), calls=%async_computation | async-start | bytes 131072 | tf_op jit(solution)/shard_map/all_to_all | solution.py:685
  62.2 0.1 slice.7
  62.2 14.8 %all-to-all-done = f32[128,1,128]{2,1,0:T(1,128)S(1)} async-done(((f32[128,1,128]{2,1,0:T(1,128)}), f32[128,1,128]{2,1,0:T(1,128)S(1)}, u32[]{:S(2)}, u32[]{:S(2)}) %all-to-all-start) | async-done | bytes 65568 | tf_op jit(solution)/shard_map/all_to_all | solution.py:685
  77.0 2.5 %edges.1 = (f32[432,256]{1,0:T(8,128)}, f32[432,256]{1,0:T(8,128)}, f32[1,128]{1,0:T(1,128)S(1)}) custom-call(s32[2]{0:T(128)S(1)} %pad_add_fusion.where, s32[4]{0:T(128)S(1)} %copy-done.1, s32[4]{0:T(128)S(1)} %copy-done.2, f32[128,128]{1,0:T(8,128)S(1)} %bitcast.13, f32[20,112,256]{2,1,0:T(8,128)S(1)} %get-tuple-element.29.part, ...), custom_call_target="tpu_custom_call" | custom-call | tf_op jit(solution)/shard_map/edges/pallas_call | solution.py:688
  79.5 0.7 collective-permute-start.6
  80.2 1.9 %collective-permute-start.7 = (f32[432,256]{1,0:T(8,128)}, f32[432,256]{1,0:T(8,128)}, u32[]{:S(2)}, u32[]{:S(2)}) collective-permute-start(f32[432,256]{1,0:T(8,128)} %get-tuple-element.34), channel_id=1, source_target_pairs={{1,2},{2,1},{3,4},{4,3},{5,6},{6,5},{9,10},{10,9},{11,12},{12,11},... | collective-permute-start | bytes 1327112 | tf_op jit(solution)/shard_map/ppermute | solution.py:581
  82.1 0.1 reshape_squeeze.3
  82.2 1.5 %middle.1.grown = f32[3,24,40,256]{3,2,1,0:T(8,128)S(1)} custom-call(s32[2]{0:T(128)S(1)} %pad_add_fusion.where, f32[20,112,256]{2,1,0:T(8,128)S(1)} %get-tuple-element.29.part, f32[6,112,256]{2,1,0:T(8,128)S(1)} %collective-permute-done.4.got_a, f32[6,112,256]{2,1,0:T(8,128)} %collective-permute-done.5.got_b), custom_call_target="tpu_custom_call" | custom-call | flops 2000000000 | tf_op jit(solution)/shard_map/middle/pallas_call | solution.py:700
  83.7 0.6 bitcast_add_fusion
  84.4 5.7 %collective-permute-done.7.got_b = f32[432,256]{1,0:T(8,128)} collective-permute-done((f32[432,256]{1,0:T(8,128)}, f32[432,256]{1,0:T(8,128)}, u32[]{:S(2)}, u32[]{:S(2)}) %collective-permute-start.7) | collective-permute-done | bytes 442400 | tf_op jit(solution)/shard_map/ppermute | solution.py:581
  90.1 9.2 %relax.1 = f32[3,16,32,256]{3,2,1,0:T(8,128)} custom-call(s32[2]{0:T(128)S(1)} %pad_add_fusion.where, f32[3,24,40,256]{3,2,1,0:T(8,128)S(1)} %middle.1.grown, f32[432,256]{1,0:T(8,128)S(1)} %collective-permute-done.6.got_a, f32[432,256]{1,0:T(8,128)} %collective-permute-done.7.got_b), custom_call_target="tpu_custom_call" | custom-call | tf_op jit(solution)/shard_map/relax/pallas_call | solution.py:710
  (14 shorter events, 0.1 us)
Async XLA Ops:
  5.4 8.7 %collective-permute-start = (f32[264,256]{1,0:T(8,128)S(1)}, f32[264,256]{1,0:T(8,128)S(1)}, u32[]{:S(2)}, u32[]{:S(2)}) collective-permute-start(f32[264,256]{1,0:T(8,128)S(1)} %get-tuple-element.19), channel_id=1, source_target_pairs={{0,8},{8,0},{16,24},{24,16},{32,40},{40,32},{48,56},{56,48},{64,72... | collective-permute-start | bytes 811016 | tf_op jit(solution)/shard_map/ppermute | solution.py:574
  7.9 10.4 %collective-permute-start.1 = (f32[264,256]{1,0:T(8,128)S(1)}, f32[264,256]{1,0:T(8,128)S(1)}, u32[]{:S(2)}, u32[]{:S(2)}) collective-permute-start(f32[264,256]{1,0:T(8,128)S(1)} %get-tuple-element.20), channel_id=1, source_target_pairs={{8,16},{16,8},{24,32},{32,24},{40,48},{48,40},{56,64},{64,56},{72,... | collective-permute-start | bytes 811016 | tf_op jit(solution)/shard_map/ppermute | solution.py:575
  18.9 7.4 %collective-permute-start.2 = (f32[192,256]{1,0:T(8,128)S(1)}, f32[192,256]{1,0:T(8,128)S(1)}, u32[]{:S(2)}, u32[]{:S(2)}) collective-permute-start(f32[192,256]{1,0:T(8,128)S(1)} %get-tuple-element.24), channel_id=1, source_target_pairs={{0,1},{1,0},{2,3},{3,2},{4,5},{5,4},{6,7},{7,6},{8,9},{9,8},{10,11... | collective-permute-start | bytes 589832 | tf_op jit(solution)/shard_map/ppermute | solution.py:580
  20.8 7.0 %collective-permute-start.3 = (f32[192,256]{1,0:T(8,128)S(1)}, f32[192,256]{1,0:T(8,128)S(1)}, u32[]{:S(2)}, u32[]{:S(2)}) collective-permute-start(f32[192,256]{1,0:T(8,128)S(1)} %get-tuple-element.25), channel_id=1, source_target_pairs={{1,2},{2,1},{3,4},{4,3},{5,6},{6,5},{9,10},{10,9},{11,12},{12,11},... | collective-permute-start | bytes 589832 | tf_op jit(solution)/shard_map/ppermute | solution.py:581
  23.9 3.9 %copy-start = (f32[3,16,32,256]{3,2,1,0:T(8,128)S(1)}, f32[3,16,32,256]{3,2,1,0:T(8,128)}, u32[]{:S(2)}) copy-start(f32[3,16,32,256]{3,2,1,0:T(8,128)} %vel.1) | copy-start | bytes 4718596
  26.2 35.9 %copy-start.3 = (f32[6,2]{0,1:T(2,128)S(1)}, f32[6,2]{0,1:T(2,128)}, u32[]{:S(2)}) copy-start(f32[6,2]{0,1:T(2,128)} %param.17) | copy-start | bytes 148
  26.2 50.7 %copy-start.1 = (s32[4]{0:T(128)S(1)}, s32[4]{0:T(128)}, u32[]{:S(2)}) copy-start(s32[4]{0:T(128)} %contact_own.1) | copy-start | bytes 52
  26.3 50.7 %copy-start.2 = (s32[4]{0:T(128)S(1)}, s32[4]{0:T(128)}, u32[]{:S(2)}) copy-start(s32[4]{0:T(128)} %contact_other.1) | copy-start | bytes 52
  49.6 27.4 %collective-permute-start.4 = (f32[6,112,256]{2,1,0:T(8,128)}, f32[6,112,256]{2,1,0:T(8,128)S(1)}, u32[]{:S(2)}, u32[]{:S(2)}) collective-permute-start(f32[6,112,256]{2,1,0:T(8,128)} %get-tuple-element.30), channel_id=1, source_target_pairs={{0,8},{8,0},{16,24},{24,16},{32,40},{40,32},{48,56},{56,48},{64,72... | collective-permute-start | bytes 2064392 | tf_op jit(solution)/shard_map/ppermute | solution.py:574
  49.6 27.4 %collective-permute-start.5 = (f32[6,112,256]{2,1,0:T(8,128)}, f32[6,112,256]{2,1,0:T(8,128)}, u32[]{:S(2)}, u32[]{:S(2)}) collective-permute-start(f32[6,112,256]{2,1,0:T(8,128)} %get-tuple-element.31), channel_id=1, source_target_pairs={{8,16},{16,8},{24,32},{32,24},{40,48},{48,40},{56,64},{64,56},{72,... | collective-permute-start | bytes 2064392 | tf_op jit(solution)/shard_map/ppermute | solution.py:575
  54.3 22.7 %all-to-all-start = ((f32[128,1,128]{2,1,0:T(1,128)}), f32[128,1,128]{2,1,0:T(1,128)S(1)}, u32[]{:S(2)}, u32[]{:S(2)}) async-start(f32[128,1,128]{2,1,0:T(1,128)} %bitcast.8), calls=%async_computation | async-start | bytes 131072 | tf_op jit(solution)/shard_map/all_to_all | solution.py:685
  79.5 4.8 %collective-permute-start.6 = (f32[432,256]{1,0:T(8,128)}, f32[432,256]{1,0:T(8,128)S(1)}, u32[]{:S(2)}, u32[]{:S(2)}) collective-permute-start(f32[432,256]{1,0:T(8,128)} %get-tuple-element.33), channel_id=1, source_target_pairs={{0,1},{1,0},{2,3},{3,2},{4,5},{5,4},{6,7},{7,6},{8,9},{9,8},{10,11... | collective-permute-start | bytes 1327112 | tf_op jit(solution)/shard_map/ppermute | solution.py:580
  80.2 9.9 %collective-permute-start.7 = (f32[432,256]{1,0:T(8,128)}, f32[432,256]{1,0:T(8,128)}, u32[]{:S(2)}, u32[]{:S(2)}) collective-permute-start(f32[432,256]{1,0:T(8,128)} %get-tuple-element.34), channel_id=1, source_target_pairs={{1,2},{2,1},{3,4},{4,3},{5,6},{6,5},{9,10},{10,9},{11,12},{12,11},... | collective-permute-start | bytes 1327112 | tf_op jit(solution)/shard_map/ppermute | solution.py:581

commit v3 on v2

--- a/solution.py
+++ b/solution.py
@@ -19,7 +19,8 @@
 ROWS = 24
 TILE = 256
 UNROLL = 4
-WIN = 8
+SIZES = (7, 8, 9)
+WIN = 10
 CYR = 112
 
 
@@ -115,8 +116,13 @@
     step_x = (lax.shift_right_logical(own, gy_shift) - where[0] + 1) & (gx - 1)
     step_y = (own & ((1 << gy_shift) - 1)) - where[1] + 1
     lane = step_x * 3 + step_y
-    bin_of = jnp.where(lane == 4, bx[...], 17 + lane)
-    slot = counting_ranks(bin_of, lambda b: markers + (b - 17) * TILE, 17)
+    x_in = jnp.logical_and(bx[...] >= 2, bx[...] <= nx - 2)
+    y_in = jnp.logical_and(by[...] >= 2, by[...] <= ny - 2)
+    at_home = jnp.where(jnp.logical_and(x_in, y_in), bx[...], 17)
+    bin_of = jnp.where(lane == 4, at_home, 18 + lane)
+    slot = counting_ranks(
+        bin_of, lambda b: jnp.where(b == 17, markers, 2 * markers + (b - 18) * TILE), 17
+    )
     slot_out[...] = slot
 
     first = lax.broadcasted_iota(I32, (1, markers), 1) < markers // 2
@@ -142,11 +148,11 @@
     base = 6 * ny
     even = (where[0] & 1) == 0
     for ref, up in ((to_a, even), (to_b, jnp.logical_not(even))):
-        tile = blocks + jnp.where(up, 6, 0)
+        tile = 2 * blocks + jnp.where(up, 6, 0)
         for k in range(3):
             ref[base + k * ROWS : base + (k + 1) * ROWS, :] = gather_tile(both, slot, tile + k)
-    middle[0] = gather_tile(both, slot, blocks + 3)
-    middle[1] = gather_tile(both, slot, blocks + 5)
+    middle[0] = gather_tile(both, slot, 2 * blocks + 3)
+    middle[1] = gather_tile(both, slot, 2 * blocks + 5)
 
     lane_row = lax.broadcasted_iota(I32, (1, 128), 1)
     line = jnp.zeros((1, 128), F32)
@@ -168,16 +174,58 @@
             to_up[at : at + 2, :] = vel[c, x, ny - 2 : ny, :]
 
 
-def home_kernel(slot, both, home):
-    count = jnp.sum((slot[...] < slot.shape[1]).astype(F32)).astype(I32)
-    for t in range(home.shape[0]):
-        home[t] = jnp.zeros((ROWS, TILE), F32)
-
-    def tile(t, carry):
-        home[t] = gather_tile(both[...], slot[...], t)
+def home_kernel(slot, both, vel, inner, rim, part, fcat):
+    markers = slot.shape[1]
+    blocks = inner.shape[0]
+    below = (slot[...] < markers).astype(F32)
+    upto = (slot[...] < 2 * markers).astype(F32)
+    count_inner = jnp.sum(below).astype(I32)
+    count_rim = jnp.sum(upto - below).astype(I32)
+    for t in range(blocks):
+        inner[t] = jnp.zeros((ROWS, TILE), F32)
+        rim[t] = jnp.zeros((ROWS, TILE), F32)
+
+    def inner_tile(t, carry):
+        inner[t] = gather_tile(both[...], slot[...], t)
         return carry
 
-    lax.fori_loop(0, (count + TILE - 1) // TILE, tile, 0)
+    def rim_tile(t, carry):
+        rim[t] = gather_tile(both[...], slot[...], blocks + t)
+        return carry
+
+    lax.fori_loop(0, (count_inner + TILE - 1) // TILE, inner_tile, 0)
+    lax.fori_loop(0, (count_rim + TILE - 1) // TILE, rim_tile, 0)
+
+    nx = part.shape[0]
+    cells = vel.shape[2]
+    tall = cells + 4
+    blank = jnp.zeros(part.shape[1:], F32)
+    for x in range(nx):
+        part[x] = blank
+    fill_own(vel, part)
+
+    def halve(x, carry):
+        to_halves(part, fcat, x)
+        return carry
+
+    lax.fori_loop(0, nx, halve, 0)
+
+
+def fill_own(vel, field):
+    cells = vel.shape[2]
+
+    def layer(x, carry):
+        for c in range(3):
+            field[x + 2, c * (cells + 4) + 2 : c * (cells + 4) + 2 + cells, :] = vel[c, x]
+        return carry
+
+    lax.fori_loop(0, vel.shape[1], layer, 0)
+
+
+def to_halves(field, fcat, x):
+    high, low = split(field[x])
+    fcat[x, :, 0:256] = high
+    fcat[x, :, 256:512] = low
 
 
 def turn_kernel(
@@ -213,86 +261,14 @@
     return value
 
 
-def couple_kernel(
-    where, vel, got_xa, got_xb, got_ya, got_yb, home, linear,
-    part, send_a, send_b, message,
-    got_left, got_right, got_down, got_up, fcat, lists, arrived, tn, tt, sacc, scat, sums,
-):
-    nx = vel.shape[1] + 4
-    cells = vel.shape[2]
-    tall = cells + 4
-    sort_out(where[0], got_xa, got_xb, got_left, got_right)
-    sort_out(where[1], got_ya, got_yb, got_down, got_up)
-    zero_pad = jnp.zeros((CYR - 3 * tall, vel.shape[3]), F32)
-
-    def fill_own(x, carry):
-        for c in range(3):
-            part[x + 2, c * tall + 2 : c * tall + 2 + cells, :] = vel[c, x]
-        return carry
-
-    lax.fori_loop(0, nx - 4, fill_own, 0)
-    for x in range(2):
-        for c in range(3):
-            rows = pl.ds((c * 2 + x) * cells, cells)
-            part[x, c * tall + 2 : c * tall + 2 + cells, :] = got_right[rows, :]
-            part[nx - 2 + x, c * tall + 2 : c * tall + 2 + cells, :] = got_left[rows, :]
-
-    zero2 = jnp.zeros((2, vel.shape[3]), F32)
-    for x in range(nx):
-        for c in range(3):
-            rows = pl.ds(x * 6 + c * 2, 2)
-            part[x, c * tall : c * tall + 2, :] = got_up[rows, :]
-            part[x, c * tall + 2 + cells : (c + 1) * tall, :] = got_down[rows, :]
-        part[x, 3 * tall : CYR, :] = zero_pad
-
-    def fill_rest(x, carry):
-        high, low = split(part[x])
-        fcat[x, :, 0:256] = high
-        fcat[x, :, 256:512] = low
-        fcat[x, :, 512:768] = high
-        for c in range(3):
-            part[x, c * tall : c * tall + 2, :] = zero2
-            part[x, c * tall + 2 + cells : (c + 1) * tall, :] = zero2
-        return carry
-
-    lax.fori_loop(0, nx, fill_rest, 0)
-    for x in (0, 1, nx - 2, nx - 1):
-        part[x] = jnp.zeros((CYR, vel.shape[3]), F32)
-
-    base = 6 * cells + ROWS
-    after = nx * 6
-    arrived[:, 0:TILE] = got_left[base : base + ROWS, :]
-    arrived[:, TILE : 2 * TILE] = got_right[base : base + ROWS, :]
-    for k in range(3):
-        rows = pl.ds(after + k * ROWS, ROWS)
-        arrived[:, (2 + k) * TILE : (3 + k) * TILE] = got_down[rows, :]
-        arrived[:, (5 + k) * TILE : (6 + k) * TILE] = got_up[rows, :]
-    total_lanes = arrived.shape[1]
-    lane_at = lax.broadcasted_iota(I32, (1, total_lanes), 1)
-    arrived[23:24, :] = (1 + lax.shift_right_logical(lane_at, 8)).astype(F32)
-    valid_all = arrived[22:23, :] > 0.5
-    count = jnp.sum(arrived[22:23, :]).astype(I32)
-    bin_all = jnp.where(valid_all, arrived[12:13, :].astype(I32), 17)
-    slot = counting_ranks(bin_all, lambda b: 0 * b + total_lanes, 17)
-    both = halves(arrived[...])
-    blocks = home.shape[0]
-    for t in range(blocks):
-        lists[t] = home[t]
-        lists[blocks + t] = jnp.zeros((ROWS, TILE), F32)
-
-    def gather_one(t, carry):
-        lists[blocks + t] = gather_tile(both, slot, t)
-        return carry
-
-    lax.fori_loop(0, (count + TILE - 1) // TILE, gather_one, 0)
-    sums[...] = jnp.zeros(sums.shape, F32)
-
+def process_tiles(count, lists, fcat, part, sums, tn, tt, sacc, *, tall):
+    nx = part.shape[0]
     row = lax.broadcasted_iota(I32, (CYR, 1), 0)
     comp = (row >= tall).astype(I32) + (row >= 2 * tall).astype(I32)
     y_of = jnp.where(row < 3 * tall, row - comp * tall, -100)
     comp = jnp.where(row < 3 * tall, comp, 3)
     z_of = lax.broadcasted_iota(I32, (256, TILE), 0)
-    win_row = lax.broadcasted_iota(I32, (WIN, TILE), 0)
+    win_row = lax.broadcasted_iota(I32, (16, TILE), 0)
     group_of = lax.broadcasted_iota(I32, (128, TILE), 0)
 
     def tile_body(t, carry):
@@ -301,7 +277,8 @@
         bxf = rec[12:13]
         x_first = jnp.min(jnp.where(valid, bxf, 99.0)).astype(I32)
         x_last = jnp.max(jnp.where(valid, bxf, -9.0)).astype(I32)
-        windows = jnp.where(x_last < 0, 0, (x_last - x_first + 4 + WIN - 1) // WIN)
+        layers = x_last - x_first + 4
+        windows = jnp.where(x_last < 0, 0, (layers + WIN - 1) // WIN)
 
         @pl.when(windows > 0)
         def _():
@@ -311,32 +288,49 @@
             table_z = chain((z_of - bzi) & 255, [rec[8 + k : 9 + k] for k in range(4)])
             high, low = split(table_z)
             tn[0:256, :] = high
-            tn[256:512, :] = high
-            tn[512:768, :] = low
+            tn[256:512, :] = low
             tt[:, 0:256] = high
-            tt[:, 256:512] = high
-            tt[:, 512:768] = low
+            tt[:, 256:512] = low
             table_y = chain(y_of - byi, [rec[4 + k : 5 + k] for k in range(4)])
             sacc[...] = jnp.zeros(sacc.shape, F32)
 
-            def window(w):
-                begin = x_first + w * WIN
-                x0 = jnp.minimum(begin, nx - WIN)
+            def window(w, size):
+                begin = x_first + w * size
+                x0 = jnp.minimum(begin, nx - size)
                 x_at = win_row + x0
                 table_x = chain(x_at - bxi, [rec[k : k + 1] for k in range(4)])
                 return x0, jnp.where(x_at >= begin, table_x, 0.0)
 
-            def sample(w, c):
-                x0, table_x = window(w)
-                block = fcat[pl.ds(x0, WIN)].reshape(WIN * CYR, 768)
-                got = jnp.dot(block, tn[...], preferred_element_type=F32)
+            def sample(w, size):
+                x0, table_x = window(w, size)
+                block_h = fcat[pl.ds(x0, size), :, 0:256].reshape(size * CYR, 256)
+                block_l = fcat[pl.ds(x0, size), :, 256:512].reshape(size * CYR, 256)
+                got = (
+                    jnp.dot(block_h, tn[0:256], preferred_element_type=F32)
+                    + jnp.dot(block_l, tn[0:256], preferred_element_type=F32)
+                    + jnp.dot(block_h, tn[256:512], preferred_element_type=F32)
+                )
                 total = sacc[...]
-                for i in range(WIN):
+                for i in range(size):
                     total = total + table_x[i : i + 1] * got[i * CYR : (i + 1) * CYR]
                 sacc[...] = total
-                return c
-
-            lax.fori_loop(0, windows, sample, 0)
+
+            def by_size(step):
+                for size in SIZES:
+                    fits = layers <= size
+                    if size > SIZES[0]:
+                        fits = jnp.logical_and(fits, layers > size - 1)
+                    pl.when(fits)(functools.partial(step, 0, size))
+
+                @pl.when(layers > SIZES[-1])
+                def _():
+                    def loop(w, c):
+                        step(w, WIN)
+                        return c
+
+                    lax.fori_loop(0, windows, loop, 0)
+
+            by_size(sample)
             weighted = sacc[...] * table_y
             force = [
                 rec[15 + c : 16 + c]
@@ -346,23 +340,20 @@
             by_row = jnp.where(comp == 0, force[0], jnp.where(comp == 1, force[1], force[2]))
             plane = table_y * by_row
 
-            def deposit(w, c):
-                x0, table_x = window(w)
-                for i in range(WIN):
-                    hi, lo = split(table_x[i : i + 1] * plane)
-                    scat[i, :, 0:256] = hi
-                    scat[i, :, 256:512] = lo
-                    scat[i, :, 512:768] = hi
-                made = lax.dot_general(
-                    scat[...].reshape(WIN * CYR, 768),
-                    tt[...],
-                    (((1,), (1,)), ((), ())),
-                    preferred_element_type=F32,
+            def deposit(w, size):
+                x0, table_x = window(w, size)
+                pieces = [split(table_x[i : i + 1] * plane) for i in range(size)]
+                high_s = jnp.concatenate([p[0] for p in pieces], axis=0)
+                low_s = jnp.concatenate([p[1] for p in pieces], axis=0)
+                nt = (((1,), (1,)), ((), ()))
+                made = (
+                    lax.dot_general(high_s, tt[:, 0:256], nt, preferred_element_type=F32)
+                    + lax.dot_general(low_s, tt[:, 0:256], nt, preferred_element_type=F32)
+                    + lax.dot_general(high_s, tt[:, 256:512], nt, preferred_element_type=F32)
                 )
-                part[pl.ds(x0, WIN)] += made.reshape(WIN, CYR, 256)
-                return c
-
-            lax.fori_loop(0, windows, deposit, 0)
+                part[pl.ds(x0, size)] += made.reshape(size, CYR, 256)
+
+            by_size(deposit)
             off = [rec[18 + c : 19 + c] for c in range(3)]
             turn = [
                 off[1] * force[2] - off[2] * force[1],
@@ -379,7 +370,84 @@
 
         return carry
 
-    lax.fori_loop(0, 2 * blocks, tile_body, 0)
+    lax.fori_loop(0, count, tile_body, 0)
+
+
+def inner_kernel(lists, fcat, part_in, part, sums, tn, tt, sacc, *, tall):
+    del part_in
+    sums[...] = jnp.zeros(sums.shape, F32)
+    process_tiles(lists.shape[0], lists, fcat, part, sums, tn, tt, sacc, tall=tall)
+
+
+def couple_kernel(
+    where, vel, got_xa, got_xb, got_ya, got_yb, rim, linear, sums_in, part_in,
+    part, send_a, send_b, message,
+    got_left, got_right, got_down, got_up, field, fcat, lists, arrived, tn, tt, sacc, sums,
+):
+    del part_in
+    nx = vel.shape[1] + 4
+    cells = vel.shape[2]
+    tall = cells + 4
+    sort_out(where[0], got_xa, got_xb, got_left, got_right)
+    sort_out(where[1], got_ya, got_yb, got_down, got_up)
+    zero_pad = jnp.zeros((CYR - 3 * tall, vel.shape[3]), F32)
+    fill_own(vel, field)
+    for x in range(2):
+        for c in range(3):
+            rows = pl.ds((c * 2 + x) * cells, cells)
+            field[x, c * tall + 2 : c * tall + 2 + cells, :] = got_right[rows, :]
+            field[nx - 2 + x, c * tall + 2 : c * tall + 2 + cells, :] = got_left[rows, :]
+    for x in range(nx):
+        for c in range(3):
+            rows = pl.ds(x * 6 + c * 2, 2)
+            field[x, c * tall : c * tall + 2, :] = got_up[rows, :]
+            field[x, c * tall + 2 + cells : (c + 1) * tall, :] = got_down[rows, :]
+        field[x, 3 * tall : CYR, :] = zero_pad
+
+    def halve(x, carry):
+        to_halves(field, fcat, x)
+        return carry
+
+    lax.fori_loop(0, nx, halve, 0)
+
+    base = 6 * cells + ROWS
+    after = nx * 6
+    blocks = rim.shape[0]
+    arrived[:, 0:TILE] = got_left[base : base + ROWS, :]
+    arrived[:, TILE : 2 * TILE] = got_right[base : base + ROWS, :]
+    for k in range(3):
+        rows = pl.ds(after + k * ROWS, ROWS)
+        arrived[:, (2 + k) * TILE : (3 + k) * TILE] = got_down[rows, :]
+        arrived[:, (5 + k) * TILE : (6 + k) * TILE] = got_up[rows, :]
+    for t in range(blocks):
+        arrived[:, (8 + t) * TILE : (9 + t) * TILE] = rim[t]
+    total_lanes = arrived.shape[1]
+    lane_at = lax.broadcasted_iota(I32, (1, total_lanes), 1)
+    list_at = 1 + lax.shift_right_logical(lane_at, TILE.bit_length() - 1)
+    arrived[23:24, :] = jnp.where(list_at > 8, 0, list_at).astype(F32)
+    valid_all = arrived[22:23, :] > 0.5
+    count = jnp.sum(arrived[22:23, :]).astype(I32)
+    few = 10 * TILE
+    beyond = jnp.sum(arrived[22:23, few:total_lanes])
+    bin_all = jnp.where(valid_all, arrived[12:13, :].astype(I32), 17)
+    slot = counting_ranks(bin_all, lambda b: 0 * b + total_lanes, 17)
+    both = halves(arrived[...])
+    for t in range(lists.shape[0]):
+        lists[t] = jnp.zeros((ROWS, TILE), F32)
+    tiles = (count + TILE - 1) // TILE
+
+    def gather_few(t, carry):
+        lists[t] = gather_tile(both[:, 0:few], slot[:, 0:few], t)
+        return carry
+
+    def gather_all(t, carry):
+        lists[t] = gather_tile(both, slot, t)
+        return carry
+
+    lax.fori_loop(0, jnp.where(beyond > 0.5, 0, tiles), gather_few, 0)
+    lax.fori_loop(0, jnp.where(beyond > 0.5, tiles, 0), gather_all, 0)
+    sums[...] = sums_in[...]
+    process_tiles(tiles, lists, fcat, part, sums, tn, tt, sacc, tall=tall)
     lane_of = lax.broadcasted_iota(I32, (128, 128), 1)
     low_part = pltpu.roll(sums[...], 120, axis=1)
     joined = jnp.where(lane_of < 6, sums[...] + low_part, 0.0)
@@ -393,7 +461,9 @@
         send_b[x] = part[jnp.where(even, 0, nx - 6) + x]
 
 
-def motion(where, contact_own, contact_other, got, out, moved, *, gx, gy, per_sphere):
+def motion_kernel(
+    where, contact_own, contact_other, angular, got, out, moved, *, gx, gy, per_sphere
+):
     here = where[0] * gy + where[1]
     data = got[...]
     total = jnp.zeros(data.shape, F32)
@@ -421,19 +491,19 @@
         lower = jnp.where(which > local, pltpu.roll(line, 122, axis=1), 0.0)
         of_own = jnp.logical_and(lane >= local * 6, lane < local * 6 + 3)
         spring = spring + jnp.where(of_own, same + higher + lower - mine, 0.0)
-    out[...] = mine + DASHPOT * spring
-
-
-def edges_kernel(
-    where, contact_own, contact_other, got, part, got_a, got_b, to_a, to_b, line,
-    moved, low, high, *, tall, gx, gy, per_sphere
-):
-    motion(where, contact_own, contact_other, got, line, moved, gx=gx, gy=gy, per_sphere=per_sphere)
+    result = mine + DASHPOT * spring
+    out[0:1, :] = result[:, 0:6] + angular[0:1, :]
+    out[1:2, :] = pltpu.roll(result, 122, axis=1)[:, 0:6] + angular[1:2, :]
+
+
+def edges_kernel(where, part, got_a, got_b, to_a, to_b, *, tall):
     nx = part.shape[0]
     even = (where[0] & 1) == 0
+    even_y = (where[1] & 1) == 0
     for x in range(nx + 4):
         for c in range(3):
-            for ref, at in ((low, c * tall), (high, (c + 1) * tall - 6)):
+            values = []
+            for at in (c * tall, (c + 1) * tall - 6):
                 rows = pl.ds(at, 6)
                 pieces = []
                 if 2 <= x < nx + 2:
@@ -446,8 +516,10 @@
                 total = pieces[0]
                 for piece in pieces[1:]:
                     total = total + piece
-                ref[x * 18 + c * 6 : x * 18 + c * 6 + 6, :] = total
-    sort_out(where[1], high, low, to_a, to_b)
+                values.append(total)
+            to = pl.ds(x * 18 + c * 6, 6)
+            to_a[to, :] = jnp.where(even_y, values[1], values[0])
+            to_b[to, :] = jnp.where(even_y, values[0], values[1])
 
 
 def middle_kernel(where, part, got_a, got_b, rhs, *, tall):
@@ -633,15 +705,34 @@
         ),
     )
     got_xa, got_xb = swap_x(to_a, to_b)
-    home = pl.pallas_call(
+    field = array(nx + 4, CYR, nz)
+    halved = array(nx + 4, CYR, 2 * nz, dtype=BF16)
+    lists = array(blocks, ROWS, TILE)
+    inner, rim, part, fcat = pl.pallas_call(
         home_kernel,
-        out_shape=array(blocks, ROWS, TILE),
-        in_specs=[VMEM] * 2,
-        out_specs=VMEM,
+        out_shape=(lists, lists, field, halved),
+        in_specs=[VMEM] * 3,
+        out_specs=(VMEM,) * 4,
         compiler_params=params(8),
         cost_estimate=pl.CostEstimate(flops=2_000_000_000, bytes_accessed=0, transcendentals=0),
         name="home",
-    )(slot, both)
+    )(slot, both, velocity)
+    tile_scratch = [
+        pltpu.VMEM((2 * nz, TILE), BF16),
+        pltpu.VMEM((nz, 2 * TILE), BF16),
+        pltpu.VMEM((CYR, TILE), F32),
+    ]
+    part, sums = pl.pallas_call(
+        functools.partial(inner_kernel, tall=tall),
+        out_shape=(field, array(128, 128)),
+        in_specs=[VMEM] * 3,
+        out_specs=(VMEM,) * 2,
+        input_output_aliases={2: 0},
+        scratch_shapes=tile_scratch,
+        compiler_params=params(8),
+        cost_estimate=pl.CostEstimate(flops=4_000_000_000, bytes_accessed=0, transcendentals=0),
+        name="inner",
+    )(inner, fcat, part)
     x_buffer = pltpu.VMEM((x_rows, nz), F32)
     y_buffer = pltpu.VMEM((y_rows, nz), F32)
     got_ya, got_yb = swap_y(
@@ -660,42 +751,49 @@
     slab = array(6, CYR, nz)
     part, send_a, send_b, message = pl.pallas_call(
         couple_kernel,
-        out_shape=(array(nx + 4, CYR, nz), slab, slab, array(devices, 128)),
-        in_specs=[SMEM] + [VMEM] * 7,
+        out_shape=(field, slab, slab, array(devices, 128)),
+        in_specs=[SMEM] + [VMEM] * 9,
         out_specs=(VMEM,) * 4,
+        input_output_aliases={9: 0},
         scratch_shapes=[
             x_buffer,
             x_buffer,
             y_buffer,
             y_buffer,
-            pltpu.VMEM((nx + 4, CYR, 768), BF16),
+            pltpu.VMEM(field.shape, F32),
+            pltpu.VMEM(halved.shape, BF16),
             pltpu.VMEM((2 * blocks, ROWS, TILE), F32),
-            pltpu.VMEM((ROWS, markers), F32),
-            pltpu.VMEM((768, 256), BF16),
-            pltpu.VMEM((256, 768), BF16),
-            pltpu.VMEM((CYR, TILE), F32),
-            pltpu.VMEM((WIN, CYR, 768), BF16),
+            pltpu.VMEM((ROWS, 2 * markers), F32),
+            *tile_scratch,
             pltpu.VMEM((128, 128), F32),
         ],
-        compiler_params=params(24),
+        compiler_params=params(16),
         name="couple",
-    )(where, velocity, got_xa, got_xb, got_ya, got_yb, home, linear)
+    )(where, velocity, got_xa, got_xb, got_ya, got_yb, rim, linear, sums, part)
 
     got_a, got_b = swap_x(send_a, send_b)
     everyone = lax.all_to_all(message, ("gx", "gy"), 0, 0, tiled=True)
     strip = array((nx + 8) * 18, nz)
+    everyone, part = lax.optimization_barrier((everyone, part))
     strip_buffer = pltpu.VMEM(strip.shape, F32)
-    to_ya, to_yb, line = pl.pallas_call(
-        functools.partial(edges_kernel, tall=tall, gx=gx, gy=gy, per_sphere=per_sphere),
-        out_shape=(strip, strip, array(1, 128)),
-        in_specs=[SMEM] * 3 + [VMEM] * 4,
-        out_specs=(VMEM,) * 3,
-        scratch_shapes=[pltpu.VMEM((devices, 128), F32), strip_buffer, strip_buffer],
+    to_ya, to_yb = pl.pallas_call(
+        functools.partial(edges_kernel, tall=tall),
+        out_shape=(strip, strip),
+        in_specs=[SMEM] + [VMEM] * 3,
+        out_specs=(VMEM,) * 2,
         compiler_params=params(4),
         name="edges",
-    )(where, contact_sphere, contact_partner, everyone, part, got_a, got_b)
-    found = line[0, 0 : 6 * spheres].reshape(spheres, 6).T
-    new_motion = found + jnp.concatenate([jnp.zeros((3, spheres), F32), sphere_motion[3:6]], axis=0)
+    )(where, part, got_a, got_b)
+    angular = jnp.concatenate([jnp.zeros((3, spheres), F32), sphere_motion[3:6]], axis=0).T
+    new_motion = pl.pallas_call(
+        functools.partial(motion_kernel, gx=gx, gy=gy, per_sphere=per_sphere),
+        out_shape=array(spheres, 6),
+        in_specs=[SMEM] * 3 + [VMEM] * 2,
+        out_specs=VMEM,
+        scratch_shapes=[pltpu.VMEM((devices, 128), F32)],
+        compiler_params=params(4),
+        name="motion",
+    )(where, contact_sphere, contact_partner, angular, everyone).T
     got_ea, got_eb = swap_y(to_ya, to_yb)
     grown = pl.pallas_call(
         functools.partial(middle_kernel, tall=tall),

time: 98.9 us -> 89.7 us (0.907)
  waiting for transfers between devices: 28 us -> 6.61 us
  blocking collectives: 0 us -> 18.4 us
  starting transfers between devices: 27.1 us -> 19.3 us
  local copies, waits for them, and re-layouts: 0.2 us -> 1.58 us
    all_to_all x0 -> x1, blocking collectives: none -> 18.4 us  [on_device(): everyone = lax.all_to_all(message, ('gx', 'gy'), 0, 0, tiled=True)]
    all_to_all x1 -> x0, waiting for transfers between devices: 14.8 us -> none  [on_device(): everyone = lax.all_to_all(message, ('gx', 'gy'), 0, 0, tiled=True)]
    all_to_all x1 -> x0, starting transfers between devices: 7.8 us -> none  [on_device(): everyone = lax.all_to_all(message, ('gx', 'gy'), 0, 0, tiled=True)]
    ppermute x2, waiting for transfers between devices: 4.22 us -> 1.55 us  [swap_x(): lax.ppermute(second, 'gx', pairs(gx, 1, True))]
    ppermute x2, waiting for transfers between devices: 7.25 us -> 5.04 us  [swap_y(): lax.ppermute(second, 'gy', pairs(gy, 1, False))]
    ppermute x2, waiting for transfers between devices: 1.75 us -> 0.01 us  [swap_x(): lax.ppermute(first, 'gx', pairs(gx, 0, True))]
    unnamed x8 -> x10, local copies, waits for them, and re-layouts: 0.03 us -> 1.43 us
    pallas_call x3 -> x5, Pallas kernels: 26.6 us -> 27.4 us  [the longest x1 16.5 us: on_device(): pl.pallas_call(couple_kernel, out_shape=(field, slab, slab, array(devices...]
  transfers between devices with their start and end apart: 9 -> 8, of which waited for: 5 -> 2; matrix products, arithmetic and copies ran while one was open for 1% -> 0% of each run, Pallas kernels for 4% -> 12%
where the time goes in v3:
time: 89.7 us; the launch traced here: 89.3 us
  Pallas kernels  42.4 us (47%)
  starting transfers between devices  19.3 us (22%)
  blocking collectives  18.4 us (21%)
  waiting for transfers between devices  6.61 us (7%)
  local copies, waits for them, and re-layouts  1.58 us (2%)
  between operations  0.95 us (1%)
    all_to_all x1, blocking collectives, on_device(): everyone = lax.all_to_all(message, ('gx', 'gy'), 0, 0, tiled=True)  18.4 us
    pallas_call x1, Pallas kernels, on_device(): pl.pallas_call(couple_kernel, out_shape=(field, slab, slab, array(devices...  16.5 us
    ppermute x2, starting transfers between devices, swap_x(): lax.ppermute(second, 'gx', pairs(gx, 1, True))  9.01 us
    pallas_call x1, Pallas kernels, on_device(): pl.pallas_call(functools.partial(relax_kernel, rows=ny * gy), out_shape=a...  8.76 us
    pallas_call x1, Pallas kernels, on_device(): pl.pallas_call(functools.partial(inner_kernel, tall=tall), out_shape=(fie...  5.6 us
    ppermute x2, waiting for transfers between devices, swap_y(): lax.ppermute(second, 'gy', pairs(gy, 1, False))  5.04 us
    ppermute x2, starting transfers between devices, swap_y(): lax.ppermute(second, 'gy', pairs(gy, 1, False))  5.01 us
    pallas_call x1, Pallas kernels, on_device(): pl.pallas_call(functools.partial(route_kernel, gx=gx, gy_shift=gy.bit_len...  4.64 us
  transfers between devices with their start and end apart: 8, of which 2 were waited for; matrix products, arithmetic and copies ran while one was open for 0% of the time, Pallas kernels for 12%

profile of v3, /device:TPU:1, one launch (start us, length us, event | category | flops | bytes accessed | tf_op | source)
XLA Modules:
  0.0 89.3 jit_solution(14352001708497816502)
XLA Ops:
  0.6 0.1 pad_add_fusion.where
  0.7 4.6 %route.1 = (f32[264,256]{1,0:T(8,128)S(1)}, f32[264,256]{1,0:T(8,128)S(1)}, f32[2,24,256]{2,1,0:T(8,128)S(1)}, f32[192,256]{1,0:T(8,128)S(1)}, f32[192,256]{1,0:...) custom-call(s32[2]{0:T(128)S(1)} %pad_add_fusion.where, f32[2,6]{1,0:T(2,128)} %bitcast.20, ...), custom_call_target="tpu_custom_call" | custom-call | tf_op jit(solution)/shard_map/route/pallas_call | solution.py:662
  5.4 2.5 %collective-permute-start = (f32[264,256]{1,0:T(8,128)S(1)}, f32[264,256]{1,0:T(8,128)S(1)}, u32[]{:S(2)}, u32[]{:S(2)}) collective-permute-start(f32[264,256]{1,0:T(8,128)S(1)} %get-tuple-element.26), channel_id=1, source_target_pairs={{0,8},{8,0},{16,24},{24,16},{32,40},{40,32},{48,56},{56,48},{64,72... | collective-permute-start | bytes 811016 | tf_op jit(solution)/shard_map/ppermute | solution.py:646
  7.9 4.4 %collective-permute-start.1 = (f32[264,256]{1,0:T(8,128)S(1)}, f32[264,256]{1,0:T(8,128)S(1)}, u32[]{:S(2)}, u32[]{:S(2)}) collective-permute-start(f32[264,256]{1,0:T(8,128)S(1)} %get-tuple-element.27), channel_id=1, source_target_pairs={{8,16},{16,8},{24,32},{32,24},{40,48},{48,40},{56,64},{64,56},{72,... | collective-permute-start | bytes 811016 | tf_op jit(solution)/shard_map/ppermute | solution.py:647
  12.3 1.4 %copy-done = f32[3,16,32,256]{3,2,1,0:T(8,128)S(1)} copy-done((f32[3,16,32,256]{3,2,1,0:T(8,128)S(1)}, f32[3,16,32,256]{3,2,1,0:T(8,128)}, u32[]{:S(2)}) %copy-start) | copy-done | bytes 1572888
  13.7 3.0 %home.1 = (f32[8,24,256]{2,1,0:T(8,128)S(1)}, f32[8,24,256]{2,1,0:T(8,128)S(1)}, f32[20,112,256]{2,1,0:T(8,128)S(1)}, bf16[20,112,512]{2,1,0:T(8,128)(2,1)S(1)}) custom-call(s32[1,2048]{1,0:T(1,128)S(1)} %get-tuple-element.33.slot, bf16[48,2048]{1,0:T(8,128)(2,1)S(1)} %get-tuple-element.34.both, f32[3,16,32,256]{3,2,1,0:T(8,128)S(1)} %copy-done), custom_call_target="tpu_custom_call" | custom-call | flops 2000000000 | tf_op jit(solution)/shard_map/home/pallas_call | solution.py:711
  16.7 1.5 %collective-permute-done.1.got_b.got_xb = f32[264,256]{1,0:T(8,128)S(1)} collective-permute-done((f32[264,256]{1,0:T(8,128)S(1)}, f32[264,256]{1,0:T(8,128)S(1)}, u32[]{:S(2)}, u32[]{:S(2)}) %collective-permute-start.1) | collective-permute-done | bytes 270368 | tf_op jit(solution)/shard_map/ppermute | solution.py:647
  18.3 0.6 turn.1
  18.9 1.9 %collective-permute-start.2 = (f32[192,256]{1,0:T(8,128)S(1)}, f32[192,256]{1,0:T(8,128)S(1)}, u32[]{:S(2)}, u32[]{:S(2)}) collective-permute-start(f32[192,256]{1,0:T(8,128)S(1)} %get-tuple-element.31), channel_id=1, source_target_pairs={{0,1},{1,0},{2,3},{3,2},{4,5},{5,4},{6,7},{7,6},{8,9},{9,8},{10,11... | collective-permute-start | bytes 589832 | tf_op jit(solution)/shard_map/ppermute | solution.py:652
  20.8 3.1 %collective-permute-start.3 = (f32[192,256]{1,0:T(8,128)S(1)}, f32[192,256]{1,0:T(8,128)S(1)}, u32[]{:S(2)}, u32[]{:S(2)}) collective-permute-start(f32[192,256]{1,0:T(8,128)S(1)} %get-tuple-element.32), channel_id=1, source_target_pairs={{1,2},{2,1},{3,4},{4,3},{5,6},{6,5},{9,10},{10,9},{11,12},{12,11},... | collective-permute-start | bytes 589832 | tf_op jit(solution)/shard_map/ppermute | solution.py:653
  23.9 5.6 %inner.1 = (f32[20,112,256]{2,1,0:T(8,128)S(1)}, f32[128,128]{1,0:T(8,128)S(1)}) custom-call(f32[8,24,256]{2,1,0:T(8,128)S(1)} %get-tuple-element.37.lists, bf16[20,112,512]{2,1,0:T(8,128)(2,1)S(1)} %get-tuple-element.38.fcat, f32[20,112,256]{2,1,0:T(8,128)S(1)} %get-tuple-element.39.part_in), custom_call_target="tpu_custom_call", output_to_operand_aliasing={{0}: (2, {})} | custom-call | flops 4000000000 | tf_op jit(solution)/shard_map/inner/pallas_call | solution.py:725
  29.6 16.5 %couple.1 = (f32[20,112,256]{2,1,0:T(8,128)S(1)}, f32[6,112,256]{2,1,0:T(8,128)S(1)}, f32[6,112,256]{2,1,0:T(8,128)S(1)}, f32[128,128]{1,0:T(8,128)S(1)}) custom-call(s32[2]{0:T(128)S(1)} %pad_add_fusion.where, f32[3,16,32,256]{3,2,1,0:T(8,128)S(1)} %copy-done.1, f32[264,256]{1,0:T(8,128)S(1)} %collective-permute-done.got_a.got_xa, ...), custom_call_target="tpu_custom_call", output_to_operand_aliasing={{0}: (9, {})} | custom-call | tf_op jit(solution)/shard_map/couple/pallas_call | solution.py:752
  46.1 0.1 collective-permute-start.4
  46.2 4.6 %collective-permute-start.5 = (f32[6,112,256]{2,1,0:T(8,128)S(1)}, f32[6,112,256]{2,1,0:T(8,128)S(1)}, u32[]{:S(2)}, u32[]{:S(2)}) collective-permute-start(f32[6,112,256]{2,1,0:T(8,128)S(1)} %get-tuple-element.46), channel_id=1, source_target_pairs={{8,16},{16,8},{24,32},{32,24},{40,48},{48,40},{56,64},{64,56},{72,... | collective-permute-start | bytes 2064392 | tf_op jit(solution)/shard_map/ppermute | solution.py:647
  50.8 18.4 %all_to_all.12 = f32[128,1,128]{2,1,0:T(1,128)S(1)} all-to-all(f32[128,1,128]{2,1,0:T(1,128)S(1)} %bitcast.15), channel_id=1, replica_groups=mesh['gx'=16,'gy'=8] {'gx','gy'}, dimensions={0} | all-to-all | bytes 131072 | tf_op jit(solution)/shard_map/all_to_all | solution.py:775
  69.2 0.8 edges.1
  70.0 0.8 collective-permute-start.6
  70.8 1.9 %collective-permute-start.7 = (f32[432,256]{1,0:T(8,128)S(1)}, f32[432,256]{1,0:T(8,128)S(1)}, u32[]{:S(2)}, u32[]{:S(2)}) collective-permute-start(f32[432,256]{1,0:T(8,128)S(1)} %get-tuple-element.48), channel_id=1, source_target_pairs={{1,2},{2,1},{3,4},{4,3},{5,6},{6,5},{9,10},{10,9},{11,12},{12,11},... | collective-permute-start | bytes 1327112 | tf_op jit(solution)/shard_map/ppermute | solution.py:653
  72.7 0.1 slice.3
  72.8 0.1 pad_bitcast_fusion.angular
  72.8 1.5 %motion.1 = f32[2,6]{1,0:T(2,128)} custom-call(s32[2]{0:T(128)S(1)} %pad_add_fusion.where, s32[4]{0:T(128)S(1)} %copy-done.2, s32[4]{0:T(128)S(1)} %copy-done.3, f32[2,6]{1,0:T(2,128)S(1)} %pad_bitcast_fusion.angular, f32[128,128]{1,0:T(8,128)S(1)} %bitcast.14), custom_call_target="tpu_custom_call" | custom-call | tf_op jit(solution)/shard_map/motion/pallas_call | solution.py:788
  74.3 1.0 %middle.1.grown = f32[3,24,40,256]{3,2,1,0:T(8,128)S(1)} custom-call(s32[2]{0:T(128)S(1)} %pad_add_fusion.where, f32[20,112,256]{2,1,0:T(8,128)S(1)} %get-tuple-element.44.part, f32[6,112,256]{2,1,0:T(8,128)S(1)} %collective-permute-done.4.got_a, f32[6,112,256]{2,1,0:T(8,128)S(1)} %collective-permute-done.5.got_b), custom_call_target="tpu_custom_call" | custom-call | flops 2000000000 | tf_op jit(solution)/shard_map/middle/pallas_call | solution.py:798
  75.3 5.0 %collective-permute-done.7.got_b = f32[432,256]{1,0:T(8,128)S(1)} collective-permute-done((f32[432,256]{1,0:T(8,128)S(1)}, f32[432,256]{1,0:T(8,128)S(1)}, u32[]{:S(2)}, u32[]{:S(2)}) %collective-permute-start.7) | collective-permute-done | bytes 442400 | tf_op jit(solution)/shard_map/ppermute | solution.py:653
  80.4 8.8 %relax.1 = f32[3,16,32,256]{3,2,1,0:T(8,128)} custom-call(s32[2]{0:T(128)S(1)} %pad_add_fusion.where, f32[3,24,40,256]{3,2,1,0:T(8,128)S(1)} %middle.1.grown, f32[432,256]{1,0:T(8,128)S(1)} %collective-permute-done.6.got_a, f32[432,256]{1,0:T(8,128)S(1)} %collective-permute-done.7.got_b), custom_call_target="tpu_custom_call" | custom-call | tf_op jit(solution)/shard_map/relax/pallas_call | solution.py:808
  (15 shorter events, 0.0 us)
Async XLA Ops:
  5.4 11.4 %collective-permute-start = (f32[264,256]{1,0:T(8,128)S(1)}, f32[264,256]{1,0:T(8,128)S(1)}, u32[]{:S(2)}, u32[]{:S(2)}) collective-permute-start(f32[264,256]{1,0:T(8,128)S(1)} %get-tuple-element.26), channel_id=1, source_target_pairs={{0,8},{8,0},{16,24},{24,16},{32,40},{40,32},{48,56},{56,48},{64,72... | collective-permute-start | bytes 811016 | tf_op jit(solution)/shard_map/ppermute | solution.py:646
  7.9 10.4 %collective-permute-start.1 = (f32[264,256]{1,0:T(8,128)S(1)}, f32[264,256]{1,0:T(8,128)S(1)}, u32[]{:S(2)}, u32[]{:S(2)}) collective-permute-start(f32[264,256]{1,0:T(8,128)S(1)} %get-tuple-element.27), channel_id=1, source_target_pairs={{8,16},{16,8},{24,32},{32,24},{40,48},{48,40},{56,64},{64,56},{72,... | collective-permute-start | bytes 811016 | tf_op jit(solution)/shard_map/ppermute | solution.py:647
  12.3 1.4 %copy-start = (f32[3,16,32,256]{3,2,1,0:T(8,128)S(1)}, f32[3,16,32,256]{3,2,1,0:T(8,128)}, u32[]{:S(2)}) copy-start(f32[3,16,32,256]{3,2,1,0:T(8,128)} %vel.3) | copy-start | bytes 4718596
  18.9 10.6 %collective-permute-start.2 = (f32[192,256]{1,0:T(8,128)S(1)}, f32[192,256]{1,0:T(8,128)S(1)}, u32[]{:S(2)}, u32[]{:S(2)}) collective-permute-start(f32[192,256]{1,0:T(8,128)S(1)} %get-tuple-element.31), channel_id=1, source_target_pairs={{0,1},{1,0},{2,3},{3,2},{4,5},{5,4},{6,7},{7,6},{8,9},{9,8},{10,11... | collective-permute-start | bytes 589832 | tf_op jit(solution)/shard_map/ppermute | solution.py:652
  20.8 8.7 %collective-permute-start.3 = (f32[192,256]{1,0:T(8,128)S(1)}, f32[192,256]{1,0:T(8,128)S(1)}, u32[]{:S(2)}, u32[]{:S(2)}) collective-permute-start(f32[192,256]{1,0:T(8,128)S(1)} %get-tuple-element.32), channel_id=1, source_target_pairs={{1,2},{2,1},{3,4},{4,3},{5,6},{6,5},{9,10},{10,9},{11,12},{12,11},... | collective-permute-start | bytes 589832 | tf_op jit(solution)/shard_map/ppermute | solution.py:653
  23.9 5.6 %copy-start.1 = (f32[3,16,32,256]{3,2,1,0:T(8,128)S(1)}, f32[3,16,32,256]{3,2,1,0:T(8,128)}, u32[]{:S(2)}) copy-start(f32[3,16,32,256]{3,2,1,0:T(8,128)} %vel.3) | copy-start | bytes 4718596
  46.1 26.6 %copy-start.4 = (f32[6,2]{0,1:T(2,128)S(1)}, f32[6,2]{0,1:T(2,128)}, u32[]{:S(2)}) copy-start(f32[6,2]{0,1:T(2,128)} %param.17) | copy-start | bytes 148
  46.1 26.8 %copy-start.2 = (s32[4]{0:T(128)S(1)}, s32[4]{0:T(128)}, u32[]{:S(2)}) copy-start(s32[4]{0:T(128)} %contact_own.1) | copy-start | bytes 52
  46.1 26.8 %copy-start.3 = (s32[4]{0:T(128)S(1)}, s32[4]{0:T(128)}, u32[]{:S(2)}) copy-start(s32[4]{0:T(128)} %contact_other.1) | copy-start | bytes 52
  46.1 23.1 %collective-permute-start.4 = (f32[6,112,256]{2,1,0:T(8,128)S(1)}, f32[6,112,256]{2,1,0:T(8,128)S(1)}, u32[]{:S(2)}, u32[]{:S(2)}) collective-permute-start(f32[6,112,256]{2,1,0:T(8,128)S(1)} %get-tuple-element.45), channel_id=1, source_target_pairs={{0,8},{8,0},{16,24},{24,16},{32,40},{40,32},{48,56},{56,48},{64,72... | collective-permute-start | bytes 2064392 | tf_op jit(solution)/shard_map/ppermute | solution.py:646
  46.2 23.0 %collective-permute-start.5 = (f32[6,112,256]{2,1,0:T(8,128)S(1)}, f32[6,112,256]{2,1,0:T(8,128)S(1)}, u32[]{:S(2)}, u32[]{:S(2)}) collective-permute-start(f32[6,112,256]{2,1,0:T(8,128)S(1)} %get-tuple-element.46), channel_id=1, source_target_pairs={{8,16},{16,8},{24,32},{32,24},{40,48},{48,40},{56,64},{64,56},{72,... | collective-permute-start | bytes 2064392 | tf_op jit(solution)/shard_map/ppermute | solution.py:647
  70.0 5.3 %collective-permute-start.6 = (f32[432,256]{1,0:T(8,128)S(1)}, f32[432,256]{1,0:T(8,128)S(1)}, u32[]{:S(2)}, u32[]{:S(2)}) collective-permute-start(f32[432,256]{1,0:T(8,128)S(1)} %get-tuple-element.47), channel_id=1, source_target_pairs={{0,1},{1,0},{2,3},{3,2},{4,5},{5,4},{6,7},{7,6},{8,9},{9,8},{10,11... | collective-permute-start | bytes 1327112 | tf_op jit(solution)/shard_map/ppermute | solution.py:652
  70.8 9.6 %collective-permute-start.7 = (f32[432,256]{1,0:T(8,128)S(1)}, f32[432,256]{1,0:T(8,128)S(1)}, u32[]{:S(2)}, u32[]{:S(2)}) collective-permute-start(f32[432,256]{1,0:T(8,128)S(1)} %get-tuple-element.48), channel_id=1, source_target_pairs={{1,2},{2,1},{3,4},{4,3},{5,6},{6,5},{9,10},{10,9},{11,12},{12,11},... | collective-permute-start | bytes 1327112 | tf_op jit(solution)/shard_map/ppermute | solution.py:653

commit v4 on v3

--- a/solution.py
+++ b/solution.py
@@ -19,7 +19,8 @@
 ROWS = 24
 TILE = 256
 UNROLL = 4
-SIZES = (7, 8, 9)
+EARLY = 2
+SIZES = (6, 7, 8, 9)
 WIN = 10
 CYR = 112
 
@@ -68,8 +69,9 @@
 
 
 def gather_tile(both, slot, tile):
-    place = lax.broadcasted_iota(I32, (TILE, slot.shape[1]), 0)
-    pick = (slot - tile * TILE == place).astype(F32).astype(BF16)
+    place = lax.broadcasted_iota(I32, (TILE, slot.shape[1]), 0).astype(F32).astype(BF16)
+    local = jnp.clip(slot - tile * TILE, -1, TILE).astype(F32).astype(BF16)
+    pick = jnp.where(place == local, jnp.ones((), BF16), jnp.zeros((), BF16))
     out = lax.dot_general(both, pick, (((1,), (1,)), ((), ())), preferred_element_type=F32)
     return out[0:ROWS] + out[ROWS : 2 * ROWS]
 
@@ -87,8 +89,8 @@
 
 def route_kernel(
     where, motion_h, owner_h, bx_h, by_h, bz_h, weights_h, offset_h, velocity_h,
-    to_a, to_b, middle, to_down, to_up, slot_out, both_out, linear,
-    motion, owner, bx, by, bz, weights, offset, vel, rec, sems, edge_sem, *, gx, gy_shift
+    to_a, to_b, middle, to_down, to_up, slot_out, both_out, linear, vel,
+    motion, owner, bx, by, bz, weights, offset, rec, sems, edge_sem, *, gx, gy_shift
 ):
     markers = owner.shape[1]
     blocks = markers // TILE
@@ -174,7 +176,7 @@
             to_up[at : at + 2, :] = vel[c, x, ny - 2 : ny, :]
 
 
-def home_kernel(slot, both, vel, inner, rim, part, fcat):
+def home_kernel(slot, both, vel, inner, rim, part, fcat, sums, tn, tt, sacc):
     markers = slot.shape[1]
     blocks = inner.shape[0]
     below = (slot[...] < markers).astype(F32)
@@ -209,6 +211,8 @@
         return carry
 
     lax.fori_loop(0, nx, halve, 0)
+    sums[...] = jnp.zeros(sums.shape, F32)
+    process_tiles(0, EARLY, inner, fcat, part, sums, tn, tt, sacc, tall=tall)
 
 
 def fill_own(vel, field):
@@ -255,19 +259,19 @@
 
 
 def chain(distance, rows):
-    value = jnp.where(distance == 3, rows[3], 0.0)
+    value = jnp.where(distance == 3, rows[3], jnp.zeros((), rows[3].dtype))
     for k in (2, 1, 0):
         value = jnp.where(distance == k, rows[k], value)
     return value
 
 
-def process_tiles(count, lists, fcat, part, sums, tn, tt, sacc, *, tall):
+def process_tiles(first_tile, stop, lists, fcat, part, sums, tn, tt, sacc, *, tall):
     nx = part.shape[0]
     row = lax.broadcasted_iota(I32, (CYR, 1), 0)
     comp = (row >= tall).astype(I32) + (row >= 2 * tall).astype(I32)
     y_of = jnp.where(row < 3 * tall, row - comp * tall, -100)
     comp = jnp.where(row < 3 * tall, comp, 3)
-    z_of = lax.broadcasted_iota(I32, (256, TILE), 0)
+    z_of = lax.broadcasted_iota(I32, (256, TILE), 0).astype(F32).astype(BF16)
     win_row = lax.broadcasted_iota(I32, (16, TILE), 0)
     group_of = lax.broadcasted_iota(I32, (128, TILE), 0)
 
@@ -284,9 +288,11 @@
         def _():
             bxi = bxf.astype(I32)
             byi = rec[13:14].astype(I32)
-            bzi = rec[14:15].astype(I32)
-            table_z = chain((z_of - bzi) & 255, [rec[8 + k : 9 + k] for k in range(4)])
-            high, low = split(table_z)
+            ahead = z_of - rec[14:15].astype(BF16)
+            ahead = jnp.where(ahead < 0, ahead + 256, ahead)
+            parts = [split(rec[8 + k : 9 + k]) for k in range(4)]
+            high = chain(ahead, [p[0] for p in parts])
+            low = chain(ahead, [p[1] for p in parts])
             tn[0:256, :] = high
             tn[256:512, :] = low
             tt[:, 0:256] = high
@@ -370,13 +376,13 @@
 
         return carry
 
-    lax.fori_loop(0, count, tile_body, 0)
-
-
-def inner_kernel(lists, fcat, part_in, part, sums, tn, tt, sacc, *, tall):
+    lax.fori_loop(first_tile, stop, tile_body, 0)
+
+
+def inner_kernel(lists, fcat, part_in, sums_in, part, sums, tn, tt, sacc, *, tall):
     del part_in
-    sums[...] = jnp.zeros(sums.shape, F32)
-    process_tiles(lists.shape[0], lists, fcat, part, sums, tn, tt, sacc, tall=tall)
+    del sums_in
+    process_tiles(EARLY, lists.shape[0], lists, fcat, part, sums, tn, tt, sacc, tall=tall)
 
 
 def couple_kernel(
@@ -427,8 +433,7 @@
     arrived[23:24, :] = jnp.where(list_at > 8, 0, list_at).astype(F32)
     valid_all = arrived[22:23, :] > 0.5
     count = jnp.sum(arrived[22:23, :]).astype(I32)
-    few = 10 * TILE
-    beyond = jnp.sum(arrived[22:23, few:total_lanes])
+    used = 8 + (jnp.sum(arrived[22:23, 8 * TILE : total_lanes]).astype(I32) + TILE - 1) // TILE
     bin_all = jnp.where(valid_all, arrived[12:13, :].astype(I32), 17)
     slot = counting_ranks(bin_all, lambda b: 0 * b + total_lanes, 17)
     both = halves(arrived[...])
@@ -436,18 +441,18 @@
         lists[t] = jnp.zeros((ROWS, TILE), F32)
     tiles = (count + TILE - 1) // TILE
 
-    def gather_few(t, carry):
-        lists[t] = gather_tile(both[:, 0:few], slot[:, 0:few], t)
-        return carry
-
-    def gather_all(t, carry):
-        lists[t] = gather_tile(both, slot, t)
-        return carry
-
-    lax.fori_loop(0, jnp.where(beyond > 0.5, 0, tiles), gather_few, 0)
-    lax.fori_loop(0, jnp.where(beyond > 0.5, tiles, 0), gather_all, 0)
+    reach = 0
+    for size in (9, 10, 11, 12, 16):
+        wanted = jnp.logical_and(used > reach, used <= size)
+        reach = size
+
+        def gather_some(t, carry, lanes=size * TILE):
+            lists[t] = gather_tile(both[:, 0:lanes], slot[:, 0:lanes], t)
+            return carry
+
+        lax.fori_loop(0, jnp.where(wanted, tiles, 0), gather_some, 0)
     sums[...] = sums_in[...]
-    process_tiles(tiles, lists, fcat, part, sums, tn, tt, sacc, tall=tall)
+    process_tiles(0, tiles, lists, fcat, part, sums, tn, tt, sacc, tall=tall)
     lane_of = lax.broadcasted_iota(I32, (128, 128), 1)
     low_part = pltpu.roll(sums[...], 120, axis=1)
     joined = jnp.where(lane_of < 6, sums[...] + low_part, 0.0)
@@ -659,7 +664,7 @@
 
     x_rows = 6 * ny + 3 * ROWS
     y_rows = 6 * (nx + 4) + 3 * ROWS
-    to_a, to_b, middle, own_down, own_up, slot, both, linear = pl.pallas_call(
+    to_a, to_b, middle, own_down, own_up, slot, both, linear, vel = pl.pallas_call(
         functools.partial(route_kernel, gx=gx, gy_shift=gy.bit_length() - 1),
         out_shape=(
             array(x_rows, nz),
@@ -670,9 +675,10 @@
             array(1, markers, dtype=I32),
             array(2 * ROWS, markers, dtype=BF16),
             array(1, 128),
+            array(3, nx, ny, nz),
         ),
         in_specs=[SMEM] + [HBM] * 8,
-        out_specs=(VMEM,) * 8,
+        out_specs=(VMEM,) * 9,
         scratch_shapes=[
             pltpu.SMEM((spheres, 6), F32),
             pltpu.VMEM((1, markers), I32),
@@ -681,7 +687,6 @@
             pltpu.VMEM((1, markers), I32),
             pltpu.VMEM((12, markers), F32),
             pltpu.VMEM((3, markers), F32),
-            pltpu.VMEM((3, nx, ny, nz), F32),
             pltpu.VMEM((ROWS, markers), F32),
             pltpu.SemaphoreType.DMA((7,)),
             pltpu.SemaphoreType.DMA((1,)),
@@ -708,31 +713,32 @@
     field = array(nx + 4, CYR, nz)
     halved = array(nx + 4, CYR, 2 * nz, dtype=BF16)
     lists = array(blocks, ROWS, TILE)
-    inner, rim, part, fcat = pl.pallas_call(
-        home_kernel,
-        out_shape=(lists, lists, field, halved),
-        in_specs=[VMEM] * 3,
-        out_specs=(VMEM,) * 4,
-        compiler_params=params(8),
-        cost_estimate=pl.CostEstimate(flops=2_000_000_000, bytes_accessed=0, transcendentals=0),
-        name="home",
-    )(slot, both, velocity)
     tile_scratch = [
         pltpu.VMEM((2 * nz, TILE), BF16),
         pltpu.VMEM((nz, 2 * TILE), BF16),
         pltpu.VMEM((CYR, TILE), F32),
     ]
+    inner, rim, part, fcat, sums = pl.pallas_call(
+        home_kernel,
+        out_shape=(lists, lists, field, halved, array(128, 128)),
+        in_specs=[VMEM] * 3,
+        out_specs=(VMEM,) * 5,
+        scratch_shapes=tile_scratch,
+        compiler_params=params(8),
+        cost_estimate=pl.CostEstimate(flops=2_000_000_000, bytes_accessed=0, transcendentals=0),
+        name="home",
+    )(slot, both, vel)
     part, sums = pl.pallas_call(
         functools.partial(inner_kernel, tall=tall),
         out_shape=(field, array(128, 128)),
-        in_specs=[VMEM] * 3,
+        in_specs=[VMEM] * 4,
         out_specs=(VMEM,) * 2,
-        input_output_aliases={2: 0},
+        input_output_aliases={2: 0, 3: 1},
         scratch_shapes=tile_scratch,
         compiler_params=params(8),
         cost_estimate=pl.CostEstimate(flops=4_000_000_000, bytes_accessed=0, transcendentals=0),
         name="inner",
-    )(inner, fcat, part)
+    )(inner, fcat, part, sums)
     x_buffer = pltpu.VMEM((x_rows, nz), F32)
     y_buffer = pltpu.VMEM((y_rows, nz), F32)
     got_ya, got_yb = swap_y(
@@ -769,7 +775,7 @@
         ],
         compiler_params=params(16),
         name="couple",
-    )(where, velocity, got_xa, got_xb, got_ya, got_yb, rim, linear, sums, part)
+    )(where, vel, got_xa, got_xb, got_ya, got_yb, rim, linear, sums, part)
 
     got_a, got_b = swap_x(send_a, send_b)
     everyone = lax.all_to_all(message, ("gx", "gy"), 0, 0, tiled=True)

time: 89.7 us -> 88.2 us (0.983)
  starting transfers between devices: 19.3 us -> 22.5 us
  Pallas kernels: 42.4 us -> 40.1 us
  local copies, waits for them, and re-layouts: 1.58 us -> 0.17 us
  blocking collectives: 18.4 us -> 17.5 us
    ppermute x2, starting transfers between devices: 9.01 us -> 12.5 us  [swap_x(): lax.ppermute(second, 'gx', pairs(gx, 1, True))]
    pallas_call x1, Pallas kernels: 5.6 us -> 2.17 us  [on_device(): pl.pallas_call(functools.partial(inner_kernel, tall=tall), out_shape=(fie...]
    pallas_call x1, Pallas kernels: 2.98 us -> 6.39 us  [on_device(): pl.pallas_call(home_kernel, out_shape=(lists, lists, field, halved, array...]
    pallas_call x1, Pallas kernels: 16.5 us -> 14.3 us  [on_device(): pl.pallas_call(couple_kernel, out_shape=(field, slab, slab, array(devices...]
    ppermute x2, waiting for transfers between devices: 1.55 us -> 0.01 us  [swap_x(): lax.ppermute(second, 'gx', pairs(gx, 1, True))]
    ppermute x2, waiting for transfers between devices: 5.04 us -> 6.54 us  [swap_y(): lax.ppermute(second, 'gy', pairs(gy, 1, False))]
    unnamed x10 -> x6, local copies, waits for them, and re-layouts: 1.43 us -> 0.02 us
    all_to_all x1, blocking collectives: 18.4 us -> 17.5 us  [on_device(): everyone = lax.all_to_all(message, ('gx', 'gy'), 0, 0, tiled=True)]
  transfers between devices with their start and end apart: 8 -> 8, of which waited for: 2 -> 2; matrix products, arithmetic and copies ran while one was open for 0% -> 0% of each run, Pallas kernels for 12% -> 13%
where the time goes in v4:
time: 88.2 us; the launch traced here: 87.8 us
  Pallas kernels  40.1 us (45%)
  starting transfers between devices  22.5 us (26%)
  blocking collectives  17.5 us (20%)
  waiting for transfers between devices  6.55 us (7%)
  between operations  0.95 us (1%)
    all_to_all x1, blocking collectives, on_device(): everyone = lax.all_to_all(message, ('gx', 'gy'), 0, 0, tiled=True)  17.5 us
    pallas_call x1, Pallas kernels, on_device(): pl.pallas_call(couple_kernel, out_shape=(field, slab, slab, array(devices...  14.3 us
    ppermute x2, starting transfers between devices, swap_x(): lax.ppermute(second, 'gx', pairs(gx, 1, True))  12.5 us
    pallas_call x1, Pallas kernels, on_device(): pl.pallas_call(functools.partial(relax_kernel, rows=ny * gy), out_shape=a...  8.76 us
    ppermute x2, waiting for transfers between devices, swap_y(): lax.ppermute(second, 'gy', pairs(gy, 1, False))  6.54 us
    pallas_call x1, Pallas kernels, on_device(): pl.pallas_call(home_kernel, out_shape=(lists, lists, field, halved, array...  6.39 us
    ppermute x2, starting transfers between devices, swap_y(): lax.ppermute(second, 'gy', pairs(gy, 1, False))  5.19 us
    pallas_call x1, Pallas kernels, on_device(): pl.pallas_call(functools.partial(route_kernel, gx=gx, gy_shift=gy.bit_len...  4.55 us
  transfers between devices with their start and end apart: 8, of which 2 were waited for; matrix products, arithmetic and copies ran while one was open for 0% of the time, Pallas kernels for 13%

profile of v4, /device:TPU:1, one launch (start us, length us, event | category | flops | bytes accessed | tf_op | source)
XLA Modules:
  0.0 87.8 jit_solution(1497173328253976072)
XLA Ops:
  0.6 0.1 pad_add_fusion.where
  0.7 4.5 %route.1 = (f32[264,256]{1,0:T(8,128)S(1)}, f32[264,256]{1,0:T(8,128)S(1)}, f32[2,24,256]{2,1,0:T(8,128)S(1)}, f32[192,256]{1,0:T(8,128)S(1)}, f32[192,256]{1,0:...) custom-call(s32[2]{0:T(128)S(1)} %pad_add_fusion.where, ...), custom_call_target="tpu_custom_call" | custom-call | tf_op jit(solution)/shard_map/route/pallas_call | solution.py:667
  5.3 2.5 %collective-permute-start = (f32[264,256]{1,0:T(8,128)S(1)}, f32[264,256]{1,0:T(8,128)S(1)}, u32[]{:S(2)}, u32[]{:S(2)}) collective-permute-start(f32[264,256]{1,0:T(8,128)S(1)} %get-tuple-element.29), channel_id=1, source_target_pairs={{0,8},{8,0},{16,24},{24,16},{32,40},{40,32},{48,56},{56,48},{64,72... | collective-permute-start | bytes 811016 | tf_op jit(solution)/shard_map/ppermute | solution.py:651
  7.8 4.4 %collective-permute-start.1 = (f32[264,256]{1,0:T(8,128)S(1)}, f32[264,256]{1,0:T(8,128)S(1)}, u32[]{:S(2)}, u32[]{:S(2)}) collective-permute-start(f32[264,256]{1,0:T(8,128)S(1)} %get-tuple-element.30), channel_id=1, source_target_pairs={{8,16},{16,8},{24,32},{32,24},{40,48},{48,40},{56,64},{64,56},{72,... | collective-permute-start | bytes 811016 | tf_op jit(solution)/shard_map/ppermute | solution.py:652
  12.2 6.4 %home.1 = (f32[8,24,256]{2,1,0:T(8,128)S(1)}, f32[8,24,256]{2,1,0:T(8,128)S(1)}, f32[20,112,256]{2,1,0:T(8,128)S(1)}, bf16[20,112,512]{2,1,0:T(8,128)(2,1)S(1)}, f32[128,128]{1,0:T(8,128)S(1)}) custom-call(s32[1,2048]{1,0:T(1,128)S(1)} %get-tuple-element.36.slot, bf16[48,2048]{1,0:T(8,128)(2,1)S(1)} %get-tuple-element.37.both, ...), custom_call_target="tpu_custom_call" | custom-call | flops 2000000000 | tf_op jit(solution)/shard_map/home/pallas_call | solution.py:721
  18.7 0.6 turn.1
  19.3 1.4 %collective-permute-start.2 = (f32[192,256]{1,0:T(8,128)S(1)}, f32[192,256]{1,0:T(8,128)S(1)}, u32[]{:S(2)}, u32[]{:S(2)}) collective-permute-start(f32[192,256]{1,0:T(8,128)S(1)} %get-tuple-element.34), channel_id=1, source_target_pairs={{0,1},{1,0},{2,3},{3,2},{4,5},{5,4},{6,7},{7,6},{8,9},{9,8},{10,11... | collective-permute-start | bytes 589832 | tf_op jit(solution)/shard_map/ppermute | solution.py:657
  20.7 3.3 %collective-permute-start.3 = (f32[192,256]{1,0:T(8,128)S(1)}, f32[192,256]{1,0:T(8,128)S(1)}, u32[]{:S(2)}, u32[]{:S(2)}) collective-permute-start(f32[192,256]{1,0:T(8,128)S(1)} %get-tuple-element.35), channel_id=1, source_target_pairs={{1,2},{2,1},{3,4},{4,3},{5,6},{6,5},{9,10},{10,9},{11,12},{12,11},... | collective-permute-start | bytes 589832 | tf_op jit(solution)/shard_map/ppermute | solution.py:658
  24.0 2.2 %inner.1 = (f32[20,112,256]{2,1,0:T(8,128)S(1)}, f32[128,128]{1,0:T(8,128)S(1)}) custom-call(f32[8,24,256]{2,1,0:T(8,128)S(1)} %get-tuple-element.40.lists, bf16[20,112,512]{2,1,0:T(8,128)(2,1)S(1)} %get-tuple-element.41.fcat, f32[20,112,256]{2,1,0:T(8,128)S(1)} %get-tuple-element.42.part_in, ...), custom_call_target="tpu_custom_call", output_to_operand_aliasing={{0}: (2, {}), {1}: (3, {})} | custom-call | flops 4000000000 | tf_op jit(solution)/shard_map/inner/pallas_call | solution.py:731
  26.2 1.5 %collective-permute-done.3.got_yb = f32[192,256]{1,0:T(8,128)S(1)} collective-permute-done((f32[192,256]{1,0:T(8,128)S(1)}, f32[192,256]{1,0:T(8,128)S(1)}, u32[]{:S(2)}, u32[]{:S(2)}) %collective-permute-start.3) | collective-permute-done | bytes 196640 | tf_op jit(solution)/shard_map/ppermute | solution.py:658
  27.7 14.3 %couple.1 = (f32[20,112,256]{2,1,0:T(8,128)S(1)}, f32[6,112,256]{2,1,0:T(8,128)S(1)}, f32[6,112,256]{2,1,0:T(8,128)S(1)}, f32[128,128]{1,0:T(8,128)S(1)}) custom-call(s32[2]{0:T(128)S(1)} %pad_add_fusion.where, f32[3,16,32,256]{3,2,1,0:T(8,128)S(1)} %get-tuple-element.28.vel, ...), custom_call_target="tpu_custom_call", output_to_operand_aliasing={{0}: (9, {})} | custom-call | tf_op jit(solution)/shard_map/couple/pallas_call | solution.py:758
  42.0 0.0 copy-start.2
  42.0 0.1 collective-permute-start.4
  42.1 8.1 %collective-permute-start.5 = (f32[6,112,256]{2,1,0:T(8,128)S(1)}, f32[6,112,256]{2,1,0:T(8,128)S(1)}, u32[]{:S(2)}, u32[]{:S(2)}) collective-permute-start(f32[6,112,256]{2,1,0:T(8,128)S(1)} %get-tuple-element.50), channel_id=1, source_target_pairs={{8,16},{16,8},{24,32},{32,24},{40,48},{48,40},{56,64},{64,56},{72,... | collective-permute-start | bytes 2064392 | tf_op jit(solution)/shard_map/ppermute | solution.py:652
  50.2 17.5 %all_to_all.12 = f32[128,1,128]{2,1,0:T(1,128)S(1)} all-to-all(f32[128,1,128]{2,1,0:T(1,128)S(1)} %bitcast.15), channel_id=1, replica_groups=mesh['gx'=16,'gy'=8] {'gx','gy'}, dimensions={0} | all-to-all | bytes 131072 | tf_op jit(solution)/shard_map/all_to_all | solution.py:781
  67.7 0.8 edges.1
  68.5 0.8 collective-permute-start.6
  69.3 1.9 %collective-permute-start.7 = (f32[432,256]{1,0:T(8,128)S(1)}, f32[432,256]{1,0:T(8,128)S(1)}, u32[]{:S(2)}, u32[]{:S(2)}) collective-permute-start(f32[432,256]{1,0:T(8,128)S(1)} %get-tuple-element.52), channel_id=1, source_target_pairs={{1,2},{2,1},{3,4},{4,3},{5,6},{6,5},{9,10},{10,9},{11,12},{12,11},... | collective-permute-start | bytes 1327112 | tf_op jit(solution)/shard_map/ppermute | solution.py:658
  71.2 0.1 slice.3
  71.3 0.1 pad_bitcast_fusion.angular
  71.4 1.5 %motion.1 = f32[2,6]{1,0:T(2,128)} custom-call(s32[2]{0:T(128)S(1)} %pad_add_fusion.where, s32[4]{0:T(128)S(1)} %copy-done, s32[4]{0:T(128)S(1)} %copy-done.1, f32[2,6]{1,0:T(2,128)S(1)} %pad_bitcast_fusion.angular, f32[128,128]{1,0:T(8,128)S(1)} %bitcast.14), custom_call_target="tpu_custom_call" | custom-call | tf_op jit(solution)/shard_map/motion/pallas_call | solution.py:794
  72.8 1.0 %middle.1.grown = f32[3,24,40,256]{3,2,1,0:T(8,128)S(1)} custom-call(s32[2]{0:T(128)S(1)} %pad_add_fusion.where, f32[20,112,256]{2,1,0:T(8,128)S(1)} %get-tuple-element.48.part, f32[6,112,256]{2,1,0:T(8,128)S(1)} %collective-permute-done.4.got_a, f32[6,112,256]{2,1,0:T(8,128)S(1)} %collective-permute-done.5.got_b), custom_call_target="tpu_custom_call" | custom-call | flops 2000000000 | tf_op jit(solution)/shard_map/middle/pallas_call | solution.py:804
  73.8 5.0 %collective-permute-done.7.got_b = f32[432,256]{1,0:T(8,128)S(1)} collective-permute-done((f32[432,256]{1,0:T(8,128)S(1)}, f32[432,256]{1,0:T(8,128)S(1)}, u32[]{:S(2)}, u32[]{:S(2)}) %collective-permute-start.7) | collective-permute-done | bytes 442400 | tf_op jit(solution)/shard_map/ppermute | solution.py:658
  78.9 8.8 %relax.1 = f32[3,16,32,256]{3,2,1,0:T(8,128)} custom-call(s32[2]{0:T(128)S(1)} %pad_add_fusion.where, f32[3,24,40,256]{3,2,1,0:T(8,128)S(1)} %middle.1.grown, f32[432,256]{1,0:T(8,128)S(1)} %collective-permute-done.6.got_a, f32[432,256]{1,0:T(8,128)S(1)} %collective-permute-done.7.got_b), custom_call_target="tpu_custom_call" | custom-call | tf_op jit(solution)/shard_map/relax/pallas_call | solution.py:814
  (11 shorter events, 0.0 us)
Async XLA Ops:
  5.3 13.4 %collective-permute-start = (f32[264,256]{1,0:T(8,128)S(1)}, f32[264,256]{1,0:T(8,128)S(1)}, u32[]{:S(2)}, u32[]{:S(2)}) collective-permute-start(f32[264,256]{1,0:T(8,128)S(1)} %get-tuple-element.29), channel_id=1, source_target_pairs={{0,8},{8,0},{16,24},{24,16},{32,40},{40,32},{48,56},{56,48},{64,72... | collective-permute-start | bytes 811016 | tf_op jit(solution)/shard_map/ppermute | solution.py:651
  7.8 10.9 %collective-permute-start.1 = (f32[264,256]{1,0:T(8,128)S(1)}, f32[264,256]{1,0:T(8,128)S(1)}, u32[]{:S(2)}, u32[]{:S(2)}) collective-permute-start(f32[264,256]{1,0:T(8,128)S(1)} %get-tuple-element.30), channel_id=1, source_target_pairs={{8,16},{16,8},{24,32},{32,24},{40,48},{48,40},{56,64},{64,56},{72,... | collective-permute-start | bytes 811016 | tf_op jit(solution)/shard_map/ppermute | solution.py:652
  19.3 6.9 %collective-permute-start.2 = (f32[192,256]{1,0:T(8,128)S(1)}, f32[192,256]{1,0:T(8,128)S(1)}, u32[]{:S(2)}, u32[]{:S(2)}) collective-permute-start(f32[192,256]{1,0:T(8,128)S(1)} %get-tuple-element.34), channel_id=1, source_target_pairs={{0,1},{1,0},{2,3},{3,2},{4,5},{5,4},{6,7},{7,6},{8,9},{9,8},{10,11... | collective-permute-start | bytes 589832 | tf_op jit(solution)/shard_map/ppermute | solution.py:657
  20.7 7.0 %collective-permute-start.3 = (f32[192,256]{1,0:T(8,128)S(1)}, f32[192,256]{1,0:T(8,128)S(1)}, u32[]{:S(2)}, u32[]{:S(2)}) collective-permute-start(f32[192,256]{1,0:T(8,128)S(1)} %get-tuple-element.35), channel_id=1, source_target_pairs={{1,2},{2,1},{3,4},{4,3},{5,6},{6,5},{9,10},{10,9},{11,12},{12,11},... | collective-permute-start | bytes 589832 | tf_op jit(solution)/shard_map/ppermute | solution.py:658
  42.0 29.2 %copy-start.2 = (f32[6,2]{0,1:T(2,128)S(1)}, f32[6,2]{0,1:T(2,128)}, u32[]{:S(2)}) copy-start(f32[6,2]{0,1:T(2,128)} %param.17) | copy-start | bytes 148
  42.0 29.4 %copy-start = (s32[4]{0:T(128)S(1)}, s32[4]{0:T(128)}, u32[]{:S(2)}) copy-start(s32[4]{0:T(128)} %contact_own.1) | copy-start | bytes 52
  42.0 29.3 %copy-start.1 = (s32[4]{0:T(128)S(1)}, s32[4]{0:T(128)}, u32[]{:S(2)}) copy-start(s32[4]{0:T(128)} %contact_other.1) | copy-start | bytes 52
  42.0 25.7 %collective-permute-start.4 = (f32[6,112,256]{2,1,0:T(8,128)S(1)}, f32[6,112,256]{2,1,0:T(8,128)S(1)}, u32[]{:S(2)}, u32[]{:S(2)}) collective-permute-start(f32[6,112,256]{2,1,0:T(8,128)S(1)} %get-tuple-element.49), channel_id=1, source_target_pairs={{0,8},{8,0},{16,24},{24,16},{32,40},{40,32},{48,56},{56,48},{64,72... | collective-permute-start | bytes 2064392 | tf_op jit(solution)/shard_map/ppermute | solution.py:651
  42.1 25.6 %collective-permute-start.5 = (f32[6,112,256]{2,1,0:T(8,128)S(1)}, f32[6,112,256]{2,1,0:T(8,128)S(1)}, u32[]{:S(2)}, u32[]{:S(2)}) collective-permute-start(f32[6,112,256]{2,1,0:T(8,128)S(1)} %get-tuple-element.50), channel_id=1, source_target_pairs={{8,16},{16,8},{24,32},{32,24},{40,48},{48,40},{56,64},{64,56},{72,... | collective-permute-start | bytes 2064392 | tf_op jit(solution)/shard_map/ppermute | solution.py:652
  68.5 5.3 %collective-permute-start.6 = (f32[432,256]{1,0:T(8,128)S(1)}, f32[432,256]{1,0:T(8,128)S(1)}, u32[]{:S(2)}, u32[]{:S(2)}) collective-permute-start(f32[432,256]{1,0:T(8,128)S(1)} %get-tuple-element.51), channel_id=1, source_target_pairs={{0,1},{1,0},{2,3},{3,2},{4,5},{5,4},{6,7},{7,6},{8,9},{9,8},{10,11... | collective-permute-start | bytes 1327112 | tf_op jit(solution)/shard_map/ppermute | solution.py:657
  69.3 9.6 %collective-permute-start.7 = (f32[432,256]{1,0:T(8,128)S(1)}, f32[432,256]{1,0:T(8,128)S(1)}, u32[]{:S(2)}, u32[]{:S(2)}) collective-permute-start(f32[432,256]{1,0:T(8,128)S(1)} %get-tuple-element.52), channel_id=1, source_target_pairs={{1,2},{2,1},{3,4},{4,3},{5,6},{6,5},{9,10},{10,9},{11,12},{12,11},... | collective-permute-start | bytes 1327112 | tf_op jit(solution)/shard_map/ppermute | solution.py:658

commit v5 on v4

--- a/solution.py
+++ b/solution.py
@@ -18,7 +18,8 @@
 
 ROWS = 24
 TILE = 256
-UNROLL = 4
+UNROLLS = (11, 10, 9, 4)
+UNROLL = UNROLLS[-1]
 EARLY = 2
 SIZES = (6, 7, 8, 9)
 WIN = 10
@@ -462,8 +463,9 @@
     message[...] = jnp.broadcast_to(line, message.shape)
     even = (where[0] & 1) == 0
     for x in range(6):
-        send_a[x] = part[jnp.where(even, nx - 6, 0) + x]
-        send_b[x] = part[jnp.where(even, 0, nx - 6) + x]
+        rows = pl.ds(x * 3 * tall, 3 * tall)
+        send_a[rows, :] = part[jnp.where(even, nx - 6, 0) + x, 0 : 3 * tall, :]
+        send_b[rows, :] = part[jnp.where(even, 0, nx - 6) + x, 0 : 3 * tall, :]
 
 
 def motion_kernel(
@@ -514,10 +516,11 @@
                 if 2 <= x < nx + 2:
                     pieces.append(part[x - 2, rows, :])
                 if x < 6:
-                    pieces.append(jnp.where(even, got_b[x, rows, :], got_a[x, rows, :]))
+                    slab = pl.ds(x * 3 * tall + at, 6)
+                    pieces.append(jnp.where(even, got_b[slab, :], got_a[slab, :]))
                 if x >= nx - 2:
-                    y = x - (nx - 2)
-                    pieces.append(jnp.where(even, got_a[y, rows, :], got_b[y, rows, :]))
+                    slab = pl.ds((x - (nx - 2)) * 3 * tall + at, 6)
+                    pieces.append(jnp.where(even, got_a[slab, :], got_b[slab, :]))
                 total = pieces[0]
                 for piece in pieces[1:]:
                     total = total + piece
@@ -548,7 +551,11 @@
         return lambda rows_of: part[at, rows_of, :]
 
     def chosen(at, first, second):
-        return lambda rows_of: jnp.where(even, first[at, rows_of, :], second[at, rows_of, :])
+        def source(rows_of):
+            slab = pl.ds(at * 3 * tall + rows_of.start, tall)
+            return jnp.where(even, first[slab, :], second[slab, :])
+
+        return source
 
     for x in range(6):
         fill(x, [chosen(x, got_b, got_a)] + ([from_part(x - 2)] if x >= 2 else []))
@@ -586,6 +593,7 @@
     for sweep in range(ITERS):
         target = (va, vb)[sweep % 2]
         last = sweep == ITERS - 1
+        size = UNROLLS[sweep]
 
         def layer(x, state=state, target=target, last=last):
             for c in range(3):
@@ -599,16 +607,16 @@
                 else:
                     target[c, x] = new
 
-        def group(g, carry, sweep=sweep, layer=layer, last=last):
-            for k in range(UNROLL):
-                layer(jnp.minimum(sweep + 1 + g * UNROLL + k, long - 2 - sweep))
+        def group(g, carry, sweep=sweep, layer=layer, last=last, size=size):
+            for k in range(size):
+                layer(jnp.minimum(sweep + 1 + g * size + k, long - 2 - sweep))
             if last:
                 for c in range(3):
                     part = pl.ds(g * UNROLL, UNROLL)
                     pltpu.make_async_copy(out.at[c, part], out_h.at[c, part], sems.at[g * 3 + c]).start()
             return carry
 
-        lax.fori_loop(0, (long - 2 - 2 * sweep + UNROLL - 1) // UNROLL, group, 0)
+        lax.fori_loop(0, (long - 2 - 2 * sweep + size - 1) // size, group, 0)
         state = target
     for g in range(nx // UNROLL):
         for c in range(3):
@@ -754,7 +762,7 @@
     )
 
     devices = gx * gy
-    slab = array(6, CYR, nz)
+    slab = array(6 * 3 * tall, nz)
     part, send_a, send_b, message = pl.pallas_call(
         couple_kernel,
         out_shape=(field, slab, slab, array(devices, 128)),

time: 88.2 us -> 86.9 us (0.985)
  blocking collectives: 17.5 us -> 21.7 us
  starting transfers between devices: 22.5 us -> 18.9 us
  Pallas kernels: 40.1 us -> 39 us
    all_to_all x1, blocking collectives: 17.5 us -> 21.7 us  [on_device(): everyone = lax.all_to_all(message, ('gx', 'gy'), 0, 0, tiled=True)]
    ppermute x2, starting transfers between devices: 12.5 us -> 8.87 us  [swap_x(): lax.ppermute(second, 'gx', pairs(gx, 1, True))]
    pallas_call x1, Pallas kernels: 8.76 us -> 7.7 us  [on_device(): pl.pallas_call(functools.partial(relax_kernel, rows=ny * gy), out_shape=a...]
where the time goes in v5:
time: 86.9 us; the launch traced here: 87.3 us
  Pallas kernels  39 us (45%)
  blocking collectives  21.7 us (25%)
  starting transfers between devices  18.9 us (22%)
  waiting for transfers between devices  6.55 us (8%)
  between operations  0.96 us (1%)
    all_to_all x1, blocking collectives, on_device(): everyone = lax.all_to_all(message, ('gx', 'gy'), 0, 0, tiled=True)  21.7 us
    pallas_call x1, Pallas kernels, on_device(): pl.pallas_call(couple_kernel, out_shape=(field, slab, slab, array(devices...  14.3 us
    ppermute x2, starting transfers between devices, swap_x(): lax.ppermute(second, 'gx', pairs(gx, 1, True))  8.87 us
    pallas_call x1, Pallas kernels, on_device(): pl.pallas_call(functools.partial(relax_kernel, rows=ny * gy), out_shape=a...  7.7 us
    ppermute x2, waiting for transfers between devices, swap_y(): lax.ppermute(second, 'gy', pairs(gy, 1, False))  6.54 us
    pallas_call x1, Pallas kernels, on_device(): pl.pallas_call(home_kernel, out_shape=(lists, lists, field, halved, array...  6.38 us
    ppermute x2, starting transfers between devices, swap_y(): lax.ppermute(second, 'gy', pairs(gy, 1, False))  5.17 us
    pallas_call x1, Pallas kernels, on_device(): pl.pallas_call(functools.partial(route_kernel, gx=gx, gy_shift=gy.bit_len...  4.55 us
  transfers between devices with their start and end apart: 8, of which 2 were waited for; matrix products, arithmetic and copies ran while one was open for 0% of the time, Pallas kernels for 13%

profile of v5, /device:TPU:1, one launch (start us, length us, event | category | flops | bytes accessed | tf_op | source)
XLA Modules:
  0.0 87.3 jit_solution(12066416346420964457)
XLA Ops:
  0.6 0.1 pad_add_fusion.where
  0.7 4.5 %route.1 = (f32[264,256]{1,0:T(8,128)S(1)}, f32[264,256]{1,0:T(8,128)S(1)}, f32[2,24,256]{2,1,0:T(8,128)S(1)}, f32[192,256]{1,0:T(8,128)S(1)}, f32[192,256]{1,0:...) custom-call(s32[2]{0:T(128)S(1)} %pad_add_fusion.where, ...), custom_call_target="tpu_custom_call" | custom-call | tf_op jit(solution)/shard_map/route/pallas_call | solution.py:675
  5.3 2.5 %collective-permute-start = (f32[264,256]{1,0:T(8,128)S(1)}, f32[264,256]{1,0:T(8,128)S(1)}, u32[]{:S(2)}, u32[]{:S(2)}) collective-permute-start(f32[264,256]{1,0:T(8,128)S(1)} %get-tuple-element.29), channel_id=1, source_target_pairs={{0,8},{8,0},{16,24},{24,16},{32,40},{40,32},{48,56},{56,48},{64,72... | collective-permute-start | bytes 811016 | tf_op jit(solution)/shard_map/ppermute | solution.py:659
  7.8 4.4 %collective-permute-start.1 = (f32[264,256]{1,0:T(8,128)S(1)}, f32[264,256]{1,0:T(8,128)S(1)}, u32[]{:S(2)}, u32[]{:S(2)}) collective-permute-start(f32[264,256]{1,0:T(8,128)S(1)} %get-tuple-element.30), channel_id=1, source_target_pairs={{8,16},{16,8},{24,32},{32,24},{40,48},{48,40},{56,64},{64,56},{72,... | collective-permute-start | bytes 811016 | tf_op jit(solution)/shard_map/ppermute | solution.py:660
  12.2 6.4 %home.1 = (f32[8,24,256]{2,1,0:T(8,128)S(1)}, f32[8,24,256]{2,1,0:T(8,128)S(1)}, f32[20,112,256]{2,1,0:T(8,128)S(1)}, bf16[20,112,512]{2,1,0:T(8,128)(2,1)S(1)}, f32[128,128]{1,0:T(8,128)S(1)}) custom-call(s32[1,2048]{1,0:T(1,128)S(1)} %get-tuple-element.36.slot, bf16[48,2048]{1,0:T(8,128)(2,1)S(1)} %get-tuple-element.37.both, ...), custom_call_target="tpu_custom_call" | custom-call | flops 2000000000 | tf_op jit(solution)/shard_map/home/pallas_call | solution.py:729
  18.6 0.6 turn.1
  19.3 1.5 %collective-permute-start.2 = (f32[192,256]{1,0:T(8,128)S(1)}, f32[192,256]{1,0:T(8,128)S(1)}, u32[]{:S(2)}, u32[]{:S(2)}) collective-permute-start(f32[192,256]{1,0:T(8,128)S(1)} %get-tuple-element.34), channel_id=1, source_target_pairs={{0,1},{1,0},{2,3},{3,2},{4,5},{5,4},{6,7},{7,6},{8,9},{9,8},{10,11... | collective-permute-start | bytes 589832 | tf_op jit(solution)/shard_map/ppermute | solution.py:665
  20.7 3.3 %collective-permute-start.3 = (f32[192,256]{1,0:T(8,128)S(1)}, f32[192,256]{1,0:T(8,128)S(1)}, u32[]{:S(2)}, u32[]{:S(2)}) collective-permute-start(f32[192,256]{1,0:T(8,128)S(1)} %get-tuple-element.35), channel_id=1, source_target_pairs={{1,2},{2,1},{3,4},{4,3},{5,6},{6,5},{9,10},{10,9},{11,12},{12,11},... | collective-permute-start | bytes 589832 | tf_op jit(solution)/shard_map/ppermute | solution.py:666
  24.0 2.2 %inner.1 = (f32[20,112,256]{2,1,0:T(8,128)S(1)}, f32[128,128]{1,0:T(8,128)S(1)}) custom-call(f32[8,24,256]{2,1,0:T(8,128)S(1)} %get-tuple-element.40.lists, bf16[20,112,512]{2,1,0:T(8,128)(2,1)S(1)} %get-tuple-element.41.fcat, f32[20,112,256]{2,1,0:T(8,128)S(1)} %get-tuple-element.42.part_in, ...), custom_call_target="tpu_custom_call", output_to_operand_aliasing={{0}: (2, {}), {1}: (3, {})} | custom-call | flops 4000000000 | tf_op jit(solution)/shard_map/inner/pallas_call | solution.py:739
  26.2 1.5 %collective-permute-done.3.got_yb = f32[192,256]{1,0:T(8,128)S(1)} collective-permute-done((f32[192,256]{1,0:T(8,128)S(1)}, f32[192,256]{1,0:T(8,128)S(1)}, u32[]{:S(2)}, u32[]{:S(2)}) %collective-permute-start.3) | collective-permute-done | bytes 196640 | tf_op jit(solution)/shard_map/ppermute | solution.py:666
  27.7 14.3 %couple.1 = (f32[20,112,256]{2,1,0:T(8,128)S(1)}, f32[648,256]{1,0:T(8,128)S(1)}, f32[648,256]{1,0:T(8,128)S(1)}, f32[128,128]{1,0:T(8,128)S(1)}) custom-call(s32[2]{0:T(128)S(1)} %pad_add_fusion.where, f32[3,16,32,256]{3,2,1,0:T(8,128)S(1)} %get-tuple-element.28.vel, ...), custom_call_target="tpu_custom_call", output_to_operand_aliasing={{0}: (9, {})} | custom-call | tf_op jit(solution)/shard_map/couple/pallas_call | solution.py:766
  42.0 0.0 copy-start.2
  42.1 0.1 collective-permute-start.4
  42.2 4.4 %collective-permute-start.5 = (f32[648,256]{1,0:T(8,128)S(1)}, f32[648,256]{1,0:T(8,128)S(1)}, u32[]{:S(2)}, u32[]{:S(2)}) collective-permute-start(f32[648,256]{1,0:T(8,128)S(1)} %get-tuple-element.50), channel_id=1, source_target_pairs={{8,16},{16,8},{24,32},{32,24},{40,48},{48,40},{56,64},{64,56},{72,... | collective-permute-start | bytes 1990664 | tf_op jit(solution)/shard_map/ppermute | solution.py:660
  46.6 21.7 %all_to_all.12 = f32[128,1,128]{2,1,0:T(1,128)S(1)} all-to-all(f32[128,1,128]{2,1,0:T(1,128)S(1)} %bitcast.15), channel_id=1, replica_groups=mesh['gx'=16,'gy'=8] {'gx','gy'}, dimensions={0} | all-to-all | bytes 131072 | tf_op jit(solution)/shard_map/all_to_all | solution.py:789
  68.2 0.8 edges.1
  69.1 0.8 collective-permute-start.6
  69.8 1.9 %collective-permute-start.7 = (f32[432,256]{1,0:T(8,128)S(1)}, f32[432,256]{1,0:T(8,128)S(1)}, u32[]{:S(2)}, u32[]{:S(2)}) collective-permute-start(f32[432,256]{1,0:T(8,128)S(1)} %get-tuple-element.52), channel_id=1, source_target_pairs={{1,2},{2,1},{3,4},{4,3},{5,6},{6,5},{9,10},{10,9},{11,12},{12,11},... | collective-permute-start | bytes 1327112 | tf_op jit(solution)/shard_map/ppermute | solution.py:666
  71.8 0.1 slice.3
  71.8 0.1 pad_bitcast_fusion.angular
  71.9 1.5 %motion.1 = f32[2,6]{1,0:T(2,128)} custom-call(s32[2]{0:T(128)S(1)} %pad_add_fusion.where, s32[4]{0:T(128)S(1)} %copy-done, s32[4]{0:T(128)S(1)} %copy-done.1, f32[2,6]{1,0:T(2,128)S(1)} %pad_bitcast_fusion.angular, f32[128,128]{1,0:T(8,128)S(1)} %bitcast.14), custom_call_target="tpu_custom_call" | custom-call | tf_op jit(solution)/shard_map/motion/pallas_call | solution.py:802
  73.4 1.0 %middle.1.grown = f32[3,24,40,256]{3,2,1,0:T(8,128)S(1)} custom-call(s32[2]{0:T(128)S(1)} %pad_add_fusion.where, f32[20,112,256]{2,1,0:T(8,128)S(1)} %get-tuple-element.48.part, f32[648,256]{1,0:T(8,128)S(1)} %collective-permute-done.4.got_a, f32[648,256]{1,0:T(8,128)S(1)} %collective-permute-done.5.got_b), custom_call_target="tpu_custom_call" | custom-call | flops 2000000000 | tf_op jit(solution)/shard_map/middle/pallas_call | solution.py:812
  74.4 5.0 %collective-permute-done.7.got_b = f32[432,256]{1,0:T(8,128)S(1)} collective-permute-done((f32[432,256]{1,0:T(8,128)S(1)}, f32[432,256]{1,0:T(8,128)S(1)}, u32[]{:S(2)}, u32[]{:S(2)}) %collective-permute-start.7) | collective-permute-done | bytes 442400 | tf_op jit(solution)/shard_map/ppermute | solution.py:666
  79.5 7.7 %relax.1 = f32[3,16,32,256]{3,2,1,0:T(8,128)} custom-call(s32[2]{0:T(128)S(1)} %pad_add_fusion.where, f32[3,24,40,256]{3,2,1,0:T(8,128)S(1)} %middle.1.grown, f32[432,256]{1,0:T(8,128)S(1)} %collective-permute-done.6.got_a, f32[432,256]{1,0:T(8,128)S(1)} %collective-permute-done.7.got_b), custom_call_target="tpu_custom_call" | custom-call | tf_op jit(solution)/shard_map/relax/pallas_call | solution.py:822
  (11 shorter events, 0.0 us)
Async XLA Ops:
  5.3 13.4 %collective-permute-start = (f32[264,256]{1,0:T(8,128)S(1)}, f32[264,256]{1,0:T(8,128)S(1)}, u32[]{:S(2)}, u32[]{:S(2)}) collective-permute-start(f32[264,256]{1,0:T(8,128)S(1)} %get-tuple-element.29), channel_id=1, source_target_pairs={{0,8},{8,0},{16,24},{24,16},{32,40},{40,32},{48,56},{56,48},{64,72... | collective-permute-start | bytes 811016 | tf_op jit(solution)/shard_map/ppermute | solution.py:659
  7.8 10.8 %collective-permute-start.1 = (f32[264,256]{1,0:T(8,128)S(1)}, f32[264,256]{1,0:T(8,128)S(1)}, u32[]{:S(2)}, u32[]{:S(2)}) collective-permute-start(f32[264,256]{1,0:T(8,128)S(1)} %get-tuple-element.30), channel_id=1, source_target_pairs={{8,16},{16,8},{24,32},{32,24},{40,48},{48,40},{56,64},{64,56},{72,... | collective-permute-start | bytes 811016 | tf_op jit(solution)/shard_map/ppermute | solution.py:660
  19.3 6.9 %collective-permute-start.2 = (f32[192,256]{1,0:T(8,128)S(1)}, f32[192,256]{1,0:T(8,128)S(1)}, u32[]{:S(2)}, u32[]{:S(2)}) collective-permute-start(f32[192,256]{1,0:T(8,128)S(1)} %get-tuple-element.34), channel_id=1, source_target_pairs={{0,1},{1,0},{2,3},{3,2},{4,5},{5,4},{6,7},{7,6},{8,9},{9,8},{10,11... | collective-permute-start | bytes 589832 | tf_op jit(solution)/shard_map/ppermute | solution.py:665
  20.7 7.0 %collective-permute-start.3 = (f32[192,256]{1,0:T(8,128)S(1)}, f32[192,256]{1,0:T(8,128)S(1)}, u32[]{:S(2)}, u32[]{:S(2)}) collective-permute-start(f32[192,256]{1,0:T(8,128)S(1)} %get-tuple-element.35), channel_id=1, source_target_pairs={{1,2},{2,1},{3,4},{4,3},{5,6},{6,5},{9,10},{10,9},{11,12},{12,11},... | collective-permute-start | bytes 589832 | tf_op jit(solution)/shard_map/ppermute | solution.py:666
  42.0 29.7 %copy-start.2 = (f32[6,2]{0,1:T(2,128)S(1)}, f32[6,2]{0,1:T(2,128)}, u32[]{:S(2)}) copy-start(f32[6,2]{0,1:T(2,128)} %param.17) | copy-start | bytes 148
  42.0 29.9 %copy-start = (s32[4]{0:T(128)S(1)}, s32[4]{0:T(128)}, u32[]{:S(2)}) copy-start(s32[4]{0:T(128)} %contact_own.1) | copy-start | bytes 52
  42.0 29.9 %copy-start.1 = (s32[4]{0:T(128)S(1)}, s32[4]{0:T(128)}, u32[]{:S(2)}) copy-start(s32[4]{0:T(128)} %contact_other.1) | copy-start | bytes 52
  42.1 26.2 %collective-permute-start.4 = (f32[648,256]{1,0:T(8,128)S(1)}, f32[648,256]{1,0:T(8,128)S(1)}, u32[]{:S(2)}, u32[]{:S(2)}) collective-permute-start(f32[648,256]{1,0:T(8,128)S(1)} %get-tuple-element.49), channel_id=1, source_target_pairs={{0,8},{8,0},{16,24},{24,16},{32,40},{40,32},{48,56},{56,48},{64,72... | collective-permute-start | bytes 1990664 | tf_op jit(solution)/shard_map/ppermute | solution.py:659
  42.2 26.1 %collective-permute-start.5 = (f32[648,256]{1,0:T(8,128)S(1)}, f32[648,256]{1,0:T(8,128)S(1)}, u32[]{:S(2)}, u32[]{:S(2)}) collective-permute-start(f32[648,256]{1,0:T(8,128)S(1)} %get-tuple-element.50), channel_id=1, source_target_pairs={{8,16},{16,8},{24,32},{32,24},{40,48},{48,40},{56,64},{64,56},{72,... | collective-permute-start | bytes 1990664 | tf_op jit(solution)/shard_map/ppermute | solution.py:660
  69.1 5.3 %collective-permute-start.6 = (f32[432,256]{1,0:T(8,128)S(1)}, f32[432,256]{1,0:T(8,128)S(1)}, u32[]{:S(2)}, u32[]{:S(2)}) collective-permute-start(f32[432,256]{1,0:T(8,128)S(1)} %get-tuple-element.51), channel_id=1, source_target_pairs={{0,1},{1,0},{2,3},{3,2},{4,5},{5,4},{6,7},{7,6},{8,9},{9,8},{10,11... | collective-permute-start | bytes 1327112 | tf_op jit(solution)/shard_map/ppermute | solution.py:665
  69.8 9.6 %collective-permute-start.7 = (f32[432,256]{1,0:T(8,128)S(1)}, f32[432,256]{1,0:T(8,128)S(1)}, u32[]{:S(2)}, u32[]{:S(2)}) collective-permute-start(f32[432,256]{1,0:T(8,128)S(1)} %get-tuple-element.52), channel_id=1, source_target_pairs={{1,2},{2,1},{3,4},{4,3},{5,6},{6,5},{9,10},{10,9},{11,12},{12,11},... | collective-permute-start | bytes 1327112 | tf_op jit(solution)/shard_map/ppermute | solution.py:666

commit v6 on v5

--- a/solution.py
+++ b/solution.py
@@ -211,7 +211,7 @@
         to_halves(part, fcat, x)
         return carry
 
-    lax.fori_loop(0, nx, halve, 0)
+    lax.fori_loop(0, nx, halve, 0, unroll=5)
     sums[...] = jnp.zeros(sums.shape, F32)
     process_tiles(0, EARLY, inner, fcat, part, sums, tn, tt, sacc, tall=tall)
 
@@ -224,7 +224,7 @@
             field[x + 2, c * (cells + 4) + 2 : c * (cells + 4) + 2 + cells, :] = vel[c, x]
         return carry
 
-    lax.fori_loop(0, vel.shape[1], layer, 0)
+    lax.fori_loop(0, vel.shape[1], layer, 0, unroll=4)
 
 
 def to_halves(field, fcat, x):
@@ -415,7 +415,7 @@
         to_halves(field, fcat, x)
         return carry
 
-    lax.fori_loop(0, nx, halve, 0)
+    lax.fori_loop(0, nx, halve, 0, unroll=5)
 
     base = 6 * cells + ROWS
     after = nx * 6

time: 86.9 us -> 86.4 us (level); the launches traced: 87.3 us -> 85.9 us
  starting transfers between devices: 18.9 us -> 22.4 us
  blocking collectives: 21.7 us -> 18.4 us
  Pallas kernels: 39 us -> 36.1 us
  waiting for transfers between devices: 6.55 us -> 7.79 us
    ppermute x2, starting transfers between devices: 8.87 us -> 12.6 us  [swap_x(): lax.ppermute(second, 'gx', pairs(gx, 1, True))]
    all_to_all x1, blocking collectives: 21.7 us -> 18.4 us  [on_device(): everyone = lax.all_to_all(message, ('gx', 'gy'), 0, 0, tiled=True)]
    pallas_call x1, Pallas kernels: 14.3 us -> 12.2 us  [on_device(): pl.pallas_call(couple_kernel, out_shape=(field, slab, slab, array(devices...]
    pallas_call x1, Pallas kernels: 2.17 us -> 0.91 us  [on_device(): pl.pallas_call(functools.partial(inner_kernel, tall=tall), out_shape=(fie...]
    ppermute x2, waiting for transfers between devices: 6.54 us -> 7.78 us  [swap_y(): lax.ppermute(second, 'gy', pairs(gy, 1, False))]
  transfers between devices with their start and end apart: 8 -> 8, of which waited for: 2 -> 2; matrix products, arithmetic and copies ran while one was open for 0% -> 0% of each run, Pallas kernels for 13% -> 12%
where the time goes in v6:
time: 86.4 us; the launch traced here: 85.9 us
  Pallas kernels  36.1 us (42%)
  starting transfers between devices  22.4 us (26%)
  blocking collectives  18.4 us (21%)
  waiting for transfers between devices  7.79 us (9%)
  between operations  0.96 us (1%)
    all_to_all x1, blocking collectives, on_device(): everyone = lax.all_to_all(message, ('gx', 'gy'), 0, 0, tiled=True)  18.4 us
    ppermute x2, starting transfers between devices, swap_x(): lax.ppermute(second, 'gx', pairs(gx, 1, True))  12.6 us
    pallas_call x1, Pallas kernels, on_device(): pl.pallas_call(couple_kernel, out_shape=(field, slab, slab, array(devices...  12.2 us
    ppermute x2, waiting for transfers between devices, swap_y(): lax.ppermute(second, 'gy', pairs(gy, 1, False))  7.78 us
    pallas_call x1, Pallas kernels, on_device(): pl.pallas_call(functools.partial(relax_kernel, rows=ny * gy), out_shape=a...  7.7 us
    pallas_call x1, Pallas kernels, on_device(): pl.pallas_call(home_kernel, out_shape=(lists, lists, field, halved, array...  6.76 us
    ppermute x2, starting transfers between devices, swap_y(): lax.ppermute(second, 'gy', pairs(gy, 1, False))  5.19 us
    pallas_call x1, Pallas kernels, on_device(): pl.pallas_call(functools.partial(route_kernel, gx=gx, gy_shift=gy.bit_len...  4.55 us
  transfers between devices with their start and end apart: 8, of which 2 were waited for; matrix products, arithmetic and copies ran while one was open for 0% of the time, Pallas kernels for 12%

profile of v6, /device:TPU:1, one launch (start us, length us, event | category | flops | bytes accessed | tf_op | source)
XLA Modules:
  0.0 85.9 jit_solution(13118999014934214485)
XLA Ops:
  0.6 0.1 pad_add_fusion.where
  0.7 4.5 %route.1 = (f32[264,256]{1,0:T(8,128)S(1)}, f32[264,256]{1,0:T(8,128)S(1)}, f32[2,24,256]{2,1,0:T(8,128)S(1)}, f32[192,256]{1,0:T(8,128)S(1)}, f32[192,256]{1,0:...) custom-call(s32[2]{0:T(128)S(1)} %pad_add_fusion.where, ...), custom_call_target="tpu_custom_call" | custom-call | tf_op jit(solution)/shard_map/route/pallas_call | solution.py:675
  5.3 2.5 %collective-permute-start = (f32[264,256]{1,0:T(8,128)S(1)}, f32[264,256]{1,0:T(8,128)S(1)}, u32[]{:S(2)}, u32[]{:S(2)}) collective-permute-start(f32[264,256]{1,0:T(8,128)S(1)} %get-tuple-element.29), channel_id=1, source_target_pairs={{0,8},{8,0},{16,24},{24,16},{32,40},{40,32},{48,56},{56,48},{64,72... | collective-permute-start | bytes 811016 | tf_op jit(solution)/shard_map/ppermute | solution.py:659
  7.8 4.4 %collective-permute-start.1 = (f32[264,256]{1,0:T(8,128)S(1)}, f32[264,256]{1,0:T(8,128)S(1)}, u32[]{:S(2)}, u32[]{:S(2)}) collective-permute-start(f32[264,256]{1,0:T(8,128)S(1)} %get-tuple-element.30), channel_id=1, source_target_pairs={{8,16},{16,8},{24,32},{32,24},{40,48},{48,40},{56,64},{64,56},{72,... | collective-permute-start | bytes 811016 | tf_op jit(solution)/shard_map/ppermute | solution.py:660
  12.2 6.8 %home.1 = (f32[8,24,256]{2,1,0:T(8,128)S(1)}, f32[8,24,256]{2,1,0:T(8,128)S(1)}, f32[20,112,256]{2,1,0:T(8,128)S(1)}, bf16[20,112,512]{2,1,0:T(8,128)(2,1)S(1)}, f32[128,128]{1,0:T(8,128)S(1)}) custom-call(s32[1,2048]{1,0:T(1,128)S(1)} %get-tuple-element.36.slot, bf16[48,2048]{1,0:T(8,128)(2,1)S(1)} %get-tuple-element.37.both, ...), custom_call_target="tpu_custom_call" | custom-call | flops 2000000000 | tf_op jit(solution)/shard_map/home/pallas_call | solution.py:729
  19.0 0.6 turn.1
  19.7 1.1 %collective-permute-start.2 = (f32[192,256]{1,0:T(8,128)S(1)}, f32[192,256]{1,0:T(8,128)S(1)}, u32[]{:S(2)}, u32[]{:S(2)}) collective-permute-start(f32[192,256]{1,0:T(8,128)S(1)} %get-tuple-element.34), channel_id=1, source_target_pairs={{0,1},{1,0},{2,3},{3,2},{4,5},{5,4},{6,7},{7,6},{8,9},{9,8},{10,11... | collective-permute-start | bytes 589832 | tf_op jit(solution)/shard_map/ppermute | solution.py:665
  20.7 3.3 %collective-permute-start.3 = (f32[192,256]{1,0:T(8,128)S(1)}, f32[192,256]{1,0:T(8,128)S(1)}, u32[]{:S(2)}, u32[]{:S(2)}) collective-permute-start(f32[192,256]{1,0:T(8,128)S(1)} %get-tuple-element.35), channel_id=1, source_target_pairs={{1,2},{2,1},{3,4},{4,3},{5,6},{6,5},{9,10},{10,9},{11,12},{12,11},... | collective-permute-start | bytes 589832 | tf_op jit(solution)/shard_map/ppermute | solution.py:666
  24.0 0.9 %inner.1 = (f32[20,112,256]{2,1,0:T(8,128)S(1)}, f32[128,128]{1,0:T(8,128)S(1)}) custom-call(f32[8,24,256]{2,1,0:T(8,128)S(1)} %get-tuple-element.40.lists, bf16[20,112,512]{2,1,0:T(8,128)(2,1)S(1)} %get-tuple-element.41.fcat, f32[20,112,256]{2,1,0:T(8,128)S(1)} %get-tuple-element.42.part_in, ...), custom_call_target="tpu_custom_call", output_to_operand_aliasing={{0}: (2, {}), {1}: (3, {})} | custom-call | flops 4000000000 | tf_op jit(solution)/shard_map/inner/pallas_call | solution.py:739
  24.9 2.8 %collective-permute-done.3.got_yb = f32[192,256]{1,0:T(8,128)S(1)} collective-permute-done((f32[192,256]{1,0:T(8,128)S(1)}, f32[192,256]{1,0:T(8,128)S(1)}, u32[]{:S(2)}, u32[]{:S(2)}) %collective-permute-start.3) | collective-permute-done | bytes 196640 | tf_op jit(solution)/shard_map/ppermute | solution.py:666
  27.7 12.2 %couple.1 = (f32[20,112,256]{2,1,0:T(8,128)S(1)}, f32[648,256]{1,0:T(8,128)S(1)}, f32[648,256]{1,0:T(8,128)S(1)}, f32[128,128]{1,0:T(8,128)S(1)}) custom-call(s32[2]{0:T(128)S(1)} %pad_add_fusion.where, f32[3,16,32,256]{3,2,1,0:T(8,128)S(1)} %get-tuple-element.28.vel, ...), custom_call_target="tpu_custom_call", output_to_operand_aliasing={{0}: (9, {})} | custom-call | tf_op jit(solution)/shard_map/couple/pallas_call | solution.py:766
  39.9 0.0 copy-start.2
  40.0 0.1 collective-permute-start.4
  40.1 8.2 %collective-permute-start.5 = (f32[648,256]{1,0:T(8,128)S(1)}, f32[648,256]{1,0:T(8,128)S(1)}, u32[]{:S(2)}, u32[]{:S(2)}) collective-permute-start(f32[648,256]{1,0:T(8,128)S(1)} %get-tuple-element.50), channel_id=1, source_target_pairs={{8,16},{16,8},{24,32},{32,24},{40,48},{48,40},{56,64},{64,56},{72,... | collective-permute-start | bytes 1990664 | tf_op jit(solution)/shard_map/ppermute | solution.py:660
  48.2 18.4 %all_to_all.12 = f32[128,1,128]{2,1,0:T(1,128)S(1)} all-to-all(f32[128,1,128]{2,1,0:T(1,128)S(1)} %bitcast.15), channel_id=1, replica_groups=mesh['gx'=16,'gy'=8] {'gx','gy'}, dimensions={0} | all-to-all | bytes 131072 | tf_op jit(solution)/shard_map/all_to_all | solution.py:789
  66.6 0.8 edges.1
  67.5 0.9 %collective-permute-start.6 = (f32[432,256]{1,0:T(8,128)S(1)}, f32[432,256]{1,0:T(8,128)S(1)}, u32[]{:S(2)}, u32[]{:S(2)}) collective-permute-start(f32[432,256]{1,0:T(8,128)S(1)} %get-tuple-element.51), channel_id=1, source_target_pairs={{0,1},{1,0},{2,3},{3,2},{4,5},{5,4},{6,7},{7,6},{8,9},{9,8},{10,11... | collective-permute-start | bytes 1327112 | tf_op jit(solution)/shard_map/ppermute | solution.py:665
  68.4 1.9 %collective-permute-start.7 = (f32[432,256]{1,0:T(8,128)S(1)}, f32[432,256]{1,0:T(8,128)S(1)}, u32[]{:S(2)}, u32[]{:S(2)}) collective-permute-start(f32[432,256]{1,0:T(8,128)S(1)} %get-tuple-element.52), channel_id=1, source_target_pairs={{1,2},{2,1},{3,4},{4,3},{5,6},{6,5},{9,10},{10,9},{11,12},{12,11},... | collective-permute-start | bytes 1327112 | tf_op jit(solution)/shard_map/ppermute | solution.py:666
  70.3 0.1 slice.3
  70.4 0.1 pad_bitcast_fusion.angular
  70.5 1.5 %motion.1 = f32[2,6]{1,0:T(2,128)} custom-call(s32[2]{0:T(128)S(1)} %pad_add_fusion.where, s32[4]{0:T(128)S(1)} %copy-done, s32[4]{0:T(128)S(1)} %copy-done.1, f32[2,6]{1,0:T(2,128)S(1)} %pad_bitcast_fusion.angular, f32[128,128]{1,0:T(8,128)S(1)} %bitcast.14), custom_call_target="tpu_custom_call" | custom-call | tf_op jit(solution)/shard_map/motion/pallas_call | solution.py:802
  72.0 1.0 %middle.1.grown = f32[3,24,40,256]{3,2,1,0:T(8,128)S(1)} custom-call(s32[2]{0:T(128)S(1)} %pad_add_fusion.where, f32[20,112,256]{2,1,0:T(8,128)S(1)} %get-tuple-element.48.part, f32[648,256]{1,0:T(8,128)S(1)} %collective-permute-done.4.got_a, f32[648,256]{1,0:T(8,128)S(1)} %collective-permute-done.5.got_b), custom_call_target="tpu_custom_call" | custom-call | flops 2000000000 | tf_op jit(solution)/shard_map/middle/pallas_call | solution.py:812
  73.0 5.0 %collective-permute-done.7.got_b = f32[432,256]{1,0:T(8,128)S(1)} collective-permute-done((f32[432,256]{1,0:T(8,128)S(1)}, f32[432,256]{1,0:T(8,128)S(1)}, u32[]{:S(2)}, u32[]{:S(2)}) %collective-permute-start.7) | collective-permute-done | bytes 442400 | tf_op jit(solution)/shard_map/ppermute | solution.py:666
  78.0 7.7 %relax.1 = f32[3,16,32,256]{3,2,1,0:T(8,128)} custom-call(s32[2]{0:T(128)S(1)} %pad_add_fusion.where, f32[3,24,40,256]{3,2,1,0:T(8,128)S(1)} %middle.1.grown, f32[432,256]{1,0:T(8,128)S(1)} %collective-permute-done.6.got_a, f32[432,256]{1,0:T(8,128)S(1)} %collective-permute-done.7.got_b), custom_call_target="tpu_custom_call" | custom-call | tf_op jit(solution)/shard_map/relax/pallas_call | solution.py:822
  (11 shorter events, 0.0 us)
Async XLA Ops:
  5.3 13.8 %collective-permute-start = (f32[264,256]{1,0:T(8,128)S(1)}, f32[264,256]{1,0:T(8,128)S(1)}, u32[]{:S(2)}, u32[]{:S(2)}) collective-permute-start(f32[264,256]{1,0:T(8,128)S(1)} %get-tuple-element.29), channel_id=1, source_target_pairs={{0,8},{8,0},{16,24},{24,16},{32,40},{40,32},{48,56},{56,48},{64,72... | collective-permute-start | bytes 811016 | tf_op jit(solution)/shard_map/ppermute | solution.py:659
  7.8 11.2 %collective-permute-start.1 = (f32[264,256]{1,0:T(8,128)S(1)}, f32[264,256]{1,0:T(8,128)S(1)}, u32[]{:S(2)}, u32[]{:S(2)}) collective-permute-start(f32[264,256]{1,0:T(8,128)S(1)} %get-tuple-element.30), channel_id=1, source_target_pairs={{8,16},{16,8},{24,32},{32,24},{40,48},{48,40},{56,64},{64,56},{72,... | collective-permute-start | bytes 811016 | tf_op jit(solution)/shard_map/ppermute | solution.py:660
  19.7 5.3 %collective-permute-start.2 = (f32[192,256]{1,0:T(8,128)S(1)}, f32[192,256]{1,0:T(8,128)S(1)}, u32[]{:S(2)}, u32[]{:S(2)}) collective-permute-start(f32[192,256]{1,0:T(8,128)S(1)} %get-tuple-element.34), channel_id=1, source_target_pairs={{0,1},{1,0},{2,3},{3,2},{4,5},{5,4},{6,7},{7,6},{8,9},{9,8},{10,11... | collective-permute-start | bytes 589832 | tf_op jit(solution)/shard_map/ppermute | solution.py:665
  20.7 7.0 %collective-permute-start.3 = (f32[192,256]{1,0:T(8,128)S(1)}, f32[192,256]{1,0:T(8,128)S(1)}, u32[]{:S(2)}, u32[]{:S(2)}) collective-permute-start(f32[192,256]{1,0:T(8,128)S(1)} %get-tuple-element.35), channel_id=1, source_target_pairs={{1,2},{2,1},{3,4},{4,3},{5,6},{6,5},{9,10},{10,9},{11,12},{12,11},... | collective-permute-start | bytes 589832 | tf_op jit(solution)/shard_map/ppermute | solution.py:666
  39.9 30.4 %copy-start.2 = (f32[6,2]{0,1:T(2,128)S(1)}, f32[6,2]{0,1:T(2,128)}, u32[]{:S(2)}) copy-start(f32[6,2]{0,1:T(2,128)} %param.17) | copy-start | bytes 148
  40.0 30.5 %copy-start = (s32[4]{0:T(128)S(1)}, s32[4]{0:T(128)}, u32[]{:S(2)}) copy-start(s32[4]{0:T(128)} %contact_own.1) | copy-start | bytes 52
  40.0 30.5 %copy-start.1 = (s32[4]{0:T(128)S(1)}, s32[4]{0:T(128)}, u32[]{:S(2)}) copy-start(s32[4]{0:T(128)} %contact_other.1) | copy-start | bytes 52
  40.0 26.6 %collective-permute-start.4 = (f32[648,256]{1,0:T(8,128)S(1)}, f32[648,256]{1,0:T(8,128)S(1)}, u32[]{:S(2)}, u32[]{:S(2)}) collective-permute-start(f32[648,256]{1,0:T(8,128)S(1)} %get-tuple-element.49), channel_id=1, source_target_pairs={{0,8},{8,0},{16,24},{24,16},{32,40},{40,32},{48,56},{56,48},{64,72... | collective-permute-start | bytes 1990664 | tf_op jit(solution)/shard_map/ppermute | solution.py:659
  40.1 26.5 %collective-permute-start.5 = (f32[648,256]{1,0:T(8,128)S(1)}, f32[648,256]{1,0:T(8,128)S(1)}, u32[]{:S(2)}, u32[]{:S(2)}) collective-permute-start(f32[648,256]{1,0:T(8,128)S(1)} %get-tuple-element.50), channel_id=1, source_target_pairs={{8,16},{16,8},{24,32},{32,24},{40,48},{48,40},{56,64},{64,56},{72,... | collective-permute-start | bytes 1990664 | tf_op jit(solution)/shard_map/ppermute | solution.py:660
  67.5 5.5 %collective-permute-start.6 = (f32[432,256]{1,0:T(8,128)S(1)}, f32[432,256]{1,0:T(8,128)S(1)}, u32[]{:S(2)}, u32[]{:S(2)}) collective-permute-start(f32[432,256]{1,0:T(8,128)S(1)} %get-tuple-element.51), channel_id=1, source_target_pairs={{0,1},{1,0},{2,3},{3,2},{4,5},{5,4},{6,7},{7,6},{8,9},{9,8},{10,11... | collective-permute-start | bytes 1327112 | tf_op jit(solution)/shard_map/ppermute | solution.py:665
  68.4 9.6 %collective-permute-start.7 = (f32[432,256]{1,0:T(8,128)S(1)}, f32[432,256]{1,0:T(8,128)S(1)}, u32[]{:S(2)}, u32[]{:S(2)}) collective-permute-start(f32[432,256]{1,0:T(8,128)S(1)} %get-tuple-element.52), channel_id=1, source_target_pairs={{1,2},{2,1},{3,4},{4,3},{5,6},{6,5},{9,10},{10,9},{11,12},{12,11},... | collective-permute-start | bytes 1327112 | tf_op jit(solution)/shard_map/ppermute | solution.py:666
